TPU v7x, 32 devices: a whole 2x2x4 slice. The times are simulated.
32 devices in a mesh: emb: 8 (over z, core), dp: 4 (over y, x).
Axes of the slice: x: 2, y: 2, z: 4, core: 2. Of those that a mesh axis runs over, the one named last changes fastest.
Arguments:
- embeddings: bfloat16 [512, 256, 256], P('emb', 'dp'), may hold values from -9 to 9
- machine_projection: bfloat16 [512, 32], replicated, may hold values from -0.015625 to 0.015625
- w_lcb: bfloat16 [512, 512], P('dp'), may hold values from -0.25 to 0.25
- w_fmb: bfloat16 [32, 256], replicated, may hold values from -1 to 1
- ln_gain: float32 [512, 256], P('emb'), may hold values from 0.5 to 1.5
- ln_bias: float32 [512, 256], P('emb'), may hold values from -1.8 to 1.8
Outputs:
- layer_out: bfloat16 [512, 256, 256], P('emb', 'dp')
All inputs are finite; a program needn't handle non-finite values.
Results may differ from a plain program's by a relative error of at most 0.007.
Values may be sent and summed in bfloat16 or wider, within the bound.
No kernel may reach another device: no remote copies, remote signals or barrier semaphores. Data moves between devices by JAX's collectives and lax.ppermute only.
A program may use at most 64 MiB of HBM per device.

v0:
```python
import functools

import jax
import jax.numpy as jnp
from jax import lax
from jax.experimental import pallas as pl
from jax.experimental.pallas import tpu as pltpu
from jax.sharding import PartitionSpec as P


GROUP = 8
EPS = 1e-05


def target(me, m, count):
    if count & (count - 1) == 0:
        return me ^ m
    return lax.rem(me + m, count)


def origin(me, m, count):
    if count & (count - 1) == 0:
        return me ^ m
    return lax.rem(me + count - m, count)


def send(value, m, axis, count, back=False):
    if m == 0:
        return value
    pairs = []
    for i in range(count):
        j = i ^ m if count & (count - 1) == 0 else (i + m) % count
        pairs.append((j, i) if back else (i, j))
    return lax.ppermute(value, axis, pairs)


def row_block(rows):
    size = 32
    while rows % size:
        size //= 2
    return size


def pick_matrix(height, width, inner_out, inner_in):
    i = lax.broadcasted_iota(jnp.int32, (height, width), 0)
    j = lax.broadcasted_iota(jnp.int32, (height, width), 1)
    hit = (i // inner_out == j % inner_in) & (i % inner_out == j // inner_in)
    return jnp.where(hit, 1.0, 0.0).astype(jnp.bfloat16)


def split_kernel(messages, chunks, count, x_ref, *refs):
    outs = refs[: len(messages)]
    landed, sems = refs[len(messages) :]
    rows, _, width = x_ref.shape
    me = lax.axis_index("emb")
    distinct = sorted({m for m, _ in messages}, key=[m for m, _ in messages].index)

    def fetch(k):
        first = pl.multiple_of(target(me, distinct[k], count) * GROUP, GROUP)
        return pltpu.make_async_copy(x_ref.at[:, pl.ds(first, GROUP), :], landed.at[k], sems.at[k])

    for k in range(len(distinct)):
        fetch(k).start()
    block = row_block(rows)
    part = GROUP // chunks
    pick = pick_matrix(GROUP * block, block * GROUP, block, GROUP)
    for k, m in enumerate(distinct):
        fetch(k).wait()
        for q, (m2, c) in enumerate(messages):
            if m2 != m:
                continue
            for b in range(rows // block):
                piece = landed[k, b * block : (b + 1) * block].reshape(block * GROUP, width)
                moved = jnp.dot(
                    pick[c * part * block : (c + 1) * part * block], piece, preferred_element_type=jnp.float32
                )
                outs[q][:, b * block : (b + 1) * block, :] = moved.astype(jnp.bfloat16).reshape(part, block, width)


def split(x, messages, chunks, count):
    rows, _, width = x.shape
    part = GROUP // chunks
    distinct = len({m for m, _ in messages})
    out = jax.ShapeDtypeStruct((part, rows, width), jnp.bfloat16)
    return pl.pallas_call(
        functools.partial(split_kernel, messages, chunks, count),
        out_shape=[out] * len(messages),
        in_specs=[pl.BlockSpec(memory_space=pltpu.HBM)],
        out_specs=[pl.BlockSpec(memory_space=pltpu.VMEM)] * len(messages),
        scratch_shapes=[
            pltpu.VMEM((distinct, rows, GROUP, width), jnp.bfloat16),
            pltpu.SemaphoreType.DMA((distinct,)),
        ],
        compiler_params=pltpu.CompilerParams(vmem_limit_bytes=12 * 1024 * 1024),
        cost_estimate=pl.CostEstimate(flops=10**8, bytes_accessed=10**6, transcendentals=0),
        name="split",
    )(x)


def merge_kernel(messages, chunks, count, first, *refs):
    pieces = refs[: len(messages) * chunks]
    gain_ref, bias_ref = refs[len(messages) * chunks : len(messages) * chunks + 2]
    rest = refs[len(messages) * chunks + 2 :]
    out_ref, ready, sems = rest if first else rest[1:]
    _, rows, width = pieces[0].shape
    me = lax.axis_index("emb")
    block = row_block(rows)
    pick = pick_matrix(block * GROUP, GROUP * block, GROUP, block)
    copies = []
    for k, m in enumerate(messages):
        for b in range(rows // block):
            here = slice(b * block, (b + 1) * block)
            gain, bias = gain_ref[here], bias_ref[here]
            done = [
                (pieces[k * chunks + c][:, here, :].astype(jnp.float32) * gain[None] + bias[None]).astype(jnp.bfloat16)
                for c in range(chunks)
            ]
            done = jnp.concatenate(done, axis=0).reshape(GROUP * block, width)
            moved = jnp.dot(pick, done, preferred_element_type=jnp.float32)
            ready[k, here] = moved.astype(jnp.bfloat16).reshape(block, GROUP, width)
        start = pl.multiple_of(target(me, m, count) * GROUP, GROUP)
        copies.append(pltpu.make_async_copy(ready.at[k], out_ref.at[:, pl.ds(start, GROUP), :], sems.at[k]))
        copies[-1].start()
    for copy in copies:
        copy.wait()


def merge(out, pieces, gain, bias, messages, chunks, count, samples):
    _, rows, width = pieces[0].shape
    first = out is None
    vmem = pl.BlockSpec(memory_space=pltpu.VMEM)
    hbm = pl.BlockSpec(memory_space=pl.ANY)
    operands = list(pieces) + [gain, bias] + ([] if first else [out])
    return pl.pallas_call(
        functools.partial(merge_kernel, messages, chunks, count, first),
        out_shape=jax.ShapeDtypeStruct((rows, samples, width), jnp.bfloat16),
        in_specs=[vmem] * (len(pieces) + 2) + ([] if first else [hbm]),
        out_specs=hbm,
        input_output_aliases={} if first else {len(operands) - 1: 0},
        scratch_shapes=[
            pltpu.VMEM((len(messages), rows, GROUP, width), jnp.bfloat16),
            pltpu.SemaphoreType.DMA((len(messages),)),
        ],
        compiler_params=pltpu.CompilerParams(vmem_limit_bytes=12 * 1024 * 1024),
        cost_estimate=pl.CostEstimate(flops=10**8, bytes_accessed=10**6, transcendentals=0),
        name="merge",
    )(*operands)


def layer_kernel(count, pieces_w, *refs):
    blocks = refs[:count]
    weights = refs[count : count + pieces_w]
    proj_ref, fmb_ref = refs[count + pieces_w : count + pieces_w + 2]
    outs = refs[count + pieces_w + 2 : count + pieces_w + 2 + count]
    full_w, held, mixed = refs[count + pieces_w + 2 + count :]
    part, rows, width = blocks[0].shape
    total = count * rows
    me = lax.axis_index("emb")
    mine = lax.axis_index("dp")
    share_w = weights[0].shape[0]
    for q in range(pieces_w):
        full_w[pl.ds(pl.multiple_of(origin(mine, q, pieces_w) * share_w, share_w), share_w), :] = weights[q][...]
    entries = float(total * width)
    starts = [pl.multiple_of(origin(me, m, count) * rows, rows) for m in range(count)]

    def one(s, _):
        for m in range(count):
            held[pl.ds(starts[m], rows), :] = blocks[m][s]
        x = held[...]
        summed = lax.dot_general(proj_ref[...], x, (((0,), (0,)), ((), ())), preferred_element_type=jnp.float32)
        factor = summed.astype(jnp.bfloat16)
        inner = lax.dot_general(x, factor, (((1,), (1,)), ((), ())), preferred_element_type=jnp.float32)
        fmb = jnp.dot(inner.astype(jnp.bfloat16), fmb_ref[...], preferred_element_type=jnp.float32)
        compressed = jnp.dot(full_w[...], x, preferred_element_type=jnp.float32)
        value = x.astype(jnp.float32) + compressed + fmb
        mixed[...] = value
        average = jnp.sum(value) / entries
        centered = mixed[...] - average
        spread = jnp.sum(centered * centered) / entries
        scale = lax.rsqrt(jnp.full((1, width), spread + EPS, jnp.float32))
        for m in range(count):
            outs[m][s] = ((mixed[pl.ds(starts[m], rows), :] - average) * scale).astype(jnp.bfloat16)
        return 0

    lax.fori_loop(0, part, one, 0)


def layer(blocks, weights, proj, w_fmb):
    part, rows, width = blocks[0].shape
    count = len(blocks)
    total = count * rows
    vmem = pl.BlockSpec(memory_space=pltpu.VMEM)
    return pl.pallas_call(
        functools.partial(layer_kernel, count, len(weights)),
        out_shape=[jax.ShapeDtypeStruct((part, rows, width), jnp.bfloat16)] * count,
        in_specs=[vmem] * (count + len(weights) + 2),
        out_specs=[vmem] * count,
        scratch_shapes=[
            pltpu.VMEM((weights[0].shape[0] * len(weights), total), jnp.bfloat16),
            pltpu.VMEM((total, width), jnp.bfloat16),
            pltpu.VMEM((total, width), jnp.float32),
        ],
        compiler_params=pltpu.CompilerParams(vmem_limit_bytes=12 * 1024 * 1024),
        cost_estimate=pl.CostEstimate(
            flops=2 * part * total * total * width, bytes_accessed=4 * part * total * width, transcendentals=0
        ),
        name="layer",
    )(*blocks, *weights, proj, w_fmb)


def body(embeddings, machine_projection, w_lcb, w_fmb, ln_gain, ln_bias):
    rows, samples, width = embeddings.shape
    count = lax.axis_size("emb")
    others = lax.axis_size("dp")
    share = samples // count
    chunks = 2 if share % 2 == 0 else 1
    part = share // chunks
    far = [m for m in range(count) if m >= count // 2]
    near = [m for m in range(1, count) if m < count // 2]
    fast = share == GROUP
    sends = {}

    if fast:

        def cut(names):
            sends.update(zip(names, split(embeddings, names, chunks, count)))

    else:
        turned = embeddings.reshape(rows, count, chunks, part, width).transpose(1, 2, 3, 0, 4)
        me = lax.axis_index("emb")

        def cut(names):
            for m, c in names:
                sends[m, c] = lax.dynamic_index_in_dim(turned, target(me, m, count), 0, keepdims=False)[c]

    arrived = {}

    def forward(names):
        for m, c in names:
            arrived[m, c] = send(sends[m, c], m, "emb", count)

    cut([(m, 0) for m in far])
    forward([(m, 0) for m in far])
    cut([(m, 0) for m in near] + [(0, 0)] + [(m, c) for c in range(1, chunks) for m in far + near + [0]])
    forward([(m, 0) for m in near + [0]])
    weights = []
    for q in range(others):
        weights.append(send(w_lcb, q, "dp", others))
    for c in range(1, chunks):
        forward([(m, c) for m in far + near + [0]])

    returned = {}
    for c in range(chunks):
        done = layer([arrived[m, c] for m in range(count)], weights, machine_projection, w_fmb)
        for m in near + far + [0]:
            returned[m, c] = send(done[m], m, "emb", count, back=True)

    if fast:
        out = None
        for messages in [[0] + near] + [[m] for m in far]:
            pieces = [returned[m, c] for m in messages for c in range(chunks)]
            out = merge(out, pieces, ln_gain, ln_bias, messages, chunks, count, samples)
        return out
    me = lax.axis_index("emb")
    stacked = jnp.stack([jnp.concatenate([returned[m, c] for c in range(chunks)]) for m in range(count)])
    finished = (stacked.astype(jnp.float32) * ln_gain + ln_bias).astype(jnp.bfloat16)
    order = jnp.stack([_message_to(me, j, count) for j in range(count)])
    finished = jnp.take(finished, order, axis=0)
    return finished.transpose(2, 0, 1, 3).reshape(rows, samples, width)


def _message_to(me, j, count):
    if count & (count - 1) == 0:
        return me ^ j
    return lax.rem(j - me + count, count)


def solution(mesh):
    return jax.shard_map(
        body,
        mesh=mesh,
        in_specs=(P("emb", "dp", None), P(), P("dp", None), P(), P("emb", None), P("emb", None)),
        out_specs=P("emb", "dp", None),
        check_vma=False,
    )
```

profile of v0, /device:TPU:9, one launch (start us, length us, event | category | flops | bytes accessed | tf_op | source)
XLA Modules:
  0.0 106.8 jit_solution(658709571211438586)
XLA Ops:
  0.0 2.2 %collective-permute-start.9 = (bf16[128,512]{1,0:T(8,128)(2,1)}, bf16[128,512]{1,0:T(8,128)(2,1)S(1)}, u32[]{:S(2)}, u32[]{:S(2)}) collective-permute-start(bf16[128,512]{1,0:T(8,128)(2,1)} %refs_8_.4), channel_id=1, source_target_pairs={{0,3},{1,2},{2,1},{3,0},{4,7},{5,6},{6,5},{7,4},{8,11},{9,10},{10,... | collective-permute-start | bytes 393224 | tf_op jit(solution)/shard_map/ppermute | solution.py:34
  2.7 1.6 %copy-done = bf16[64,64,256]{2,1,0:T(8,128)(2,1)S(1)} copy-done((bf16[64,64,256]{2,1,0:T(8,128)(2,1)S(1)}, bf16[64,64,256]{2,1,0:T(8,128)(2,1)}, u32[]{:S(2)}) %copy-start) | copy-done | bytes 2097176
  5.2 2.4 %collective-permute-start.3 = (bf16[4,64,256]{2,1,0:T(8,128)(2,1)S(1)}, bf16[4,64,256]{2,1,0:T(8,128)(2,1)S(1)}, u32[]{:S(2)}, u32[]{:S(2)}) collective-permute-start(bf16[4,64,256]{2,1,0:T(8,128)(2,1)S(1)} %get-tuple-element.41), channel_id=1, source_target_pairs={{0,16},{4,20},{8,24},{12,28},{16,0},{20,4},{24,8},{28,12},{1,17},{... | collective-permute-start | bytes 393224 | tf_op jit(solution)/shard_map/ppermute | solution.py:34
  7.6 1.7 %collective-permute-start.4 = (bf16[4,64,256]{2,1,0:T(8,128)(2,1)S(1)}, bf16[4,64,256]{2,1,0:T(8,128)(2,1)S(1)}, u32[]{:S(2)}, u32[]{:S(2)}) collective-permute-start(bf16[4,64,256]{2,1,0:T(8,128)(2,1)S(1)} %get-tuple-element.42), channel_id=1, source_target_pairs={{0,20},{4,16},{8,28},{12,24},{16,4},{20,0},{24,12},{28,8},{1,21},{... | collective-permute-start | bytes 393224 | tf_op jit(solution)/shard_map/ppermute | solution.py:34
  11.0 2.1 %split.2 = (bf16[4,64,256]{2,1,0:T(8,128)(2,1)S(1)}, bf16[4,64,256]{2,1,0:T(8,128)(2,1)S(1)}, bf16[4,64,256]{2,1,0:T(8,128)(2,1)S(1)}, bf16[4,64,256]{2,1,0:T(8,...) custom-call(bf16[64,64,256]{2,1,0:T(8,128)(2,1)S(1)} %copy-done), custom_call_target="tpu_custom_call" | custom-call | flops 100000000 | bytes 1000000 | tf_op jit(solution)/shard_map/split/pallas_call | solution.py:85
  13.4 8.5 %collective-permute-done.3.refs_4_ = bf16[4,64,256]{2,1,0:T(8,128)(2,1)S(1)} collective-permute-done((bf16[4,64,256]{2,1,0:T(8,128)(2,1)S(1)}, bf16[4,64,256]{2,1,0:T(8,128)(2,1)S(1)}, u32[]{:S(2)}, u32[]{:S(2)}) %collective-permute-start.3) | collective-permute-done | bytes 131104 | tf_op jit(solution)/shard_map/ppermute | solution.py:34
  21.9 2.8 %collective-permute-done.4.refs_5_ = bf16[4,64,256]{2,1,0:T(8,128)(2,1)S(1)} collective-permute-done((bf16[4,64,256]{2,1,0:T(8,128)(2,1)S(1)}, bf16[4,64,256]{2,1,0:T(8,128)(2,1)S(1)}, u32[]{:S(2)}, u32[]{:S(2)}) %collective-permute-start.4) | collective-permute-done | bytes 131104 | tf_op jit(solution)/shard_map/ppermute | solution.py:34
  25.1 2.5 %collective-permute-done.5.refs_6_ = bf16[4,64,256]{2,1,0:T(8,128)(2,1)S(1)} collective-permute-done((bf16[4,64,256]{2,1,0:T(8,128)(2,1)S(1)}, bf16[4,64,256]{2,1,0:T(8,128)(2,1)S(1)}, u32[]{:S(2)}, u32[]{:S(2)}) %collective-permute-start.5) | collective-permute-done | bytes 131104 | tf_op jit(solution)/shard_map/ppermute | solution.py:34
  30.4 2.1 %collective-permute-start.13 = (bf16[4,64,256]{2,1,0:T(8,128)(2,1)S(1)}, bf16[4,64,256]{2,1,0:T(8,128)(2,1)S(1)}, u32[]{:S(2)}, u32[]{:S(2)}) collective-permute-start(bf16[4,64,256]{2,1,0:T(8,128)(2,1)S(1)} %get-tuple-element.49), channel_id=1, source_target_pairs={{0,12},{4,8},{8,4},{12,0},{16,28},{20,24},{24,20},{28,16},{1,13},{... | collective-permute-start | bytes 393224 | tf_op jit(solution)/shard_map/ppermute | solution.py:34
  34.8 2.2 %collective-permute-start.16 = (bf16[4,64,256]{2,1,0:T(8,128)(2,1)S(1)}, bf16[4,64,256]{2,1,0:T(8,128)(2,1)S(1)}, u32[]{:S(2)}, u32[]{:S(2)}) collective-permute-start(bf16[4,64,256]{2,1,0:T(8,128)(2,1)S(1)} %get-tuple-element.52), channel_id=1, source_target_pairs={{0,24},{4,28},{8,16},{12,20},{16,8},{20,12},{24,0},{28,4},{1,25},{... | collective-permute-start | bytes 393224 | tf_op jit(solution)/shard_map/ppermute | solution.py:34
  39.2 4.5 %layer.2 = (bf16[4,64,256]{2,1,0:T(8,128)(2,1)S(1)}, bf16[4,64,256]{2,1,0:T(8,128)(2,1)S(1)}, bf16[4,64,256]{2,1,0:T(8,128)(2,1)S(1)}, bf16[4,64,256]{2,1,0:T(8,...) custom-call(bf16[4,64,256]{2,1,0:T(8,128)(2,1)S(1)} %get-tuple-eleme, ...), custom_call_target="tpu_custom_call" | custom-call | flops 536870912 | bytes 2097152 | tf_op jit(solution)/shard_map/layer/pallas_call | solution.py:193
  43.7 2.4 %collective-permute-start.21 = (bf16[4,64,256]{2,1,0:T(8,128)(2,1)S(1)}, bf16[4,64,256]{2,1,0:T(8,128)(2,1)S(1)}, u32[]{:S(2)}, u32[]{:S(2)}) collective-permute-start(bf16[4,64,256]{2,1,0:T(8,128)(2,1)S(1)} %get-tuple-element.57), channel_id=1, source_target_pairs={{20,0},{16,4},{28,8},{24,12},{4,16},{0,20},{12,24},{8,28},{21,1},{... | collective-permute-start | bytes 393224 | tf_op jit(solution)/shard_map/ppermute | solution.py:34
  46.1 10.0 %collective-permute-done.15.refs_5_ = bf16[4,64,256]{2,1,0:T(8,128)(2,1)S(1)} collective-permute-done((bf16[4,64,256]{2,1,0:T(8,128)(2,1)S(1)}, bf16[4,64,256]{2,1,0:T(8,128)(2,1)S(1)}, u32[]{:S(2)}, u32[]{:S(2)}) %collective-permute-start.15) | collective-permute-done | bytes 131104 | tf_op jit(solution)/shard_map/ppermute | solution.py:34
  56.1 2.8 %collective-permute-start.25 = (bf16[4,64,256]{2,1,0:T(8,128)(2,1)S(1)}, bf16[4,64,256]{2,1,0:T(8,128)(2,1)S(1)}, u32[]{:S(2)}, u32[]{:S(2)}) collective-permute-start(bf16[4,64,256]{2,1,0:T(8,128)(2,1)S(1)} %get-tuple-element.63), channel_id=1, source_target_pairs={{4,0},{0,4},{12,8},{8,12},{20,16},{16,20},{28,24},{24,28},{5,1},{1... | collective-permute-start | bytes 393224 | tf_op jit(solution)/shard_map/ppermute | solution.py:34
  59.7 4.2 %collective-permute-done.17.refs_7_ = bf16[4,64,256]{2,1,0:T(8,128)(2,1)S(1)} collective-permute-done((bf16[4,64,256]{2,1,0:T(8,128)(2,1)S(1)}, bf16[4,64,256]{2,1,0:T(8,128)(2,1)S(1)}, u32[]{:S(2)}, u32[]{:S(2)}) %collective-permute-start.17) | collective-permute-done | bytes 131104 | tf_op jit(solution)/shard_map/ppermute | solution.py:34
  63.9 4.5 %layer.3 = (bf16[4,64,256]{2,1,0:T(8,128)(2,1)S(1)}, bf16[4,64,256]{2,1,0:T(8,128)(2,1)S(1)}, bf16[4,64,256]{2,1,0:T(8,128)(2,1)S(1)}, bf16[4,64,256]{2,1,0:T(8,...) custom-call(bf16[4,64,256]{2,1,0:T(8,128)(2,1)S(1)} %get-tuple-eleme, ...), custom_call_target="tpu_custom_call" | custom-call | flops 536870912 | bytes 2097152 | tf_op jit(solution)/shard_map/layer/pallas_call | solution.py:193
  68.4 1.6 %collective-permute-start.24 = (bf16[4,64,256]{2,1,0:T(8,128)(2,1)S(1)}, bf16[4,64,256]{2,1,0:T(8,128)(2,1)S(1)}, u32[]{:S(2)}, u32[]{:S(2)}) collective-permute-start(bf16[4,64,256]{2,1,0:T(8,128)(2,1)S(1)} %get-tuple-element.60), channel_id=1, source_target_pairs={{16,0},{20,4},{24,8},{28,12},{0,16},{4,20},{8,24},{12,28},{17,1},{... | collective-permute-start | bytes 393224 | tf_op jit(solution)/shard_map/ppermute | solution.py:34
  70.0 1.9 %collective-permute-start.26 = (bf16[4,64,256]{2,1,0:T(8,128)(2,1)S(1)}, bf16[4,64,256]{2,1,0:T(8,128)(2,1)S(1)}, u32[]{:S(2)}, u32[]{:S(2)}) collective-permute-start(bf16[4,64,256]{2,1,0:T(8,128)(2,1)S(1)} %get-tuple-element.64), channel_id=1, source_target_pairs={{4,0},{0,4},{12,8},{8,12},{20,16},{16,20},{28,24},{24,28},{5,1},{1... | collective-permute-start | bytes 393224 | tf_op jit(solution)/shard_map/ppermute | solution.py:34
  72.0 1.7 %collective-permute-start.30 = (bf16[4,64,256]{2,1,0:T(8,128)(2,1)S(1)}, bf16[4,64,256]{2,1,0:T(8,128)(2,1)S(1)}, u32[]{:S(2)}, u32[]{:S(2)}) collective-permute-start(bf16[4,64,256]{2,1,0:T(8,128)(2,1)S(1)} %get-tuple-element.68), channel_id=1, source_target_pairs={{12,0},{8,4},{4,8},{0,12},{28,16},{24,20},{20,24},{16,28},{13,1},{... | collective-permute-start | bytes 393224 | tf_op jit(solution)/shard_map/ppermute | solution.py:34
  77.2 3.1 %collective-permute-done.28.refs_5_ = bf16[4,64,256]{2,1,0:T(8,128)(2,1)S(1)} collective-permute-done((bf16[4,64,256]{2,1,0:T(8,128)(2,1)S(1)}, bf16[4,64,256]{2,1,0:T(8,128)(2,1)S(1)}, u32[]{:S(2)}, u32[]{:S(2)}) %collective-permute-start.28) | collective-permute-done | bytes 131104 | tf_op jit(solution)/shard_map/ppermute | solution.py:34
  80.3 2.3 %collective-permute-start.10 = (bf16[4,64,256]{2,1,0:T(8,128)(2,1)S(1)}, bf16[4,64,256]{2,1,0:T(8,128)(2,1)S(1)}, u32[]{:S(2)}, u32[]{:S(2)}) collective-permute-start(bf16[4,64,256]{2,1,0:T(8,128)(2,1)S(1)} %get-tuple-element.45), channel_id=1, source_target_pairs={{28,0},{24,4},{20,8},{16,12},{12,16},{8,20},{4,24},{0,28},{29,1},{... | collective-permute-start | bytes 393224 | tf_op jit(solution)/shard_map/ppermute | solution.py:34
  82.6 9.2 %collective-permute-done.30.refs_7_ = bf16[4,64,256]{2,1,0:T(8,128)(2,1)S(1)} collective-permute-done((bf16[4,64,256]{2,1,0:T(8,128)(2,1)S(1)}, bf16[4,64,256]{2,1,0:T(8,128)(2,1)S(1)}, u32[]{:S(2)}, u32[]{:S(2)}) %collective-permute-start.30) | collective-permute-done | bytes 131104 | tf_op jit(solution)/shard_map/ppermute | solution.py:34
  98.3 4.7 %collective-permute-done.10.refs_0_ = bf16[4,64,256]{2,1,0:T(8,128)(2,1)S(1)} collective-permute-done((bf16[4,64,256]{2,1,0:T(8,128)(2,1)S(1)}, bf16[4,64,256]{2,1,0:T(8,128)(2,1)S(1)}, u32[]{:S(2)}, u32[]{:S(2)}) %collective-permute-start.10) | collective-permute-done | bytes 131104 | tf_op jit(solution)/shard_map/ppermute | solution.py:34
  103.1 2.7 %collective-permute-done.18.refs_1_ = bf16[4,64,256]{2,1,0:T(8,128)(2,1)S(1)} collective-permute-done((bf16[4,64,256]{2,1,0:T(8,128)(2,1)S(1)}, bf16[4,64,256]{2,1,0:T(8,128)(2,1)S(1)}, u32[]{:S(2)}, u32[]{:S(2)}) %collective-permute-start.18) | collective-permute-done | bytes 131104 | tf_op jit(solution)/shard_map/ppermute | solution.py:34
  (58 shorter events, 22.9 us)
Async XLA Ops:
  0.0 9.3 %collective-permute-start.9 = (bf16[128,512]{1,0:T(8,128)(2,1)}, bf16[128,512]{1,0:T(8,128)(2,1)S(1)}, u32[]{:S(2)}, u32[]{:S(2)}) collective-permute-start(bf16[128,512]{1,0:T(8,128)(2,1)} %refs_8_.4), channel_id=1, source_target_pairs={{0,3},{1,2},{2,1},{3,0},{4,7},{5,6},{6,5},{7,4},{8,11},{9,10},{10,... | collective-permute-start | bytes 393224 | tf_op jit(solution)/shard_map/ppermute | solution.py:34
  2.4 10.8 %collective-permute-start.7 = (bf16[128,512]{1,0:T(8,128)(2,1)}, bf16[128,512]{1,0:T(8,128)(2,1)S(1)}, u32[]{:S(2)}, u32[]{:S(2)}) collective-permute-start(bf16[128,512]{1,0:T(8,128)(2,1)} %refs_8_.4), channel_id=1, source_target_pairs={{0,1},{1,0},{2,3},{3,2},{4,5},{5,4},{6,7},{7,6},{8,9},{9,8},{10,11... | collective-permute-start | bytes 393224 | tf_op jit(solution)/shard_map/ppermute | solution.py:34
  5.2 16.7 %collective-permute-start.3 = (bf16[4,64,256]{2,1,0:T(8,128)(2,1)S(1)}, bf16[4,64,256]{2,1,0:T(8,128)(2,1)S(1)}, u32[]{:S(2)}, u32[]{:S(2)}) collective-permute-start(bf16[4,64,256]{2,1,0:T(8,128)(2,1)S(1)} %get-tuple-element.41), channel_id=1, source_target_pairs={{0,16},{4,20},{8,24},{12,28},{16,0},{20,4},{24,8},{28,12},{1,17},{... | collective-permute-start | bytes 393224 | tf_op jit(solution)/shard_map/ppermute | solution.py:34
  7.6 17.2 %collective-permute-start.4 = (bf16[4,64,256]{2,1,0:T(8,128)(2,1)S(1)}, bf16[4,64,256]{2,1,0:T(8,128)(2,1)S(1)}, u32[]{:S(2)}, u32[]{:S(2)}) collective-permute-start(bf16[4,64,256]{2,1,0:T(8,128)(2,1)S(1)} %get-tuple-element.42), channel_id=1, source_target_pairs={{0,20},{4,16},{8,28},{12,24},{16,4},{20,0},{24,12},{28,8},{1,21},{... | collective-permute-start | bytes 393224 | tf_op jit(solution)/shard_map/ppermute | solution.py:34
  9.3 18.2 %collective-permute-start.5 = (bf16[4,64,256]{2,1,0:T(8,128)(2,1)S(1)}, bf16[4,64,256]{2,1,0:T(8,128)(2,1)S(1)}, u32[]{:S(2)}, u32[]{:S(2)}) collective-permute-start(bf16[4,64,256]{2,1,0:T(8,128)(2,1)S(1)} %get-tuple-element.43), channel_id=1, source_target_pairs={{0,24},{4,28},{8,16},{12,20},{16,8},{20,12},{24,0},{28,4},{1,25},{... | collective-permute-start | bytes 393224 | tf_op jit(solution)/shard_map/ppermute | solution.py:34
  10.6 19.7 %collective-permute-start.6 = (bf16[4,64,256]{2,1,0:T(8,128)(2,1)S(1)}, bf16[4,64,256]{2,1,0:T(8,128)(2,1)S(1)}, u32[]{:S(2)}, u32[]{:S(2)}) collective-permute-start(bf16[4,64,256]{2,1,0:T(8,128)(2,1)S(1)} %get-tuple-element.44), channel_id=1, source_target_pairs={{0,28},{4,24},{8,20},{12,16},{16,12},{20,8},{24,4},{28,0},{1,29},{... | collective-permute-start | bytes 393224 | tf_op jit(solution)/shard_map/ppermute | solution.py:34
  13.2 17.2 %collective-permute-start = (bf16[4,64,256]{2,1,0:T(8,128)(2,1)S(1)}, bf16[4,64,256]{2,1,0:T(8,128)(2,1)S(1)}, u32[]{:S(2)}, u32[]{:S(2)}) collective-permute-start(bf16[4,64,256]{2,1,0:T(8,128)(2,1)S(1)} %get-tuple-element.38), channel_id=1, source_target_pairs={{0,4},{4,0},{8,12},{12,8},{16,20},{20,16},{24,28},{28,24},{1,5},{5... | collective-permute-start | bytes 393224 | tf_op jit(solution)/shard_map/ppermute | solution.py:34
  21.9 10.6 %collective-permute-start.1 = (bf16[4,64,256]{2,1,0:T(8,128)(2,1)S(1)}, bf16[4,64,256]{2,1,0:T(8,128)(2,1)S(1)}, u32[]{:S(2)}, u32[]{:S(2)}) collective-permute-start(bf16[4,64,256]{2,1,0:T(8,128)(2,1)S(1)} %get-tuple-element.39), channel_id=1, source_target_pairs={{0,8},{4,12},{8,0},{12,4},{16,24},{20,28},{24,16},{28,20},{1,9},{5... | collective-permute-start | bytes 393224 | tf_op jit(solution)/shard_map/ppermute | solution.py:34
  30.4 13.3 %collective-permute-start.13 = (bf16[4,64,256]{2,1,0:T(8,128)(2,1)S(1)}, bf16[4,64,256]{2,1,0:T(8,128)(2,1)S(1)}, u32[]{:S(2)}, u32[]{:S(2)}) collective-permute-start(bf16[4,64,256]{2,1,0:T(8,128)(2,1)S(1)} %get-tuple-element.49), channel_id=1, source_target_pairs={{0,12},{4,8},{8,4},{12,0},{16,28},{20,24},{24,20},{28,16},{1,13},{... | collective-permute-start | bytes 393224 | tf_op jit(solution)/shard_map/ppermute | solution.py:34
  32.5 13.6 %collective-permute-start.14 = (bf16[4,64,256]{2,1,0:T(8,128)(2,1)S(1)}, bf16[4,64,256]{2,1,0:T(8,128)(2,1)S(1)}, u32[]{:S(2)}, u32[]{:S(2)}) collective-permute-start(bf16[4,64,256]{2,1,0:T(8,128)(2,1)S(1)} %get-tuple-element.50), channel_id=1, source_target_pairs={{0,16},{4,20},{8,24},{12,28},{16,0},{20,4},{24,8},{28,12},{1,17},{... | collective-permute-start | bytes 393224 | tf_op jit(solution)/shard_map/ppermute | solution.py:34
  34.0 22.1 %collective-permute-start.15 = (bf16[4,64,256]{2,1,0:T(8,128)(2,1)S(1)}, bf16[4,64,256]{2,1,0:T(8,128)(2,1)S(1)}, u32[]{:S(2)}, u32[]{:S(2)}) collective-permute-start(bf16[4,64,256]{2,1,0:T(8,128)(2,1)S(1)} %get-tuple-element.51), channel_id=1, source_target_pairs={{0,20},{4,16},{8,28},{12,24},{16,4},{20,0},{24,12},{28,8},{1,21},{... | collective-permute-start | bytes 393224 | tf_op jit(solution)/shard_map/ppermute | solution.py:34
  34.8 24.9 %collective-permute-start.16 = (bf16[4,64,256]{2,1,0:T(8,128)(2,1)S(1)}, bf16[4,64,256]{2,1,0:T(8,128)(2,1)S(1)}, u32[]{:S(2)}, u32[]{:S(2)}) collective-permute-start(bf16[4,64,256]{2,1,0:T(8,128)(2,1)S(1)} %get-tuple-element.52), channel_id=1, source_target_pairs={{0,24},{4,28},{8,16},{12,20},{16,8},{20,12},{24,0},{28,4},{1,25},{... | collective-permute-start | bytes 393224 | tf_op jit(solution)/shard_map/ppermute | solution.py:34
  37.9 26.0 %collective-permute-start.17 = (bf16[4,64,256]{2,1,0:T(8,128)(2,1)S(1)}, bf16[4,64,256]{2,1,0:T(8,128)(2,1)S(1)}, u32[]{:S(2)}, u32[]{:S(2)}) collective-permute-start(bf16[4,64,256]{2,1,0:T(8,128)(2,1)S(1)} %get-tuple-element.53), channel_id=1, source_target_pairs={{0,28},{4,24},{8,20},{12,16},{16,12},{20,8},{24,4},{28,0},{1,29},{... | collective-permute-start | bytes 393224 | tf_op jit(solution)/shard_map/ppermute | solution.py:34
  43.7 24.7 %collective-permute-start.21 = (bf16[4,64,256]{2,1,0:T(8,128)(2,1)S(1)}, bf16[4,64,256]{2,1,0:T(8,128)(2,1)S(1)}, u32[]{:S(2)}, u32[]{:S(2)}) collective-permute-start(bf16[4,64,256]{2,1,0:T(8,128)(2,1)S(1)} %get-tuple-element.57), channel_id=1, source_target_pairs={{20,0},{16,4},{28,8},{24,12},{4,16},{0,20},{12,24},{8,28},{21,1},{... | collective-permute-start | bytes 393224 | tf_op jit(solution)/shard_map/ppermute | solution.py:34
  46.1 23.9 %collective-permute-start.23 = (bf16[4,64,256]{2,1,0:T(8,128)(2,1)S(1)}, bf16[4,64,256]{2,1,0:T(8,128)(2,1)S(1)}, u32[]{:S(2)}, u32[]{:S(2)}) collective-permute-start(bf16[4,64,256]{2,1,0:T(8,128)(2,1)S(1)} %get-tuple-element.59), channel_id=1, source_target_pairs={{16,0},{20,4},{24,8},{28,12},{0,16},{4,20},{8,24},{12,28},{17,1},{... | collective-permute-start | bytes 393224 | tf_op jit(solution)/shard_map/ppermute | solution.py:34
  56.1 15.8 %collective-permute-start.25 = (bf16[4,64,256]{2,1,0:T(8,128)(2,1)S(1)}, bf16[4,64,256]{2,1,0:T(8,128)(2,1)S(1)}, u32[]{:S(2)}, u32[]{:S(2)}) collective-permute-start(bf16[4,64,256]{2,1,0:T(8,128)(2,1)S(1)} %get-tuple-element.63), channel_id=1, source_target_pairs={{4,0},{0,4},{12,8},{8,12},{20,16},{16,20},{28,24},{24,28},{5,1},{1... | collective-permute-start | bytes 393224 | tf_op jit(solution)/shard_map/ppermute | solution.py:34
  59.7 12.3 %collective-permute-start.27 = (bf16[4,64,256]{2,1,0:T(8,128)(2,1)S(1)}, bf16[4,64,256]{2,1,0:T(8,128)(2,1)S(1)}, u32[]{:S(2)}, u32[]{:S(2)}) collective-permute-start(bf16[4,64,256]{2,1,0:T(8,128)(2,1)S(1)} %get-tuple-element.65), channel_id=1, source_target_pairs={{8,0},{12,4},{0,8},{4,12},{24,16},{28,20},{16,24},{20,28},{9,1},{1... | collective-permute-start | bytes 393224 | tf_op jit(solution)/shard_map/ppermute | solution.py:34
  63.9 9.8 %collective-permute-start.29 = (bf16[4,64,256]{2,1,0:T(8,128)(2,1)S(1)}, bf16[4,64,256]{2,1,0:T(8,128)(2,1)S(1)}, u32[]{:S(2)}, u32[]{:S(2)}) collective-permute-start(bf16[4,64,256]{2,1,0:T(8,128)(2,1)S(1)} %get-tuple-element.67), channel_id=1, source_target_pairs={{12,0},{8,4},{4,8},{0,12},{28,16},{24,20},{20,24},{16,28},{13,1},{... | collective-permute-start | bytes 393224 | tf_op jit(solution)/shard_map/ppermute | solution.py:34
  72.0 19.8 %collective-permute-start.30 = (bf16[4,64,256]{2,1,0:T(8,128)(2,1)S(1)}, bf16[4,64,256]{2,1,0:T(8,128)(2,1)S(1)}, u32[]{:S(2)}, u32[]{:S(2)}) collective-permute-start(bf16[4,64,256]{2,1,0:T(8,128)(2,1)S(1)} %get-tuple-element.68), channel_id=1, source_target_pairs={{12,0},{8,4},{4,8},{0,12},{28,16},{24,20},{20,24},{16,28},{13,1},{... | collective-permute-start | bytes 393224 | tf_op jit(solution)/shard_map/ppermute | solution.py:34
  73.7 22.0 %collective-permute-start.22 = (bf16[4,64,256]{2,1,0:T(8,128)(2,1)S(1)}, bf16[4,64,256]{2,1,0:T(8,128)(2,1)S(1)}, u32[]{:S(2)}, u32[]{:S(2)}) collective-permute-start(bf16[4,64,256]{2,1,0:T(8,128)(2,1)S(1)} %get-tuple-element.58), channel_id=1, source_target_pairs={{20,0},{16,4},{28,8},{24,12},{4,16},{0,20},{12,24},{8,28},{21,1},{... | collective-permute-start | bytes 393224 | tf_op jit(solution)/shard_map/ppermute | solution.py:34
  75.8 20.9 %collective-permute-start.19 = (bf16[4,64,256]{2,1,0:T(8,128)(2,1)S(1)}, bf16[4,64,256]{2,1,0:T(8,128)(2,1)S(1)}, u32[]{:S(2)}, u32[]{:S(2)}) collective-permute-start(bf16[4,64,256]{2,1,0:T(8,128)(2,1)S(1)} %get-tuple-element.55), channel_id=1, source_target_pairs={{24,0},{28,4},{16,8},{20,12},{8,16},{12,20},{0,24},{4,28},{25,1},{... | collective-permute-start | bytes 393224 | tf_op jit(solution)/shard_map/ppermute | solution.py:34
  77.0 20.4 %collective-permute-start.20 = (bf16[4,64,256]{2,1,0:T(8,128)(2,1)S(1)}, bf16[4,64,256]{2,1,0:T(8,128)(2,1)S(1)}, u32[]{:S(2)}, u32[]{:S(2)}) collective-permute-start(bf16[4,64,256]{2,1,0:T(8,128)(2,1)S(1)} %get-tuple-element.56), channel_id=1, source_target_pairs={{24,0},{28,4},{16,8},{20,12},{8,16},{12,20},{0,24},{4,28},{25,1},{... | collective-permute-start | bytes 393224 | tf_op jit(solution)/shard_map/ppermute | solution.py:34
  80.3 22.8 %collective-permute-start.10 = (bf16[4,64,256]{2,1,0:T(8,128)(2,1)S(1)}, bf16[4,64,256]{2,1,0:T(8,128)(2,1)S(1)}, u32[]{:S(2)}, u32[]{:S(2)}) collective-permute-start(bf16[4,64,256]{2,1,0:T(8,128)(2,1)S(1)} %get-tuple-element.45), channel_id=1, source_target_pairs={{28,0},{24,4},{20,8},{16,12},{12,16},{8,20},{4,24},{0,28},{29,1},{... | collective-permute-start | bytes 393224 | tf_op jit(solution)/shard_map/ppermute | solution.py:34
  91.8 14.0 %collective-permute-start.18 = (bf16[4,64,256]{2,1,0:T(8,128)(2,1)S(1)}, bf16[4,64,256]{2,1,0:T(8,128)(2,1)S(1)}, u32[]{:S(2)}, u32[]{:S(2)}) collective-permute-start(bf16[4,64,256]{2,1,0:T(8,128)(2,1)S(1)} %get-tuple-element.54), channel_id=1, source_target_pairs={{28,0},{24,4},{20,8},{16,12},{12,16},{8,20},{4,24},{0,28},{29,1},{... | collective-permute-start | bytes 393224 | tf_op jit(solution)/shard_map/ppermute | solution.py:34
  (12 other events, 287.0 us)
where the time goes:
time: 107 us
  waiting for transfers between devices  51.4 us (48%)
  starting transfers between devices  35.4 us (33%)
  Pallas kernels  17.3 us (16%)
  local copies, waits for them, and re-layouts  2.49 us (2%)
    ppermute x31, waiting for transfers between devices, send(): return lax.ppermute(value, axis, pairs)  51.4 us
    ppermute x31, starting transfers between devices, send(): return lax.ppermute(value, axis, pairs)  35.4 us
    pallas_call x2, Pallas kernels, layer(): pl.pallas_call(functools.partial(layer_kernel, count, len(weights)), out_...  8.98 us
    pallas_call x5, Pallas kernels, merge(): pl.pallas_call(functools.partial(merge_kernel, messages, chunks, count, f...  5.22 us
    pallas_call x2, Pallas kernels, split(): pl.pallas_call(functools.partial(split_kernel, messages, chunks, count),...  3.09 us
    unnamed x11, local copies, waits for them, and re-layouts  2.49 us
  transfers between devices with their start and end apart: 31, of which 13 were waited for; matrix products, arithmetic and copies ran while one was open for 1% of the time, Pallas kernels for 15%

commit v1 on v0

--- a/solution.py
+++ b/solution.py
@@ -77,7 +77,7 @@
                 outs[q][:, b * block : (b + 1) * block, :] = moved.astype(jnp.bfloat16).reshape(part, block, width)
 
 
-def split(x, messages, chunks, count):
+def split(x, messages, chunks, count, first):
     rows, _, width = x.shape
     part = GROUP // chunks
     distinct = len({m for m, _ in messages})
@@ -94,7 +94,7 @@
         compiler_params=pltpu.CompilerParams(vmem_limit_bytes=12 * 1024 * 1024),
         cost_estimate=pl.CostEstimate(flops=10**8, bytes_accessed=10**6, transcendentals=0),
         name="split",
-    )(x)
+    )(pltpu.with_memory_space_constraint(x, pltpu.HBM) if first else x)
 
 
 def merge_kernel(messages, chunks, count, first, *refs):
@@ -167,7 +167,7 @@
         for m in range(count):
             held[pl.ds(starts[m], rows), :] = blocks[m][s]
         x = held[...]
-        summed = lax.dot_general(proj_ref[...], x, (((0,), (0,)), ((), ())), preferred_element_type=jnp.float32)
+        summed = jnp.dot(proj_ref[...], x, preferred_element_type=jnp.float32)
         factor = summed.astype(jnp.bfloat16)
         inner = lax.dot_general(x, factor, (((1,), (1,)), ((), ())), preferred_element_type=jnp.float32)
         fmb = jnp.dot(inner.astype(jnp.bfloat16), fmb_ref[...], preferred_element_type=jnp.float32)
@@ -215,7 +215,7 @@
     share = samples // count
     chunks = 2 if share % 2 == 0 else 1
     part = share // chunks
-    far = [m for m in range(count) if m >= count // 2]
+    far = [m for m in range(count - 1, 0, -1) if m >= count // 2]
     near = [m for m in range(1, count) if m < count // 2]
     fast = share == GROUP
     sends = {}
@@ -223,7 +223,7 @@
     if fast:
 
         def cut(names):
-            sends.update(zip(names, split(embeddings, names, chunks, count)))
+            sends.update(zip(names, split(embeddings, names, chunks, count, not sends)))
 
     else:
         turned = embeddings.reshape(rows, count, chunks, part, width).transpose(1, 2, 3, 0, 4)
@@ -239,25 +239,25 @@
         for m, c in names:
             arrived[m, c] = send(sends[m, c], m, "emb", count)
 
-    cut([(m, 0) for m in far])
-    forward([(m, 0) for m in far])
-    cut([(m, 0) for m in near] + [(0, 0)] + [(m, c) for c in range(1, chunks) for m in far + near + [0]])
-    forward([(m, 0) for m in near + [0]])
+    cut([(m, 0) for m in far[:2]])
+    forward([(m, 0) for m in far[:2]])
+    cut([(m, 0) for m in far[2:] + near + [0]] + [(m, c) for c in range(1, chunks) for m in far + near + [0]])
+    forward([(m, 0) for m in far[2:] + near + [0]])
     weights = []
     for q in range(others):
         weights.append(send(w_lcb, q, "dp", others))
     for c in range(1, chunks):
-        forward([(m, c) for m in far + near + [0]])
+        forward([(m, c) for m in near + far + [0]])
 
     returned = {}
     for c in range(chunks):
-        done = layer([arrived[m, c] for m in range(count)], weights, machine_projection, w_fmb)
+        done = layer([arrived[m, c] for m in range(count)], weights, machine_projection.T, w_fmb)
         for m in near + far + [0]:
             returned[m, c] = send(done[m], m, "emb", count, back=True)
 
     if fast:
         out = None
-        for messages in [[0] + near] + [[m] for m in far]:
+        for messages in [[0] + near] + [[m] for m in far[::-1]]:
             pieces = [returned[m, c] for m in messages for c in range(chunks)]
             out = merge(out, pieces, ln_gain, ln_bias, messages, chunks, count, samples)
         return out

time: 107 us -> 102 us (0.953)
  the two profiles are of different devices: /device:TPU:9 before, /device:TPU:15 now
where the time goes in v1:
time: 102 us
  starting transfers between devices  42.5 us (42%)
  waiting for transfers between devices  41.4 us (41%)
  Pallas kernels  17.7 us (17%)
    ppermute x31, starting transfers between devices, send(): return lax.ppermute(value, axis, pairs)  42.5 us
    ppermute x31, waiting for transfers between devices, send(): return lax.ppermute(value, axis, pairs)  41.4 us
    pallas_call x2, Pallas kernels, layer(): pl.pallas_call(functools.partial(layer_kernel, count, len(weights)), out_...  8.87 us
    pallas_call x5, Pallas kernels, merge(): pl.pallas_call(functools.partial(merge_kernel, messages, chunks, count, f...  5.23 us
    pallas_call x2, Pallas kernels, split(): pl.pallas_call(functools.partial(split_kernel, messages, chunks, count),...  3.57 us
  transfers between devices with their start and end apart: 31, of which 12 were waited for; matrix products, arithmetic and copies ran while one was open for 0% of the time, Pallas kernels for 16%

profile of v1, /device:TPU:15, one launch (start us, length us, event | category | flops | bytes accessed | tf_op | source)
XLA Modules:
  0.0 101.8 jit_solution(14084157532932765036)
XLA Ops:
  5.5 1.9 %collective-permute-start.6 = (bf16[4,64,256]{2,1,0:T(8,128)(2,1)S(1)}, bf16[4,64,256]{2,1,0:T(8,128)(2,1)S(1)}, u32[]{:S(2)}, u32[]{:S(2)}) collective-permute-start(bf16[4,64,256]{2,1,0:T(8,128)(2,1)S(1)} %get-tuple-element.44), channel_id=1, source_target_pairs={{0,28},{4,24},{8,20},{12,16},{16,12},{20,8},{24,4},{28,0},{1,29},{... | collective-permute-start | bytes 393224 | tf_op jit(solution)/shard_map/ppermute | solution.py:34
  7.3 2.2 %split.2 = (bf16[4,64,256]{2,1,0:T(8,128)(2,1)S(1)}, bf16[4,64,256]{2,1,0:T(8,128)(2,1)S(1)}, bf16[4,64,256]{2,1,0:T(8,128)(2,1)S(1)}, bf16[4,64,256]{2,1,0:T(8,...) custom-call(bf16[64,64,256]{2,1,0:T(8,128)(2,1)S(1)} %copy-done), custom_call_target="tpu_custom_call" | custom-call | flops 100000000 | bytes 1000000 | tf_op jit(solution)/shard_map/split/pallas_call | solution.py:85
  9.7 2.1 %collective-permute-start.1 = (bf16[4,64,256]{2,1,0:T(8,128)(2,1)S(1)}, bf16[4,64,256]{2,1,0:T(8,128)(2,1)S(1)}, u32[]{:S(2)}, u32[]{:S(2)}) collective-permute-start(bf16[4,64,256]{2,1,0:T(8,128)(2,1)S(1)} %get-tuple-element.39), channel_id=1, source_target_pairs={{0,8},{4,12},{8,0},{12,4},{16,24},{20,28},{24,16},{28,20},{1,9},{5... | collective-permute-start | bytes 393224 | tf_op jit(solution)/shard_map/ppermute | solution.py:34
  12.1 3.8 %collective-permute-start.3 = (bf16[4,64,256]{2,1,0:T(8,128)(2,1)S(1)}, bf16[4,64,256]{2,1,0:T(8,128)(2,1)S(1)}, u32[]{:S(2)}, u32[]{:S(2)}) collective-permute-start(bf16[4,64,256]{2,1,0:T(8,128)(2,1)S(1)} %get-tuple-element.41), channel_id=1, source_target_pairs={{0,16},{4,20},{8,24},{12,28},{16,0},{20,4},{24,8},{28,12},{1,17},{... | collective-permute-start | bytes 393224 | tf_op jit(solution)/shard_map/ppermute | solution.py:34
  15.9 3.2 %collective-permute-done.6.refs_7_ = bf16[4,64,256]{2,1,0:T(8,128)(2,1)S(1)} collective-permute-done((bf16[4,64,256]{2,1,0:T(8,128)(2,1)S(1)}, bf16[4,64,256]{2,1,0:T(8,128)(2,1)S(1)}, u32[]{:S(2)}, u32[]{:S(2)}) %collective-permute-start.6) | collective-permute-done | bytes 131104 | tf_op jit(solution)/shard_map/ppermute | solution.py:34
  20.1 3.6 %collective-permute-start.12 = (bf16[4,64,256]{2,1,0:T(8,128)(2,1)S(1)}, bf16[4,64,256]{2,1,0:T(8,128)(2,1)S(1)}, u32[]{:S(2)}, u32[]{:S(2)}) collective-permute-start(bf16[4,64,256]{2,1,0:T(8,128)(2,1)S(1)} %get-tuple-element.48), channel_id=1, source_target_pairs={{0,8},{4,12},{8,0},{12,4},{16,24},{20,28},{24,16},{28,20},{1,9},{5... | collective-permute-start | bytes 393224 | tf_op jit(solution)/shard_map/ppermute | solution.py:34
  24.9 2.6 %collective-permute-done.4.refs_5_ = bf16[4,64,256]{2,1,0:T(8,128)(2,1)S(1)} collective-permute-done((bf16[4,64,256]{2,1,0:T(8,128)(2,1)S(1)}, bf16[4,64,256]{2,1,0:T(8,128)(2,1)S(1)}, u32[]{:S(2)}, u32[]{:S(2)}) %collective-permute-start.4) | collective-permute-done | bytes 131104 | tf_op jit(solution)/shard_map/ppermute | solution.py:34
  27.5 3.5 %collective-permute-start.15 = (bf16[4,64,256]{2,1,0:T(8,128)(2,1)S(1)}, bf16[4,64,256]{2,1,0:T(8,128)(2,1)S(1)}, u32[]{:S(2)}, u32[]{:S(2)}) collective-permute-start(bf16[4,64,256]{2,1,0:T(8,128)(2,1)S(1)} %get-tuple-element.51), channel_id=1, source_target_pairs={{0,20},{4,16},{8,28},{12,24},{16,4},{20,0},{24,12},{28,8},{1,21},{... | collective-permute-start | bytes 393224 | tf_op jit(solution)/shard_map/ppermute | solution.py:34
  32.0 3.8 %collective-permute-start.17 = (bf16[4,64,256]{2,1,0:T(8,128)(2,1)S(1)}, bf16[4,64,256]{2,1,0:T(8,128)(2,1)S(1)}, u32[]{:S(2)}, u32[]{:S(2)}) collective-permute-start(bf16[4,64,256]{2,1,0:T(8,128)(2,1)S(1)} %get-tuple-element.53), channel_id=1, source_target_pairs={{0,28},{4,24},{8,20},{12,16},{16,12},{20,8},{24,4},{28,0},{1,29},{... | collective-permute-start | bytes 393224 | tf_op jit(solution)/shard_map/ppermute | solution.py:34
  35.8 4.4 %layer.2 = (bf16[4,64,256]{2,1,0:T(8,128)(2,1)S(1)}, bf16[4,64,256]{2,1,0:T(8,128)(2,1)S(1)}, bf16[4,64,256]{2,1,0:T(8,128)(2,1)S(1)}, bf16[4,64,256]{2,1,0:T(8,...) custom-call(bf16[4,64,256]{2,1,0:T(8,128)(2,1)S(1)} %get-tuple-eleme, ...), custom_call_target="tpu_custom_call" | custom-call | flops 536870912 | bytes 2097152 | tf_op jit(solution)/shard_map/layer/pallas_call | solution.py:193
  40.2 1.6 %collective-permute-start.21 = (bf16[4,64,256]{2,1,0:T(8,128)(2,1)S(1)}, bf16[4,64,256]{2,1,0:T(8,128)(2,1)S(1)}, u32[]{:S(2)}, u32[]{:S(2)}) collective-permute-start(bf16[4,64,256]{2,1,0:T(8,128)(2,1)S(1)} %get-tuple-element.57), channel_id=1, source_target_pairs={{20,0},{16,4},{28,8},{24,12},{4,16},{0,20},{12,24},{8,28},{21,1},{... | collective-permute-start | bytes 393224 | tf_op jit(solution)/shard_map/ppermute | solution.py:34
  41.8 6.7 %collective-permute-done.15.refs_5_ = bf16[4,64,256]{2,1,0:T(8,128)(2,1)S(1)} collective-permute-done((bf16[4,64,256]{2,1,0:T(8,128)(2,1)S(1)}, bf16[4,64,256]{2,1,0:T(8,128)(2,1)S(1)}, u32[]{:S(2)}, u32[]{:S(2)}) %collective-permute-start.15) | collective-permute-done | bytes 131104 | tf_op jit(solution)/shard_map/ppermute | solution.py:34
  48.6 4.1 %collective-permute-start.25 = (bf16[4,64,256]{2,1,0:T(8,128)(2,1)S(1)}, bf16[4,64,256]{2,1,0:T(8,128)(2,1)S(1)}, u32[]{:S(2)}, u32[]{:S(2)}) collective-permute-start(bf16[4,64,256]{2,1,0:T(8,128)(2,1)S(1)} %get-tuple-element.63), channel_id=1, source_target_pairs={{4,0},{0,4},{12,8},{8,12},{20,16},{16,20},{28,24},{24,28},{5,1},{1... | collective-permute-start | bytes 393224 | tf_op jit(solution)/shard_map/ppermute | solution.py:34
  53.9 5.8 %collective-permute-done.17.refs_7_ = bf16[4,64,256]{2,1,0:T(8,128)(2,1)S(1)} collective-permute-done((bf16[4,64,256]{2,1,0:T(8,128)(2,1)S(1)}, bf16[4,64,256]{2,1,0:T(8,128)(2,1)S(1)}, u32[]{:S(2)}, u32[]{:S(2)}) %collective-permute-start.17) | collective-permute-done | bytes 131104 | tf_op jit(solution)/shard_map/ppermute | solution.py:34
  59.7 4.4 %layer.3 = (bf16[4,64,256]{2,1,0:T(8,128)(2,1)S(1)}, bf16[4,64,256]{2,1,0:T(8,128)(2,1)S(1)}, bf16[4,64,256]{2,1,0:T(8,128)(2,1)S(1)}, bf16[4,64,256]{2,1,0:T(8,...) custom-call(bf16[4,64,256]{2,1,0:T(8,128)(2,1)S(1)} %get-tuple-eleme, ...), custom_call_target="tpu_custom_call" | custom-call | flops 536870912 | bytes 2097152 | tf_op jit(solution)/shard_map/layer/pallas_call | solution.py:193
  65.2 1.7 %collective-permute-start.26 = (bf16[4,64,256]{2,1,0:T(8,128)(2,1)S(1)}, bf16[4,64,256]{2,1,0:T(8,128)(2,1)S(1)}, u32[]{:S(2)}, u32[]{:S(2)}) collective-permute-start(bf16[4,64,256]{2,1,0:T(8,128)(2,1)S(1)} %get-tuple-element.64), channel_id=1, source_target_pairs={{4,0},{0,4},{12,8},{8,12},{20,16},{16,20},{28,24},{24,28},{5,1},{1... | collective-permute-start | bytes 393224 | tf_op jit(solution)/shard_map/ppermute | solution.py:34
  67.0 1.7 %collective-permute-start.30 = (bf16[4,64,256]{2,1,0:T(8,128)(2,1)S(1)}, bf16[4,64,256]{2,1,0:T(8,128)(2,1)S(1)}, u32[]{:S(2)}, u32[]{:S(2)}) collective-permute-start(bf16[4,64,256]{2,1,0:T(8,128)(2,1)S(1)} %get-tuple-element.68), channel_id=1, source_target_pairs={{12,0},{8,4},{4,8},{0,12},{28,16},{24,20},{20,24},{16,28},{13,1},{... | collective-permute-start | bytes 393224 | tf_op jit(solution)/shard_map/ppermute | solution.py:34
  69.1 1.4 %collective-permute-done.24.refs_1_ = bf16[4,64,256]{2,1,0:T(8,128)(2,1)S(1)} collective-permute-done((bf16[4,64,256]{2,1,0:T(8,128)(2,1)S(1)}, bf16[4,64,256]{2,1,0:T(8,128)(2,1)S(1)}, u32[]{:S(2)}, u32[]{:S(2)}) %collective-permute-start.24) | collective-permute-done | bytes 131104 | tf_op jit(solution)/shard_map/ppermute | solution.py:34
  72.0 2.7 %collective-permute-done.28.refs_5_ = bf16[4,64,256]{2,1,0:T(8,128)(2,1)S(1)} collective-permute-done((bf16[4,64,256]{2,1,0:T(8,128)(2,1)S(1)}, bf16[4,64,256]{2,1,0:T(8,128)(2,1)S(1)}, u32[]{:S(2)}, u32[]{:S(2)}) %collective-permute-start.28) | collective-permute-done | bytes 131104 | tf_op jit(solution)/shard_map/ppermute | solution.py:34
  74.7 2.2 %collective-permute-start.10 = (bf16[4,64,256]{2,1,0:T(8,128)(2,1)S(1)}, bf16[4,64,256]{2,1,0:T(8,128)(2,1)S(1)}, u32[]{:S(2)}, u32[]{:S(2)}) collective-permute-start(bf16[4,64,256]{2,1,0:T(8,128)(2,1)S(1)} %get-tuple-element.45), channel_id=1, source_target_pairs={{28,0},{24,4},{20,8},{16,12},{12,16},{8,20},{4,24},{0,28},{29,1},{... | collective-permute-start | bytes 393224 | tf_op jit(solution)/shard_map/ppermute | solution.py:34
  82.6 8.1 %collective-permute-done.19.refs_0_ = bf16[4,64,256]{2,1,0:T(8,128)(2,1)S(1)} collective-permute-done((bf16[4,64,256]{2,1,0:T(8,128)(2,1)S(1)}, bf16[4,64,256]{2,1,0:T(8,128)(2,1)S(1)}, u32[]{:S(2)}, u32[]{:S(2)}) %collective-permute-start.19) | collective-permute-done | bytes 131104 | tf_op jit(solution)/shard_map/ppermute | solution.py:34
  90.7 2.8 %collective-permute-done.20.refs_1_ = bf16[4,64,256]{2,1,0:T(8,128)(2,1)S(1)} collective-permute-done((bf16[4,64,256]{2,1,0:T(8,128)(2,1)S(1)}, bf16[4,64,256]{2,1,0:T(8,128)(2,1)S(1)}, u32[]{:S(2)}, u32[]{:S(2)}) %collective-permute-start.20) | collective-permute-done | bytes 131104 | tf_op jit(solution)/shard_map/ppermute | solution.py:34
  94.5 4.4 %collective-permute-done.10.refs_0_ = bf16[4,64,256]{2,1,0:T(8,128)(2,1)S(1)} collective-permute-done((bf16[4,64,256]{2,1,0:T(8,128)(2,1)S(1)}, bf16[4,64,256]{2,1,0:T(8,128)(2,1)S(1)}, u32[]{:S(2)}, u32[]{:S(2)}) %collective-permute-start.10) | collective-permute-done | bytes 131104 | tf_op jit(solution)/shard_map/ppermute | solution.py:34
  98.9 1.9 %collective-permute-done.18.refs_1_ = bf16[4,64,256]{2,1,0:T(8,128)(2,1)S(1)} collective-permute-done((bf16[4,64,256]{2,1,0:T(8,128)(2,1)S(1)}, bf16[4,64,256]{2,1,0:T(8,128)(2,1)S(1)}, u32[]{:S(2)}, u32[]{:S(2)}) %collective-permute-start.18) | collective-permute-done | bytes 131104 | tf_op jit(solution)/shard_map/ppermute | solution.py:34
  (59 shorter events, 21.0 us)
Async XLA Ops:
  0.0 9.5 %collective-permute-start.9 = (bf16[128,512]{1,0:T(8,128)(2,1)}, bf16[128,512]{1,0:T(8,128)(2,1)S(1)}, u32[]{:S(2)}, u32[]{:S(2)}) collective-permute-start(bf16[128,512]{1,0:T(8,128)(2,1)} %refs_8_.4), channel_id=1, source_target_pairs={{0,3},{1,2},{2,1},{3,0},{4,7},{5,6},{6,5},{7,4},{8,11},{9,10},{10,... | collective-permute-start | bytes 393224 | tf_op jit(solution)/shard_map/ppermute | solution.py:34
  1.5 10.3 %collective-permute-start.7 = (bf16[128,512]{1,0:T(8,128)(2,1)}, bf16[128,512]{1,0:T(8,128)(2,1)S(1)}, u32[]{:S(2)}, u32[]{:S(2)}) collective-permute-start(bf16[128,512]{1,0:T(8,128)(2,1)} %refs_8_.4), channel_id=1, source_target_pairs={{0,1},{1,0},{2,3},{3,2},{4,5},{5,4},{6,7},{7,6},{8,9},{9,8},{10,11... | collective-permute-start | bytes 393224 | tf_op jit(solution)/shard_map/ppermute | solution.py:34
  5.5 13.6 %collective-permute-start.6 = (bf16[4,64,256]{2,1,0:T(8,128)(2,1)S(1)}, bf16[4,64,256]{2,1,0:T(8,128)(2,1)S(1)}, u32[]{:S(2)}, u32[]{:S(2)}) collective-permute-start(bf16[4,64,256]{2,1,0:T(8,128)(2,1)S(1)} %get-tuple-element.44), channel_id=1, source_target_pairs={{0,28},{4,24},{8,20},{12,16},{16,12},{20,8},{24,4},{28,0},{1,29},{... | collective-permute-start | bytes 393224 | tf_op jit(solution)/shard_map/ppermute | solution.py:34
  9.6 9.6 %collective-permute-start = (bf16[4,64,256]{2,1,0:T(8,128)(2,1)S(1)}, bf16[4,64,256]{2,1,0:T(8,128)(2,1)S(1)}, u32[]{:S(2)}, u32[]{:S(2)}) collective-permute-start(bf16[4,64,256]{2,1,0:T(8,128)(2,1)S(1)} %get-tuple-element.38), channel_id=1, source_target_pairs={{0,4},{4,0},{8,12},{12,8},{16,20},{20,16},{24,28},{28,24},{1,5},{5... | collective-permute-start | bytes 393224 | tf_op jit(solution)/shard_map/ppermute | solution.py:34
  9.7 10.5 %collective-permute-start.1 = (bf16[4,64,256]{2,1,0:T(8,128)(2,1)S(1)}, bf16[4,64,256]{2,1,0:T(8,128)(2,1)S(1)}, u32[]{:S(2)}, u32[]{:S(2)}) collective-permute-start(bf16[4,64,256]{2,1,0:T(8,128)(2,1)S(1)} %get-tuple-element.39), channel_id=1, source_target_pairs={{0,8},{4,12},{8,0},{12,4},{16,24},{20,28},{24,16},{28,20},{1,9},{5... | collective-permute-start | bytes 393224 | tf_op jit(solution)/shard_map/ppermute | solution.py:34
  11.8 11.9 %collective-permute-start.2 = (bf16[4,64,256]{2,1,0:T(8,128)(2,1)S(1)}, bf16[4,64,256]{2,1,0:T(8,128)(2,1)S(1)}, u32[]{:S(2)}, u32[]{:S(2)}) collective-permute-start(bf16[4,64,256]{2,1,0:T(8,128)(2,1)S(1)} %get-tuple-element.40), channel_id=1, source_target_pairs={{0,12},{4,8},{8,4},{12,0},{16,28},{20,24},{24,20},{28,16},{1,13},{... | collective-permute-start | bytes 393224 | tf_op jit(solution)/shard_map/ppermute | solution.py:34
  12.1 11.7 %collective-permute-start.3 = (bf16[4,64,256]{2,1,0:T(8,128)(2,1)S(1)}, bf16[4,64,256]{2,1,0:T(8,128)(2,1)S(1)}, u32[]{:S(2)}, u32[]{:S(2)}) collective-permute-start(bf16[4,64,256]{2,1,0:T(8,128)(2,1)S(1)} %get-tuple-element.41), channel_id=1, source_target_pairs={{0,16},{4,20},{8,24},{12,28},{16,0},{20,4},{24,8},{28,12},{1,17},{... | collective-permute-start | bytes 393224 | tf_op jit(solution)/shard_map/ppermute | solution.py:34
  19.2 11.8 %collective-permute-start.11 = (bf16[4,64,256]{2,1,0:T(8,128)(2,1)S(1)}, bf16[4,64,256]{2,1,0:T(8,128)(2,1)S(1)}, u32[]{:S(2)}, u32[]{:S(2)}) collective-permute-start(bf16[4,64,256]{2,1,0:T(8,128)(2,1)S(1)} %get-tuple-element.47), channel_id=1, source_target_pairs={{0,4},{4,0},{8,12},{12,8},{16,20},{20,16},{24,28},{28,24},{1,5},{5... | collective-permute-start | bytes 393224 | tf_op jit(solution)/shard_map/ppermute | solution.py:34
  20.1 11.9 %collective-permute-start.12 = (bf16[4,64,256]{2,1,0:T(8,128)(2,1)S(1)}, bf16[4,64,256]{2,1,0:T(8,128)(2,1)S(1)}, u32[]{:S(2)}, u32[]{:S(2)}) collective-permute-start(bf16[4,64,256]{2,1,0:T(8,128)(2,1)S(1)} %get-tuple-element.48), channel_id=1, source_target_pairs={{0,8},{4,12},{8,0},{12,4},{16,24},{20,28},{24,16},{28,20},{1,9},{5... | collective-permute-start | bytes 393224 | tf_op jit(solution)/shard_map/ppermute | solution.py:34
  23.7 16.5 %collective-permute-start.13 = (bf16[4,64,256]{2,1,0:T(8,128)(2,1)S(1)}, bf16[4,64,256]{2,1,0:T(8,128)(2,1)S(1)}, u32[]{:S(2)}, u32[]{:S(2)}) collective-permute-start(bf16[4,64,256]{2,1,0:T(8,128)(2,1)S(1)} %get-tuple-element.49), channel_id=1, source_target_pairs={{0,12},{4,8},{8,4},{12,0},{16,28},{20,24},{24,20},{28,16},{1,13},{... | collective-permute-start | bytes 393224 | tf_op jit(solution)/shard_map/ppermute | solution.py:34
  23.7 18.1 %collective-permute-start.14 = (bf16[4,64,256]{2,1,0:T(8,128)(2,1)S(1)}, bf16[4,64,256]{2,1,0:T(8,128)(2,1)S(1)}, u32[]{:S(2)}, u32[]{:S(2)}) collective-permute-start(bf16[4,64,256]{2,1,0:T(8,128)(2,1)S(1)} %get-tuple-element.50), channel_id=1, source_target_pairs={{0,16},{4,20},{8,24},{12,28},{16,0},{20,4},{24,8},{28,12},{1,17},{... | collective-permute-start | bytes 393224 | tf_op jit(solution)/shard_map/ppermute | solution.py:34
  27.5 21.0 %collective-permute-start.15 = (bf16[4,64,256]{2,1,0:T(8,128)(2,1)S(1)}, bf16[4,64,256]{2,1,0:T(8,128)(2,1)S(1)}, u32[]{:S(2)}, u32[]{:S(2)}) collective-permute-start(bf16[4,64,256]{2,1,0:T(8,128)(2,1)S(1)} %get-tuple-element.51), channel_id=1, source_target_pairs={{0,20},{4,16},{8,28},{12,24},{16,4},{20,0},{24,12},{28,8},{1,21},{... | collective-permute-start | bytes 393224 | tf_op jit(solution)/shard_map/ppermute | solution.py:34
  31.0 22.1 %collective-permute-start.16 = (bf16[4,64,256]{2,1,0:T(8,128)(2,1)S(1)}, bf16[4,64,256]{2,1,0:T(8,128)(2,1)S(1)}, u32[]{:S(2)}, u32[]{:S(2)}) collective-permute-start(bf16[4,64,256]{2,1,0:T(8,128)(2,1)S(1)} %get-tuple-element.52), channel_id=1, source_target_pairs={{0,24},{4,28},{8,16},{12,20},{16,8},{20,12},{24,0},{28,4},{1,25},{... | collective-permute-start | bytes 393224 | tf_op jit(solution)/shard_map/ppermute | solution.py:34
  32.0 27.7 %collective-permute-start.17 = (bf16[4,64,256]{2,1,0:T(8,128)(2,1)S(1)}, bf16[4,64,256]{2,1,0:T(8,128)(2,1)S(1)}, u32[]{:S(2)}, u32[]{:S(2)}) collective-permute-start(bf16[4,64,256]{2,1,0:T(8,128)(2,1)S(1)} %get-tuple-element.53), channel_id=1, source_target_pairs={{0,28},{4,24},{8,20},{12,16},{16,12},{20,8},{24,4},{28,0},{1,29},{... | collective-permute-start | bytes 393224 | tf_op jit(solution)/shard_map/ppermute | solution.py:34
  40.2 23.9 %collective-permute-start.21 = (bf16[4,64,256]{2,1,0:T(8,128)(2,1)S(1)}, bf16[4,64,256]{2,1,0:T(8,128)(2,1)S(1)}, u32[]{:S(2)}, u32[]{:S(2)}) collective-permute-start(bf16[4,64,256]{2,1,0:T(8,128)(2,1)S(1)} %get-tuple-element.57), channel_id=1, source_target_pairs={{20,0},{16,4},{28,8},{24,12},{4,16},{0,20},{12,24},{8,28},{21,1},{... | collective-permute-start | bytes 393224 | tf_op jit(solution)/shard_map/ppermute | solution.py:34
  41.8 23.4 %collective-permute-start.23 = (bf16[4,64,256]{2,1,0:T(8,128)(2,1)S(1)}, bf16[4,64,256]{2,1,0:T(8,128)(2,1)S(1)}, u32[]{:S(2)}, u32[]{:S(2)}) collective-permute-start(bf16[4,64,256]{2,1,0:T(8,128)(2,1)S(1)} %get-tuple-element.59), channel_id=1, source_target_pairs={{16,0},{20,4},{24,8},{28,12},{0,16},{4,20},{8,24},{12,28},{17,1},{... | collective-permute-start | bytes 393224 | tf_op jit(solution)/shard_map/ppermute | solution.py:34
  48.6 18.4 %collective-permute-start.25 = (bf16[4,64,256]{2,1,0:T(8,128)(2,1)S(1)}, bf16[4,64,256]{2,1,0:T(8,128)(2,1)S(1)}, u32[]{:S(2)}, u32[]{:S(2)}) collective-permute-start(bf16[4,64,256]{2,1,0:T(8,128)(2,1)S(1)} %get-tuple-element.63), channel_id=1, source_target_pairs={{4,0},{0,4},{12,8},{8,12},{20,16},{16,20},{28,24},{24,28},{5,1},{1... | collective-permute-start | bytes 393224 | tf_op jit(solution)/shard_map/ppermute | solution.py:34
  53.1 13.9 %collective-permute-start.27 = (bf16[4,64,256]{2,1,0:T(8,128)(2,1)S(1)}, bf16[4,64,256]{2,1,0:T(8,128)(2,1)S(1)}, u32[]{:S(2)}, u32[]{:S(2)}) collective-permute-start(bf16[4,64,256]{2,1,0:T(8,128)(2,1)S(1)} %get-tuple-element.65), channel_id=1, source_target_pairs={{8,0},{12,4},{0,8},{4,12},{24,16},{28,20},{16,24},{20,28},{9,1},{1... | collective-permute-start | bytes 393224 | tf_op jit(solution)/shard_map/ppermute | solution.py:34
  67.0 11.2 %collective-permute-start.30 = (bf16[4,64,256]{2,1,0:T(8,128)(2,1)S(1)}, bf16[4,64,256]{2,1,0:T(8,128)(2,1)S(1)}, u32[]{:S(2)}, u32[]{:S(2)}) collective-permute-start(bf16[4,64,256]{2,1,0:T(8,128)(2,1)S(1)} %get-tuple-element.68), channel_id=1, source_target_pairs={{12,0},{8,4},{4,8},{0,12},{28,16},{24,20},{20,24},{16,28},{13,1},{... | collective-permute-start | bytes 393224 | tf_op jit(solution)/shard_map/ppermute | solution.py:34
  68.7 13.0 %collective-permute-start.22 = (bf16[4,64,256]{2,1,0:T(8,128)(2,1)S(1)}, bf16[4,64,256]{2,1,0:T(8,128)(2,1)S(1)}, u32[]{:S(2)}, u32[]{:S(2)}) collective-permute-start(bf16[4,64,256]{2,1,0:T(8,128)(2,1)S(1)} %get-tuple-element.58), channel_id=1, source_target_pairs={{20,0},{16,4},{28,8},{24,12},{4,16},{0,20},{12,24},{8,28},{21,1},{... | collective-permute-start | bytes 393224 | tf_op jit(solution)/shard_map/ppermute | solution.py:34
  70.5 20.2 %collective-permute-start.19 = (bf16[4,64,256]{2,1,0:T(8,128)(2,1)S(1)}, bf16[4,64,256]{2,1,0:T(8,128)(2,1)S(1)}, u32[]{:S(2)}, u32[]{:S(2)}) collective-permute-start(bf16[4,64,256]{2,1,0:T(8,128)(2,1)S(1)} %get-tuple-element.55), channel_id=1, source_target_pairs={{24,0},{28,4},{16,8},{20,12},{8,16},{12,20},{0,24},{4,28},{25,1},{... | collective-permute-start | bytes 393224 | tf_op jit(solution)/shard_map/ppermute | solution.py:34
  71.7 21.8 %collective-permute-start.20 = (bf16[4,64,256]{2,1,0:T(8,128)(2,1)S(1)}, bf16[4,64,256]{2,1,0:T(8,128)(2,1)S(1)}, u32[]{:S(2)}, u32[]{:S(2)}) collective-permute-start(bf16[4,64,256]{2,1,0:T(8,128)(2,1)S(1)} %get-tuple-element.56), channel_id=1, source_target_pairs={{24,0},{28,4},{16,8},{20,12},{8,16},{12,20},{0,24},{4,28},{25,1},{... | collective-permute-start | bytes 393224 | tf_op jit(solution)/shard_map/ppermute | solution.py:34
  74.7 24.1 %collective-permute-start.10 = (bf16[4,64,256]{2,1,0:T(8,128)(2,1)S(1)}, bf16[4,64,256]{2,1,0:T(8,128)(2,1)S(1)}, u32[]{:S(2)}, u32[]{:S(2)}) collective-permute-start(bf16[4,64,256]{2,1,0:T(8,128)(2,1)S(1)} %get-tuple-element.45), channel_id=1, source_target_pairs={{28,0},{24,4},{20,8},{16,12},{12,16},{8,20},{4,24},{0,28},{29,1},{... | collective-permute-start | bytes 393224 | tf_op jit(solution)/shard_map/ppermute | solution.py:34
  78.1 22.7 %collective-permute-start.18 = (bf16[4,64,256]{2,1,0:T(8,128)(2,1)S(1)}, bf16[4,64,256]{2,1,0:T(8,128)(2,1)S(1)}, u32[]{:S(2)}, u32[]{:S(2)}) collective-permute-start(bf16[4,64,256]{2,1,0:T(8,128)(2,1)S(1)} %get-tuple-element.54), channel_id=1, source_target_pairs={{28,0},{24,4},{20,8},{16,12},{12,16},{8,20},{4,24},{0,28},{29,1},{... | collective-permute-start | bytes 393224 | tf_op jit(solution)/shard_map/ppermute | solution.py:34
  (13 other events, 309.5 us)

commit v2 on v1

--- a/solution.py
+++ b/solution.py
@@ -22,6 +22,15 @@
     if count & (count - 1) == 0:
         return me ^ m
     return lax.rem(me + count - m, count)
+
+
+def sides(count):
+    half = count // 2
+    return sorted(range(half, count), key=lambda m: (-(m // 2), m)), list(range(1, half))
+
+
+def chunk_count(share):
+    return 2 if share % 2 == 0 else 1
 
 
 def send(value, m, axis, count, back=False):
@@ -106,9 +115,11 @@
     me = lax.axis_index("emb")
     block = row_block(rows)
     pick = pick_matrix(block * GROUP, GROUP * block, GROUP, block)
+    blocks = rows // block
     copies = []
     for k, m in enumerate(messages):
-        for b in range(rows // block):
+        start = pl.multiple_of(target(me, m, count) * GROUP, GROUP)
+        for b in range(blocks):
             here = slice(b * block, (b + 1) * block)
             gain, bias = gain_ref[here], bias_ref[here]
             done = [
@@ -118,9 +129,12 @@
             done = jnp.concatenate(done, axis=0).reshape(GROUP * block, width)
             moved = jnp.dot(pick, done, preferred_element_type=jnp.float32)
             ready[k, here] = moved.astype(jnp.bfloat16).reshape(block, GROUP, width)
-        start = pl.multiple_of(target(me, m, count) * GROUP, GROUP)
-        copies.append(pltpu.make_async_copy(ready.at[k], out_ref.at[:, pl.ds(start, GROUP), :], sems.at[k]))
-        copies[-1].start()
+            copies.append(
+                pltpu.make_async_copy(
+                    ready.at[k, here], out_ref.at[here, pl.ds(start, GROUP), :], sems.at[k * blocks + b]
+                )
+            )
+            copies[-1].start()
     for copy in copies:
         copy.wait()
 
@@ -139,7 +153,7 @@
         input_output_aliases={} if first else {len(operands) - 1: 0},
         scratch_shapes=[
             pltpu.VMEM((len(messages), rows, GROUP, width), jnp.bfloat16),
-            pltpu.SemaphoreType.DMA((len(messages),)),
+            pltpu.SemaphoreType.DMA((len(messages) * (rows // row_block(rows)),)),
         ],
         compiler_params=pltpu.CompilerParams(vmem_limit_bytes=12 * 1024 * 1024),
         cost_estimate=pl.CostEstimate(flops=10**8, bytes_accessed=10**6, transcendentals=0),
@@ -213,10 +227,9 @@
     count = lax.axis_size("emb")
     others = lax.axis_size("dp")
     share = samples // count
-    chunks = 2 if share % 2 == 0 else 1
+    chunks = chunk_count(share)
     part = share // chunks
-    far = [m for m in range(count - 1, 0, -1) if m >= count // 2]
-    near = [m for m in range(1, count) if m < count // 2]
+    far, near = sides(count)
     fast = share == GROUP
     sends = {}
 
@@ -257,7 +270,7 @@
 
     if fast:
         out = None
-        for messages in [[0] + near] + [[m] for m in far[::-1]]:
+        for messages in [[0] + near] + [[m] for m in sorted(far)]:
             pieces = [returned[m, c] for m in messages for c in range(chunks)]
             out = merge(out, pieces, ln_gain, ln_bias, messages, chunks, count, samples)
         return out

time: 102 us -> 102 us (level)
  the two profiles are of different devices: /device:TPU:15 before, /device:TPU:13 now
where the time goes in v2:
time: 102 us
  starting transfers between devices  42.5 us (42%)
  waiting for transfers between devices  41.4 us (41%)
  Pallas kernels  17.7 us (17%)
    ppermute x31, starting transfers between devices, send(): return lax.ppermute(value, axis, pairs)  42.5 us
    ppermute x31, waiting for transfers between devices, send(): return lax.ppermute(value, axis, pairs)  41.4 us
    pallas_call x2, Pallas kernels, layer(): pl.pallas_call(functools.partial(layer_kernel, count, len(weights)), out_...  8.87 us
    pallas_call x5, Pallas kernels, merge(): pl.pallas_call(functools.partial(merge_kernel, messages, chunks, count, f...  5.27 us
    pallas_call x2, Pallas kernels, split(): pl.pallas_call(functools.partial(split_kernel, messages, chunks, count),...  3.57 us
  transfers between devices with their start and end apart: 31, of which 12 were waited for; matrix products, arithmetic and copies ran while one was open for 0% of the time, Pallas kernels for 16%

profile of v2, /device:TPU:13, one launch (start us, length us, event | category | flops | bytes accessed | tf_op | source)
XLA Modules:
  0.0 101.8 jit_solution(6780492949073397881)
XLA Ops:
  5.5 1.9 %collective-permute-start.6 = (bf16[4,64,256]{2,1,0:T(8,128)(2,1)S(1)}, bf16[4,64,256]{2,1,0:T(8,128)(2,1)S(1)}, u32[]{:S(2)}, u32[]{:S(2)}) collective-permute-start(bf16[4,64,256]{2,1,0:T(8,128)(2,1)S(1)} %get-tuple-element.44), channel_id=1, source_target_pairs={{0,28},{4,24},{8,20},{12,16},{16,12},{20,8},{24,4},{28,0},{1,29},{... | collective-permute-start | bytes 393224 | tf_op jit(solution)/shard_map/ppermute | solution.py:43
  7.3 2.2 %split.2 = (bf16[4,64,256]{2,1,0:T(8,128)(2,1)S(1)}, bf16[4,64,256]{2,1,0:T(8,128)(2,1)S(1)}, bf16[4,64,256]{2,1,0:T(8,128)(2,1)S(1)}, bf16[4,64,256]{2,1,0:T(8,...) custom-call(bf16[64,64,256]{2,1,0:T(8,128)(2,1)S(1)} %copy-done), custom_call_target="tpu_custom_call" | custom-call | flops 100000000 | bytes 1000000 | tf_op jit(solution)/shard_map/split/pallas_call | solution.py:94
  9.7 2.1 %collective-permute-start.1 = (bf16[4,64,256]{2,1,0:T(8,128)(2,1)S(1)}, bf16[4,64,256]{2,1,0:T(8,128)(2,1)S(1)}, u32[]{:S(2)}, u32[]{:S(2)}) collective-permute-start(bf16[4,64,256]{2,1,0:T(8,128)(2,1)S(1)} %get-tuple-element.39), channel_id=1, source_target_pairs={{0,8},{4,12},{8,0},{12,4},{16,24},{20,28},{24,16},{28,20},{1,9},{5... | collective-permute-start | bytes 393224 | tf_op jit(solution)/shard_map/ppermute | solution.py:43
  12.1 3.8 %collective-permute-start.3 = (bf16[4,64,256]{2,1,0:T(8,128)(2,1)S(1)}, bf16[4,64,256]{2,1,0:T(8,128)(2,1)S(1)}, u32[]{:S(2)}, u32[]{:S(2)}) collective-permute-start(bf16[4,64,256]{2,1,0:T(8,128)(2,1)S(1)} %get-tuple-element.41), channel_id=1, source_target_pairs={{0,16},{4,20},{8,24},{12,28},{16,0},{20,4},{24,8},{28,12},{1,17},{... | collective-permute-start | bytes 393224 | tf_op jit(solution)/shard_map/ppermute | solution.py:43
  15.9 3.2 %collective-permute-done.6.refs_7_ = bf16[4,64,256]{2,1,0:T(8,128)(2,1)S(1)} collective-permute-done((bf16[4,64,256]{2,1,0:T(8,128)(2,1)S(1)}, bf16[4,64,256]{2,1,0:T(8,128)(2,1)S(1)}, u32[]{:S(2)}, u32[]{:S(2)}) %collective-permute-start.6) | collective-permute-done | bytes 131104 | tf_op jit(solution)/shard_map/ppermute | solution.py:43
  20.1 3.6 %collective-permute-start.12 = (bf16[4,64,256]{2,1,0:T(8,128)(2,1)S(1)}, bf16[4,64,256]{2,1,0:T(8,128)(2,1)S(1)}, u32[]{:S(2)}, u32[]{:S(2)}) collective-permute-start(bf16[4,64,256]{2,1,0:T(8,128)(2,1)S(1)} %get-tuple-element.48), channel_id=1, source_target_pairs={{0,8},{4,12},{8,0},{12,4},{16,24},{20,28},{24,16},{28,20},{1,9},{5... | collective-permute-start | bytes 393224 | tf_op jit(solution)/shard_map/ppermute | solution.py:43
  24.9 2.6 %collective-permute-done.4.refs_5_ = bf16[4,64,256]{2,1,0:T(8,128)(2,1)S(1)} collective-permute-done((bf16[4,64,256]{2,1,0:T(8,128)(2,1)S(1)}, bf16[4,64,256]{2,1,0:T(8,128)(2,1)S(1)}, u32[]{:S(2)}, u32[]{:S(2)}) %collective-permute-start.4) | collective-permute-done | bytes 131104 | tf_op jit(solution)/shard_map/ppermute | solution.py:43
  27.5 3.5 %collective-permute-start.15 = (bf16[4,64,256]{2,1,0:T(8,128)(2,1)S(1)}, bf16[4,64,256]{2,1,0:T(8,128)(2,1)S(1)}, u32[]{:S(2)}, u32[]{:S(2)}) collective-permute-start(bf16[4,64,256]{2,1,0:T(8,128)(2,1)S(1)} %get-tuple-element.51), channel_id=1, source_target_pairs={{0,20},{4,16},{8,28},{12,24},{16,4},{20,0},{24,12},{28,8},{1,21},{... | collective-permute-start | bytes 393224 | tf_op jit(solution)/shard_map/ppermute | solution.py:43
  32.0 3.8 %collective-permute-start.17 = (bf16[4,64,256]{2,1,0:T(8,128)(2,1)S(1)}, bf16[4,64,256]{2,1,0:T(8,128)(2,1)S(1)}, u32[]{:S(2)}, u32[]{:S(2)}) collective-permute-start(bf16[4,64,256]{2,1,0:T(8,128)(2,1)S(1)} %get-tuple-element.53), channel_id=1, source_target_pairs={{0,28},{4,24},{8,20},{12,16},{16,12},{20,8},{24,4},{28,0},{1,29},{... | collective-permute-start | bytes 393224 | tf_op jit(solution)/shard_map/ppermute | solution.py:43
  35.8 4.4 %layer.2 = (bf16[4,64,256]{2,1,0:T(8,128)(2,1)S(1)}, bf16[4,64,256]{2,1,0:T(8,128)(2,1)S(1)}, bf16[4,64,256]{2,1,0:T(8,128)(2,1)S(1)}, bf16[4,64,256]{2,1,0:T(8,...) custom-call(bf16[4,64,256]{2,1,0:T(8,128)(2,1)S(1)} %get-tuple-eleme, ...), custom_call_target="tpu_custom_call" | custom-call | flops 536870912 | bytes 2097152 | tf_op jit(solution)/shard_map/layer/pallas_call | solution.py:207
  40.2 1.6 %collective-permute-start.21 = (bf16[4,64,256]{2,1,0:T(8,128)(2,1)S(1)}, bf16[4,64,256]{2,1,0:T(8,128)(2,1)S(1)}, u32[]{:S(2)}, u32[]{:S(2)}) collective-permute-start(bf16[4,64,256]{2,1,0:T(8,128)(2,1)S(1)} %get-tuple-element.57), channel_id=1, source_target_pairs={{20,0},{16,4},{28,8},{24,12},{4,16},{0,20},{12,24},{8,28},{21,1},{... | collective-permute-start | bytes 393224 | tf_op jit(solution)/shard_map/ppermute | solution.py:43
  41.8 6.7 %collective-permute-done.15.refs_5_ = bf16[4,64,256]{2,1,0:T(8,128)(2,1)S(1)} collective-permute-done((bf16[4,64,256]{2,1,0:T(8,128)(2,1)S(1)}, bf16[4,64,256]{2,1,0:T(8,128)(2,1)S(1)}, u32[]{:S(2)}, u32[]{:S(2)}) %collective-permute-start.15) | collective-permute-done | bytes 131104 | tf_op jit(solution)/shard_map/ppermute | solution.py:43
  48.6 4.1 %collective-permute-start.25 = (bf16[4,64,256]{2,1,0:T(8,128)(2,1)S(1)}, bf16[4,64,256]{2,1,0:T(8,128)(2,1)S(1)}, u32[]{:S(2)}, u32[]{:S(2)}) collective-permute-start(bf16[4,64,256]{2,1,0:T(8,128)(2,1)S(1)} %get-tuple-element.63), channel_id=1, source_target_pairs={{4,0},{0,4},{12,8},{8,12},{20,16},{16,20},{28,24},{24,28},{5,1},{1... | collective-permute-start | bytes 393224 | tf_op jit(solution)/shard_map/ppermute | solution.py:43
  53.9 5.8 %collective-permute-done.17.refs_7_ = bf16[4,64,256]{2,1,0:T(8,128)(2,1)S(1)} collective-permute-done((bf16[4,64,256]{2,1,0:T(8,128)(2,1)S(1)}, bf16[4,64,256]{2,1,0:T(8,128)(2,1)S(1)}, u32[]{:S(2)}, u32[]{:S(2)}) %collective-permute-start.17) | collective-permute-done | bytes 131104 | tf_op jit(solution)/shard_map/ppermute | solution.py:43
  59.7 4.4 %layer.3 = (bf16[4,64,256]{2,1,0:T(8,128)(2,1)S(1)}, bf16[4,64,256]{2,1,0:T(8,128)(2,1)S(1)}, bf16[4,64,256]{2,1,0:T(8,128)(2,1)S(1)}, bf16[4,64,256]{2,1,0:T(8,...) custom-call(bf16[4,64,256]{2,1,0:T(8,128)(2,1)S(1)} %get-tuple-eleme, ...), custom_call_target="tpu_custom_call" | custom-call | flops 536870912 | bytes 2097152 | tf_op jit(solution)/shard_map/layer/pallas_call | solution.py:207
  65.3 1.7 %collective-permute-start.26 = (bf16[4,64,256]{2,1,0:T(8,128)(2,1)S(1)}, bf16[4,64,256]{2,1,0:T(8,128)(2,1)S(1)}, u32[]{:S(2)}, u32[]{:S(2)}) collective-permute-start(bf16[4,64,256]{2,1,0:T(8,128)(2,1)S(1)} %get-tuple-element.64), channel_id=1, source_target_pairs={{4,0},{0,4},{12,8},{8,12},{20,16},{16,20},{28,24},{24,28},{5,1},{1... | collective-permute-start | bytes 393224 | tf_op jit(solution)/shard_map/ppermute | solution.py:43
  67.0 1.7 %collective-permute-start.30 = (bf16[4,64,256]{2,1,0:T(8,128)(2,1)S(1)}, bf16[4,64,256]{2,1,0:T(8,128)(2,1)S(1)}, u32[]{:S(2)}, u32[]{:S(2)}) collective-permute-start(bf16[4,64,256]{2,1,0:T(8,128)(2,1)S(1)} %get-tuple-element.68), channel_id=1, source_target_pairs={{12,0},{8,4},{4,8},{0,12},{28,16},{24,20},{20,24},{16,28},{13,1},{... | collective-permute-start | bytes 393224 | tf_op jit(solution)/shard_map/ppermute | solution.py:43
  69.1 1.4 %collective-permute-done.24.refs_1_ = bf16[4,64,256]{2,1,0:T(8,128)(2,1)S(1)} collective-permute-done((bf16[4,64,256]{2,1,0:T(8,128)(2,1)S(1)}, bf16[4,64,256]{2,1,0:T(8,128)(2,1)S(1)}, u32[]{:S(2)}, u32[]{:S(2)}) %collective-permute-start.24) | collective-permute-done | bytes 131104 | tf_op jit(solution)/shard_map/ppermute | solution.py:43
  72.0 2.7 %collective-permute-done.28.refs_5_ = bf16[4,64,256]{2,1,0:T(8,128)(2,1)S(1)} collective-permute-done((bf16[4,64,256]{2,1,0:T(8,128)(2,1)S(1)}, bf16[4,64,256]{2,1,0:T(8,128)(2,1)S(1)}, u32[]{:S(2)}, u32[]{:S(2)}) %collective-permute-start.28) | collective-permute-done | bytes 131104 | tf_op jit(solution)/shard_map/ppermute | solution.py:43
  74.7 2.2 %collective-permute-start.10 = (bf16[4,64,256]{2,1,0:T(8,128)(2,1)S(1)}, bf16[4,64,256]{2,1,0:T(8,128)(2,1)S(1)}, u32[]{:S(2)}, u32[]{:S(2)}) collective-permute-start(bf16[4,64,256]{2,1,0:T(8,128)(2,1)S(1)} %get-tuple-element.45), channel_id=1, source_target_pairs={{28,0},{24,4},{20,8},{16,12},{12,16},{8,20},{4,24},{0,28},{29,1},{... | collective-permute-start | bytes 393224 | tf_op jit(solution)/shard_map/ppermute | solution.py:43
  82.6 8.0 %collective-permute-done.19.refs_0_ = bf16[4,64,256]{2,1,0:T(8,128)(2,1)S(1)} collective-permute-done((bf16[4,64,256]{2,1,0:T(8,128)(2,1)S(1)}, bf16[4,64,256]{2,1,0:T(8,128)(2,1)S(1)}, u32[]{:S(2)}, u32[]{:S(2)}) %collective-permute-start.19) | collective-permute-done | bytes 131104 | tf_op jit(solution)/shard_map/ppermute | solution.py:43
  90.7 2.8 %collective-permute-done.20.refs_1_ = bf16[4,64,256]{2,1,0:T(8,128)(2,1)S(1)} collective-permute-done((bf16[4,64,256]{2,1,0:T(8,128)(2,1)S(1)}, bf16[4,64,256]{2,1,0:T(8,128)(2,1)S(1)}, u32[]{:S(2)}, u32[]{:S(2)}) %collective-permute-start.20) | collective-permute-done | bytes 131104 | tf_op jit(solution)/shard_map/ppermute | solution.py:43
  94.5 4.4 %collective-permute-done.10.refs_0_ = bf16[4,64,256]{2,1,0:T(8,128)(2,1)S(1)} collective-permute-done((bf16[4,64,256]{2,1,0:T(8,128)(2,1)S(1)}, bf16[4,64,256]{2,1,0:T(8,128)(2,1)S(1)}, u32[]{:S(2)}, u32[]{:S(2)}) %collective-permute-start.10) | collective-permute-done | bytes 131104 | tf_op jit(solution)/shard_map/ppermute | solution.py:43
  98.9 1.9 %collective-permute-done.18.refs_1_ = bf16[4,64,256]{2,1,0:T(8,128)(2,1)S(1)} collective-permute-done((bf16[4,64,256]{2,1,0:T(8,128)(2,1)S(1)}, bf16[4,64,256]{2,1,0:T(8,128)(2,1)S(1)}, u32[]{:S(2)}, u32[]{:S(2)}) %collective-permute-start.18) | collective-permute-done | bytes 131104 | tf_op jit(solution)/shard_map/ppermute | solution.py:43
  (59 shorter events, 21.0 us)
Async XLA Ops:
  0.0 9.5 %collective-permute-start.9 = (bf16[128,512]{1,0:T(8,128)(2,1)}, bf16[128,512]{1,0:T(8,128)(2,1)S(1)}, u32[]{:S(2)}, u32[]{:S(2)}) collective-permute-start(bf16[128,512]{1,0:T(8,128)(2,1)} %refs_8_.4), channel_id=1, source_target_pairs={{0,3},{1,2},{2,1},{3,0},{4,7},{5,6},{6,5},{7,4},{8,11},{9,10},{10,... | collective-permute-start | bytes 393224 | tf_op jit(solution)/shard_map/ppermute | solution.py:43
  2.5 9.3 %collective-permute-start.7 = (bf16[128,512]{1,0:T(8,128)(2,1)}, bf16[128,512]{1,0:T(8,128)(2,1)S(1)}, u32[]{:S(2)}, u32[]{:S(2)}) collective-permute-start(bf16[128,512]{1,0:T(8,128)(2,1)} %refs_8_.4), channel_id=1, source_target_pairs={{0,1},{1,0},{2,3},{3,2},{4,5},{5,4},{6,7},{7,6},{8,9},{9,8},{10,11... | collective-permute-start | bytes 393224 | tf_op jit(solution)/shard_map/ppermute | solution.py:43
  5.5 13.6 %collective-permute-start.6 = (bf16[4,64,256]{2,1,0:T(8,128)(2,1)S(1)}, bf16[4,64,256]{2,1,0:T(8,128)(2,1)S(1)}, u32[]{:S(2)}, u32[]{:S(2)}) collective-permute-start(bf16[4,64,256]{2,1,0:T(8,128)(2,1)S(1)} %get-tuple-element.44), channel_id=1, source_target_pairs={{0,28},{4,24},{8,20},{12,16},{16,12},{20,8},{24,4},{28,0},{1,29},{... | collective-permute-start | bytes 393224 | tf_op jit(solution)/shard_map/ppermute | solution.py:43
  9.6 9.6 %collective-permute-start = (bf16[4,64,256]{2,1,0:T(8,128)(2,1)S(1)}, bf16[4,64,256]{2,1,0:T(8,128)(2,1)S(1)}, u32[]{:S(2)}, u32[]{:S(2)}) collective-permute-start(bf16[4,64,256]{2,1,0:T(8,128)(2,1)S(1)} %get-tuple-element.38), channel_id=1, source_target_pairs={{0,4},{4,0},{8,12},{12,8},{16,20},{20,16},{24,28},{28,24},{1,5},{5... | collective-permute-start | bytes 393224 | tf_op jit(solution)/shard_map/ppermute | solution.py:43
  9.7 10.4 %collective-permute-start.1 = (bf16[4,64,256]{2,1,0:T(8,128)(2,1)S(1)}, bf16[4,64,256]{2,1,0:T(8,128)(2,1)S(1)}, u32[]{:S(2)}, u32[]{:S(2)}) collective-permute-start(bf16[4,64,256]{2,1,0:T(8,128)(2,1)S(1)} %get-tuple-element.39), channel_id=1, source_target_pairs={{0,8},{4,12},{8,0},{12,4},{16,24},{20,28},{24,16},{28,20},{1,9},{5... | collective-permute-start | bytes 393224 | tf_op jit(solution)/shard_map/ppermute | solution.py:43
  11.8 11.9 %collective-permute-start.2 = (bf16[4,64,256]{2,1,0:T(8,128)(2,1)S(1)}, bf16[4,64,256]{2,1,0:T(8,128)(2,1)S(1)}, u32[]{:S(2)}, u32[]{:S(2)}) collective-permute-start(bf16[4,64,256]{2,1,0:T(8,128)(2,1)S(1)} %get-tuple-element.40), channel_id=1, source_target_pairs={{0,12},{4,8},{8,4},{12,0},{16,28},{20,24},{24,20},{28,16},{1,13},{... | collective-permute-start | bytes 393224 | tf_op jit(solution)/shard_map/ppermute | solution.py:43
  12.1 11.7 %collective-permute-start.3 = (bf16[4,64,256]{2,1,0:T(8,128)(2,1)S(1)}, bf16[4,64,256]{2,1,0:T(8,128)(2,1)S(1)}, u32[]{:S(2)}, u32[]{:S(2)}) collective-permute-start(bf16[4,64,256]{2,1,0:T(8,128)(2,1)S(1)} %get-tuple-element.41), channel_id=1, source_target_pairs={{0,16},{4,20},{8,24},{12,28},{16,0},{20,4},{24,8},{28,12},{1,17},{... | collective-permute-start | bytes 393224 | tf_op jit(solution)/shard_map/ppermute | solution.py:43
  19.2 11.8 %collective-permute-start.11 = (bf16[4,64,256]{2,1,0:T(8,128)(2,1)S(1)}, bf16[4,64,256]{2,1,0:T(8,128)(2,1)S(1)}, u32[]{:S(2)}, u32[]{:S(2)}) collective-permute-start(bf16[4,64,256]{2,1,0:T(8,128)(2,1)S(1)} %get-tuple-element.47), channel_id=1, source_target_pairs={{0,4},{4,0},{8,12},{12,8},{16,20},{20,16},{24,28},{28,24},{1,5},{5... | collective-permute-start | bytes 393224 | tf_op jit(solution)/shard_map/ppermute | solution.py:43
  20.1 11.9 %collective-permute-start.12 = (bf16[4,64,256]{2,1,0:T(8,128)(2,1)S(1)}, bf16[4,64,256]{2,1,0:T(8,128)(2,1)S(1)}, u32[]{:S(2)}, u32[]{:S(2)}) collective-permute-start(bf16[4,64,256]{2,1,0:T(8,128)(2,1)S(1)} %get-tuple-element.48), channel_id=1, source_target_pairs={{0,8},{4,12},{8,0},{12,4},{16,24},{20,28},{24,16},{28,20},{1,9},{5... | collective-permute-start | bytes 393224 | tf_op jit(solution)/shard_map/ppermute | solution.py:43
  23.7 16.5 %collective-permute-start.13 = (bf16[4,64,256]{2,1,0:T(8,128)(2,1)S(1)}, bf16[4,64,256]{2,1,0:T(8,128)(2,1)S(1)}, u32[]{:S(2)}, u32[]{:S(2)}) collective-permute-start(bf16[4,64,256]{2,1,0:T(8,128)(2,1)S(1)} %get-tuple-element.49), channel_id=1, source_target_pairs={{0,12},{4,8},{8,4},{12,0},{16,28},{20,24},{24,20},{28,16},{1,13},{... | collective-permute-start | bytes 393224 | tf_op jit(solution)/shard_map/ppermute | solution.py:43
  23.7 18.1 %collective-permute-start.14 = (bf16[4,64,256]{2,1,0:T(8,128)(2,1)S(1)}, bf16[4,64,256]{2,1,0:T(8,128)(2,1)S(1)}, u32[]{:S(2)}, u32[]{:S(2)}) collective-permute-start(bf16[4,64,256]{2,1,0:T(8,128)(2,1)S(1)} %get-tuple-element.50), channel_id=1, source_target_pairs={{0,16},{4,20},{8,24},{12,28},{16,0},{20,4},{24,8},{28,12},{1,17},{... | collective-permute-start | bytes 393224 | tf_op jit(solution)/shard_map/ppermute | solution.py:43
  27.5 21.0 %collective-permute-start.15 = (bf16[4,64,256]{2,1,0:T(8,128)(2,1)S(1)}, bf16[4,64,256]{2,1,0:T(8,128)(2,1)S(1)}, u32[]{:S(2)}, u32[]{:S(2)}) collective-permute-start(bf16[4,64,256]{2,1,0:T(8,128)(2,1)S(1)} %get-tuple-element.51), channel_id=1, source_target_pairs={{0,20},{4,16},{8,28},{12,24},{16,4},{20,0},{24,12},{28,8},{1,21},{... | collective-permute-start | bytes 393224 | tf_op jit(solution)/shard_map/ppermute | solution.py:43
  31.0 22.1 %collective-permute-start.16 = (bf16[4,64,256]{2,1,0:T(8,128)(2,1)S(1)}, bf16[4,64,256]{2,1,0:T(8,128)(2,1)S(1)}, u32[]{:S(2)}, u32[]{:S(2)}) collective-permute-start(bf16[4,64,256]{2,1,0:T(8,128)(2,1)S(1)} %get-tuple-element.52), channel_id=1, source_target_pairs={{0,24},{4,28},{8,16},{12,20},{16,8},{20,12},{24,0},{28,4},{1,25},{... | collective-permute-start | bytes 393224 | tf_op jit(solution)/shard_map/ppermute | solution.py:43
  32.0 27.7 %collective-permute-start.17 = (bf16[4,64,256]{2,1,0:T(8,128)(2,1)S(1)}, bf16[4,64,256]{2,1,0:T(8,128)(2,1)S(1)}, u32[]{:S(2)}, u32[]{:S(2)}) collective-permute-start(bf16[4,64,256]{2,1,0:T(8,128)(2,1)S(1)} %get-tuple-element.53), channel_id=1, source_target_pairs={{0,28},{4,24},{8,20},{12,16},{16,12},{20,8},{24,4},{28,0},{1,29},{... | collective-permute-start | bytes 393224 | tf_op jit(solution)/shard_map/ppermute | solution.py:43
  40.2 23.9 %collective-permute-start.21 = (bf16[4,64,256]{2,1,0:T(8,128)(2,1)S(1)}, bf16[4,64,256]{2,1,0:T(8,128)(2,1)S(1)}, u32[]{:S(2)}, u32[]{:S(2)}) collective-permute-start(bf16[4,64,256]{2,1,0:T(8,128)(2,1)S(1)} %get-tuple-element.57), channel_id=1, source_target_pairs={{20,0},{16,4},{28,8},{24,12},{4,16},{0,20},{12,24},{8,28},{21,1},{... | collective-permute-start | bytes 393224 | tf_op jit(solution)/shard_map/ppermute | solution.py:43
  41.8 23.4 %collective-permute-start.23 = (bf16[4,64,256]{2,1,0:T(8,128)(2,1)S(1)}, bf16[4,64,256]{2,1,0:T(8,128)(2,1)S(1)}, u32[]{:S(2)}, u32[]{:S(2)}) collective-permute-start(bf16[4,64,256]{2,1,0:T(8,128)(2,1)S(1)} %get-tuple-element.59), channel_id=1, source_target_pairs={{16,0},{20,4},{24,8},{28,12},{0,16},{4,20},{8,24},{12,28},{17,1},{... | collective-permute-start | bytes 393224 | tf_op jit(solution)/shard_map/ppermute | solution.py:43
  48.6 18.4 %collective-permute-start.25 = (bf16[4,64,256]{2,1,0:T(8,128)(2,1)S(1)}, bf16[4,64,256]{2,1,0:T(8,128)(2,1)S(1)}, u32[]{:S(2)}, u32[]{:S(2)}) collective-permute-start(bf16[4,64,256]{2,1,0:T(8,128)(2,1)S(1)} %get-tuple-element.63), channel_id=1, source_target_pairs={{4,0},{0,4},{12,8},{8,12},{20,16},{16,20},{28,24},{24,28},{5,1},{1... | collective-permute-start | bytes 393224 | tf_op jit(solution)/shard_map/ppermute | solution.py:43
  53.1 13.9 %collective-permute-start.27 = (bf16[4,64,256]{2,1,0:T(8,128)(2,1)S(1)}, bf16[4,64,256]{2,1,0:T(8,128)(2,1)S(1)}, u32[]{:S(2)}, u32[]{:S(2)}) collective-permute-start(bf16[4,64,256]{2,1,0:T(8,128)(2,1)S(1)} %get-tuple-element.65), channel_id=1, source_target_pairs={{8,0},{12,4},{0,8},{4,12},{24,16},{28,20},{16,24},{20,28},{9,1},{1... | collective-permute-start | bytes 393224 | tf_op jit(solution)/shard_map/ppermute | solution.py:43
  67.0 11.2 %collective-permute-start.30 = (bf16[4,64,256]{2,1,0:T(8,128)(2,1)S(1)}, bf16[4,64,256]{2,1,0:T(8,128)(2,1)S(1)}, u32[]{:S(2)}, u32[]{:S(2)}) collective-permute-start(bf16[4,64,256]{2,1,0:T(8,128)(2,1)S(1)} %get-tuple-element.68), channel_id=1, source_target_pairs={{12,0},{8,4},{4,8},{0,12},{28,16},{24,20},{20,24},{16,28},{13,1},{... | collective-permute-start | bytes 393224 | tf_op jit(solution)/shard_map/ppermute | solution.py:43
  68.7 13.0 %collective-permute-start.22 = (bf16[4,64,256]{2,1,0:T(8,128)(2,1)S(1)}, bf16[4,64,256]{2,1,0:T(8,128)(2,1)S(1)}, u32[]{:S(2)}, u32[]{:S(2)}) collective-permute-start(bf16[4,64,256]{2,1,0:T(8,128)(2,1)S(1)} %get-tuple-element.58), channel_id=1, source_target_pairs={{20,0},{16,4},{28,8},{24,12},{4,16},{0,20},{12,24},{8,28},{21,1},{... | collective-permute-start | bytes 393224 | tf_op jit(solution)/shard_map/ppermute | solution.py:43
  70.5 20.2 %collective-permute-start.19 = (bf16[4,64,256]{2,1,0:T(8,128)(2,1)S(1)}, bf16[4,64,256]{2,1,0:T(8,128)(2,1)S(1)}, u32[]{:S(2)}, u32[]{:S(2)}) collective-permute-start(bf16[4,64,256]{2,1,0:T(8,128)(2,1)S(1)} %get-tuple-element.55), channel_id=1, source_target_pairs={{24,0},{28,4},{16,8},{20,12},{8,16},{12,20},{0,24},{4,28},{25,1},{... | collective-permute-start | bytes 393224 | tf_op jit(solution)/shard_map/ppermute | solution.py:43
  71.7 21.8 %collective-permute-start.20 = (bf16[4,64,256]{2,1,0:T(8,128)(2,1)S(1)}, bf16[4,64,256]{2,1,0:T(8,128)(2,1)S(1)}, u32[]{:S(2)}, u32[]{:S(2)}) collective-permute-start(bf16[4,64,256]{2,1,0:T(8,128)(2,1)S(1)} %get-tuple-element.56), channel_id=1, source_target_pairs={{24,0},{28,4},{16,8},{20,12},{8,16},{12,20},{0,24},{4,28},{25,1},{... | collective-permute-start | bytes 393224 | tf_op jit(solution)/shard_map/ppermute | solution.py:43
  74.7 24.1 %collective-permute-start.10 = (bf16[4,64,256]{2,1,0:T(8,128)(2,1)S(1)}, bf16[4,64,256]{2,1,0:T(8,128)(2,1)S(1)}, u32[]{:S(2)}, u32[]{:S(2)}) collective-permute-start(bf16[4,64,256]{2,1,0:T(8,128)(2,1)S(1)} %get-tuple-element.45), channel_id=1, source_target_pairs={{28,0},{24,4},{20,8},{16,12},{12,16},{8,20},{4,24},{0,28},{29,1},{... | collective-permute-start | bytes 393224 | tf_op jit(solution)/shard_map/ppermute | solution.py:43
  78.1 22.7 %collective-permute-start.18 = (bf16[4,64,256]{2,1,0:T(8,128)(2,1)S(1)}, bf16[4,64,256]{2,1,0:T(8,128)(2,1)S(1)}, u32[]{:S(2)}, u32[]{:S(2)}) collective-permute-start(bf16[4,64,256]{2,1,0:T(8,128)(2,1)S(1)} %get-tuple-element.54), channel_id=1, source_target_pairs={{28,0},{24,4},{20,8},{16,12},{12,16},{8,20},{4,24},{0,28},{29,1},{... | collective-permute-start | bytes 393224 | tf_op jit(solution)/shard_map/ppermute | solution.py:43
  (13 other events, 308.5 us)

commit v3 on v2

--- a/solution.py
+++ b/solution.py
@@ -86,7 +86,28 @@
                 outs[q][:, b * block : (b + 1) * block, :] = moved.astype(jnp.bfloat16).reshape(part, block, width)
 
 
-def split(x, messages, chunks, count, first):
+def lift_kernel(m, count, x_ref, out_ref, sem):
+    first = pl.multiple_of(target(lax.axis_index("emb"), m, count) * GROUP, GROUP)
+    copy = pltpu.make_async_copy(x_ref.at[:, pl.ds(first, GROUP), :], out_ref, sem)
+    copy.start()
+    copy.wait()
+
+
+def lift(x, m, count):
+    rows, _, width = x.shape
+    return pl.pallas_call(
+        functools.partial(lift_kernel, m, count),
+        out_shape=jax.ShapeDtypeStruct((rows, GROUP, width), jnp.bfloat16),
+        in_specs=[pl.BlockSpec(memory_space=pltpu.HBM)],
+        out_specs=pl.BlockSpec(memory_space=pltpu.VMEM),
+        scratch_shapes=[pltpu.SemaphoreType.DMA],
+        compiler_params=pltpu.CompilerParams(vmem_limit_bytes=12 * 1024 * 1024),
+        cost_estimate=pl.CostEstimate(flops=10**7, bytes_accessed=10**6, transcendentals=0),
+        name="lift",
+    )(pltpu.with_memory_space_constraint(x, pltpu.HBM))
+
+
+def split(x, messages, chunks, count):
     rows, _, width = x.shape
     part = GROUP // chunks
     distinct = len({m for m, _ in messages})
@@ -103,7 +124,7 @@
         compiler_params=pltpu.CompilerParams(vmem_limit_bytes=12 * 1024 * 1024),
         cost_estimate=pl.CostEstimate(flops=10**8, bytes_accessed=10**6, transcendentals=0),
         name="split",
-    )(pltpu.with_memory_space_constraint(x, pltpu.HBM) if first else x)
+    )(x)
 
 
 def merge_kernel(messages, chunks, count, first, *refs):
@@ -161,13 +182,22 @@
     )(*operands)
 
 
-def layer_kernel(count, pieces_w, *refs):
-    blocks = refs[:count]
+def layer_kernel(count, pieces_w, raw, chunk, *refs):
+    blocks = list(refs[:count])
     weights = refs[count : count + pieces_w]
     proj_ref, fmb_ref = refs[count + pieces_w : count + pieces_w + 2]
     outs = refs[count + pieces_w + 2 : count + pieces_w + 2 + count]
-    full_w, held, mixed = refs[count + pieces_w + 2 + count :]
+    full_w, held, mixed = refs[count + pieces_w + 2 + count :][:3]
     part, rows, width = blocks[0].shape
+    if raw is not None:
+        turned = refs[-1]
+        block = row_block(rows)
+        pick = pick_matrix(GROUP * block, block * GROUP, block, GROUP)[chunk * part * block : (chunk + 1) * part * block]
+        for b in range(rows // block):
+            piece = blocks[raw][b * block : (b + 1) * block].reshape(block * GROUP, width)
+            moved = jnp.dot(pick, piece, preferred_element_type=jnp.float32)
+            turned[:, b * block : (b + 1) * block, :] = moved.astype(jnp.bfloat16).reshape(part, block, width)
+        blocks[raw] = turned
     total = count * rows
     me = lax.axis_index("emb")
     mine = lax.axis_index("dp")
@@ -199,13 +229,13 @@
     lax.fori_loop(0, part, one, 0)
 
 
-def layer(blocks, weights, proj, w_fmb):
+def layer(blocks, weights, proj, w_fmb, raw, chunk):
     part, rows, width = blocks[0].shape
     count = len(blocks)
     total = count * rows
     vmem = pl.BlockSpec(memory_space=pltpu.VMEM)
     return pl.pallas_call(
-        functools.partial(layer_kernel, count, len(weights)),
+        functools.partial(layer_kernel, count, len(weights), raw, chunk),
         out_shape=[jax.ShapeDtypeStruct((part, rows, width), jnp.bfloat16)] * count,
         in_specs=[vmem] * (count + len(weights) + 2),
         out_specs=[vmem] * count,
@@ -213,7 +243,8 @@
             pltpu.VMEM((weights[0].shape[0] * len(weights), total), jnp.bfloat16),
             pltpu.VMEM((total, width), jnp.bfloat16),
             pltpu.VMEM((total, width), jnp.float32),
-        ],
+        ]
+        + ([] if raw is None else [pltpu.VMEM((part, rows, width), jnp.bfloat16)]),
         compiler_params=pltpu.CompilerParams(vmem_limit_bytes=12 * 1024 * 1024),
         cost_estimate=pl.CostEstimate(
             flops=2 * part * total * total * width, bytes_accessed=4 * part * total * width, transcendentals=0
@@ -236,7 +267,7 @@
     if fast:
 
         def cut(names):
-            sends.update(zip(names, split(embeddings, names, chunks, count, not sends)))
+            sends.update(zip(names, split(embeddings, names, chunks, count)))
 
     else:
         turned = embeddings.reshape(rows, count, chunks, part, width).transpose(1, 2, 3, 0, 4)
@@ -252,19 +283,22 @@
         for m, c in names:
             arrived[m, c] = send(sends[m, c], m, "emb", count)
 
-    cut([(m, 0) for m in far[:2]])
-    forward([(m, 0) for m in far[:2]])
-    cut([(m, 0) for m in far[2:] + near + [0]] + [(m, c) for c in range(1, chunks) for m in far + near + [0]])
-    forward([(m, 0) for m in far[2:] + near + [0]])
+    raw = far[0] if fast else None
+    if fast:
+        lifted = lift(embeddings, raw, count)
+        lifted = send(lifted, raw, "emb", count)
+        arrived.update({(raw, c): lifted for c in range(chunks)})
+    cut([(m, c) for c in range(chunks) for m in far + near + [0] if m != raw])
+    forward([(m, 0) for m in far + near + [0] if m != raw])
     weights = []
     for q in range(others):
         weights.append(send(w_lcb, q, "dp", others))
     for c in range(1, chunks):
-        forward([(m, c) for m in near + far + [0]])
+        forward([(m, c) for m in near + far + [0] if m != raw])
 
     returned = {}
     for c in range(chunks):
-        done = layer([arrived[m, c] for m in range(count)], weights, machine_projection.T, w_fmb)
+        done = layer([arrived[m, c] for m in range(count)], weights, machine_projection.T, w_fmb, raw, c)
         for m in near + far + [0]:
             returned[m, c] = send(done[m], m, "emb", count, back=True)
 

time: 102 us -> 111 us (1.088)
  the two profiles are of different devices: /device:TPU:13 before, /device:TPU:11 now
where the time goes in v3:
time: 111 us; the launch traced here: 110 us
  waiting for transfers between devices  53 us (48%)
  starting transfers between devices  38.3 us (35%)
  Pallas kernels  17.4 us (16%)
  local copies, waits for them, and re-layouts  1.61 us (1%)
    ppermute x30, waiting for transfers between devices, send(): return lax.ppermute(value, axis, pairs)  53 us
    ppermute x30, starting transfers between devices, send(): return lax.ppermute(value, axis, pairs)  38.3 us
    pallas_call x2, Pallas kernels, layer(): pl.pallas_call(functools.partial(layer_kernel, count, len(weights), raw,...  9.16 us
    pallas_call x5, Pallas kernels, merge(): pl.pallas_call(functools.partial(merge_kernel, messages, chunks, count, f...  5.27 us
  transfers between devices with their start and end apart: 30, of which 11 were waited for; matrix products, arithmetic and copies ran while one was open for 0% of the time, Pallas kernels for 15%

profile of v3, /device:TPU:11, one launch (start us, length us, event | category | flops | bytes accessed | tf_op | source)
XLA Modules:
  0.0 110.5 jit_solution(7190763127052716722)
XLA Ops:
  2.7 1.6 %copy-done = bf16[64,64,256]{2,1,0:T(8,128)(2,1)S(1)} copy-done((bf16[64,64,256]{2,1,0:T(8,128)(2,1)S(1)}, bf16[64,64,256]{2,1,0:T(8,128)(2,1)}, u32[]{:S(2)}) %copy-start) | copy-done | bytes 2097176
  4.2 2.0 %split.1 = (bf16[4,64,256]{2,1,0:T(8,128)(2,1)S(1)}, bf16[4,64,256]{2,1,0:T(8,128)(2,1)S(1)}, bf16[4,64,256]{2,1,0:T(8,128)(2,1)S(1)}, bf16[4,64,256]{2,1,0:T(8,...) custom-call(bf16[64,64,256]{2,1,0:T(8,128)(2,1)S(1)} %copy-done), custom_call_target="tpu_custom_call" | custom-call | flops 100000000 | bytes 1000000 | tf_op jit(solution)/shard_map/split/pallas_call | solution.py:115
  6.3 1.6 %collective-permute-start = (bf16[4,64,256]{2,1,0:T(8,128)(2,1)S(1)}, bf16[4,64,256]{2,1,0:T(8,128)(2,1)S(1)}, u32[]{:S(2)}, u32[]{:S(2)}) collective-permute-start(bf16[4,64,256]{2,1,0:T(8,128)(2,1)S(1)} %get-tuple-element.36), channel_id=1, source_target_pairs={{0,4},{4,0},{8,12},{12,8},{16,20},{20,16},{24,28},{28,24},{1,5},{5... | collective-permute-start | bytes 393224 | tf_op jit(solution)/shard_map/ppermute | solution.py:43
  13.0 1.9 %collective-permute-start.4 = (bf16[4,64,256]{2,1,0:T(8,128)(2,1)S(1)}, bf16[4,64,256]{2,1,0:T(8,128)(2,1)S(1)}, u32[]{:S(2)}, u32[]{:S(2)}) collective-permute-start(bf16[4,64,256]{2,1,0:T(8,128)(2,1)S(1)} %get-tuple-element.40), channel_id=1, source_target_pairs={{0,20},{4,16},{8,28},{12,24},{16,4},{20,0},{24,12},{28,8},{1,21},{... | collective-permute-start | bytes 393224 | tf_op jit(solution)/shard_map/ppermute | solution.py:43
  16.7 17.6 %collective-permute-done.3.refs_4_ = bf16[4,64,256]{2,1,0:T(8,128)(2,1)S(1)} collective-permute-done((bf16[4,64,256]{2,1,0:T(8,128)(2,1)S(1)}, bf16[4,64,256]{2,1,0:T(8,128)(2,1)S(1)}, u32[]{:S(2)}, u32[]{:S(2)}) %collective-permute-start.3) | collective-permute-done | bytes 131104 | tf_op jit(solution)/shard_map/ppermute | solution.py:43
  34.3 2.1 %collective-permute-start.12 = (bf16[4,64,256]{2,1,0:T(8,128)(2,1)S(1)}, bf16[4,64,256]{2,1,0:T(8,128)(2,1)S(1)}, u32[]{:S(2)}, u32[]{:S(2)}) collective-permute-start(bf16[4,64,256]{2,1,0:T(8,128)(2,1)S(1)} %get-tuple-element.45), channel_id=1, source_target_pairs={{0,8},{4,12},{8,0},{12,4},{16,24},{20,28},{24,16},{28,20},{1,9},{5... | collective-permute-start | bytes 393224 | tf_op jit(solution)/shard_map/ppermute | solution.py:43
  37.1 2.4 %collective-permute-start.13 = (bf16[4,64,256]{2,1,0:T(8,128)(2,1)S(1)}, bf16[4,64,256]{2,1,0:T(8,128)(2,1)S(1)}, u32[]{:S(2)}, u32[]{:S(2)}) collective-permute-start(bf16[4,64,256]{2,1,0:T(8,128)(2,1)S(1)} %get-tuple-element.46), channel_id=1, source_target_pairs={{0,12},{4,8},{8,4},{12,0},{16,28},{20,24},{24,20},{28,16},{1,13},{... | collective-permute-start | bytes 393224 | tf_op jit(solution)/shard_map/ppermute | solution.py:43
  39.5 2.0 %collective-permute-done.6.refs_7_ = bf16[4,64,256]{2,1,0:T(8,128)(2,1)S(1)} collective-permute-done((bf16[4,64,256]{2,1,0:T(8,128)(2,1)S(1)}, bf16[4,64,256]{2,1,0:T(8,128)(2,1)S(1)}, u32[]{:S(2)}, u32[]{:S(2)}) %collective-permute-start.6) | collective-permute-done | bytes 131104 | tf_op jit(solution)/shard_map/ppermute | solution.py:43
  41.4 2.3 %collective-permute-start.15 = (bf16[4,64,256]{2,1,0:T(8,128)(2,1)S(1)}, bf16[4,64,256]{2,1,0:T(8,128)(2,1)S(1)}, u32[]{:S(2)}, u32[]{:S(2)}) collective-permute-start(bf16[4,64,256]{2,1,0:T(8,128)(2,1)S(1)} %get-tuple-element.48), channel_id=1, source_target_pairs={{0,20},{4,16},{8,28},{12,24},{16,4},{20,0},{24,12},{28,8},{1,21},{... | collective-permute-start | bytes 393224 | tf_op jit(solution)/shard_map/ppermute | solution.py:43
  43.7 1.6 %collective-permute-start.16 = (bf16[4,64,256]{2,1,0:T(8,128)(2,1)S(1)}, bf16[4,64,256]{2,1,0:T(8,128)(2,1)S(1)}, u32[]{:S(2)}, u32[]{:S(2)}) collective-permute-start(bf16[4,64,256]{2,1,0:T(8,128)(2,1)S(1)} %get-tuple-element.49), channel_id=1, source_target_pairs={{0,28},{4,24},{8,20},{12,16},{16,12},{20,8},{24,4},{28,0},{1,29},{... | collective-permute-start | bytes 393224 | tf_op jit(solution)/shard_map/ppermute | solution.py:43
  45.4 4.6 %layer.2 = (bf16[4,64,256]{2,1,0:T(8,128)(2,1)S(1)}, bf16[4,64,256]{2,1,0:T(8,128)(2,1)S(1)}, bf16[4,64,256]{2,1,0:T(8,128)(2,1)S(1)}, bf16[4,64,256]{2,1,0:T(8,...) custom-call(bf16[4,64,256]{2,1,0:T(8,128)(2,1)S(1)} %get-tuple-eleme, ...), custom_call_target="tpu_custom_call" | custom-call | flops 536870912 | bytes 2097152 | tf_op jit(solution)/shard_map/layer/pallas_call | solution.py:237
  52.4 6.5 %collective-permute-done.14.refs_4_ = bf16[4,64,256]{2,1,0:T(8,128)(2,1)S(1)} collective-permute-done((bf16[4,64,256]{2,1,0:T(8,128)(2,1)S(1)}, bf16[4,64,256]{2,1,0:T(8,128)(2,1)S(1)}, u32[]{:S(2)}, u32[]{:S(2)}) %collective-permute-start.14) | collective-permute-done | bytes 131104 | tf_op jit(solution)/shard_map/ppermute | solution.py:43
  59.0 2.6 %collective-permute-done.15.refs_5_ = bf16[4,64,256]{2,1,0:T(8,128)(2,1)S(1)} collective-permute-done((bf16[4,64,256]{2,1,0:T(8,128)(2,1)S(1)}, bf16[4,64,256]{2,1,0:T(8,128)(2,1)S(1)}, u32[]{:S(2)}, u32[]{:S(2)}) %collective-permute-start.15) | collective-permute-done | bytes 131104 | tf_op jit(solution)/shard_map/ppermute | solution.py:43
  61.6 3.1 %collective-permute-start.26 = (bf16[4,64,256]{2,1,0:T(8,128)(2,1)S(1)}, bf16[4,64,256]{2,1,0:T(8,128)(2,1)S(1)}, u32[]{:S(2)}, u32[]{:S(2)}) collective-permute-start(bf16[4,64,256]{2,1,0:T(8,128)(2,1)S(1)} %get-tuple-element.61), channel_id=1, source_target_pairs={{8,0},{12,4},{0,8},{4,12},{24,16},{28,20},{16,24},{20,28},{9,1},{1... | collective-permute-start | bytes 393224 | tf_op jit(solution)/shard_map/ppermute | solution.py:43
  64.8 1.6 %collective-permute-done.16.refs_7_ = bf16[4,64,256]{2,1,0:T(8,128)(2,1)S(1)} collective-permute-done((bf16[4,64,256]{2,1,0:T(8,128)(2,1)S(1)}, bf16[4,64,256]{2,1,0:T(8,128)(2,1)S(1)}, u32[]{:S(2)}, u32[]{:S(2)}) %collective-permute-start.16) | collective-permute-done | bytes 131104 | tf_op jit(solution)/shard_map/ppermute | solution.py:43
  66.4 4.6 %layer.3 = (bf16[4,64,256]{2,1,0:T(8,128)(2,1)S(1)}, bf16[4,64,256]{2,1,0:T(8,128)(2,1)S(1)}, bf16[4,64,256]{2,1,0:T(8,128)(2,1)S(1)}, bf16[4,64,256]{2,1,0:T(8,...) custom-call(bf16[4,64,256]{2,1,0:T(8,128)(2,1)S(1)} %get-tuple-eleme, ...), custom_call_target="tpu_custom_call" | custom-call | flops 536870912 | bytes 2097152 | tf_op jit(solution)/shard_map/layer/pallas_call | solution.py:237
  71.0 1.8 %collective-permute-start.23 = (bf16[4,64,256]{2,1,0:T(8,128)(2,1)S(1)}, bf16[4,64,256]{2,1,0:T(8,128)(2,1)S(1)}, u32[]{:S(2)}, u32[]{:S(2)}) collective-permute-start(bf16[4,64,256]{2,1,0:T(8,128)(2,1)S(1)} %get-tuple-element.56), channel_id=1, source_target_pairs={{16,0},{20,4},{24,8},{28,12},{0,16},{4,20},{8,24},{12,28},{17,1},{... | collective-permute-start | bytes 393224 | tf_op jit(solution)/shard_map/ppermute | solution.py:43
  73.7 2.7 %collective-permute-start.29 = (bf16[4,64,256]{2,1,0:T(8,128)(2,1)S(1)}, bf16[4,64,256]{2,1,0:T(8,128)(2,1)S(1)}, u32[]{:S(2)}, u32[]{:S(2)}) collective-permute-start(bf16[4,64,256]{2,1,0:T(8,128)(2,1)S(1)} %get-tuple-element.64), channel_id=1, source_target_pairs={{12,0},{8,4},{4,8},{0,12},{28,16},{24,20},{20,24},{16,28},{13,1},{... | collective-permute-start | bytes 393224 | tf_op jit(solution)/shard_map/ppermute | solution.py:43
  76.4 2.3 %collective-permute-start.21 = (bf16[4,64,256]{2,1,0:T(8,128)(2,1)S(1)}, bf16[4,64,256]{2,1,0:T(8,128)(2,1)S(1)}, u32[]{:S(2)}, u32[]{:S(2)}) collective-permute-start(bf16[4,64,256]{2,1,0:T(8,128)(2,1)S(1)} %get-tuple-element.54), channel_id=1, source_target_pairs={{20,0},{16,4},{28,8},{24,12},{4,16},{0,20},{12,24},{8,28},{21,1},{... | collective-permute-start | bytes 393224 | tf_op jit(solution)/shard_map/ppermute | solution.py:43
  78.7 1.7 %collective-permute-start.18 = (bf16[4,64,256]{2,1,0:T(8,128)(2,1)S(1)}, bf16[4,64,256]{2,1,0:T(8,128)(2,1)S(1)}, u32[]{:S(2)}, u32[]{:S(2)}) collective-permute-start(bf16[4,64,256]{2,1,0:T(8,128)(2,1)S(1)} %get-tuple-element.51), channel_id=1, source_target_pairs={{24,0},{28,4},{16,8},{20,12},{8,16},{12,20},{0,24},{4,28},{25,1},{... | collective-permute-start | bytes 393224 | tf_op jit(solution)/shard_map/ppermute | solution.py:43
  80.5 2.7 %collective-permute-done.27.refs_5_ = bf16[4,64,256]{2,1,0:T(8,128)(2,1)S(1)} collective-permute-done((bf16[4,64,256]{2,1,0:T(8,128)(2,1)S(1)}, bf16[4,64,256]{2,1,0:T(8,128)(2,1)S(1)}, u32[]{:S(2)}, u32[]{:S(2)}) %collective-permute-start.27) | collective-permute-done | bytes 131104 | tf_op jit(solution)/shard_map/ppermute | solution.py:43
  83.2 1.9 %collective-permute-start.10 = (bf16[4,64,256]{2,1,0:T(8,128)(2,1)S(1)}, bf16[4,64,256]{2,1,0:T(8,128)(2,1)S(1)}, u32[]{:S(2)}, u32[]{:S(2)}) collective-permute-start(bf16[4,64,256]{2,1,0:T(8,128)(2,1)S(1)} %get-tuple-element.42), channel_id=1, source_target_pairs={{28,0},{24,4},{20,8},{16,12},{12,16},{8,20},{4,24},{0,28},{29,1},{... | collective-permute-start | bytes 393224 | tf_op jit(solution)/shard_map/ppermute | solution.py:43
  85.0 10.1 %collective-permute-done.29.refs_7_ = bf16[4,64,256]{2,1,0:T(8,128)(2,1)S(1)} collective-permute-done((bf16[4,64,256]{2,1,0:T(8,128)(2,1)S(1)}, bf16[4,64,256]{2,1,0:T(8,128)(2,1)S(1)}, u32[]{:S(2)}, u32[]{:S(2)}) %collective-permute-start.29) | collective-permute-done | bytes 131104 | tf_op jit(solution)/shard_map/ppermute | solution.py:43
  101.0 7.2 %collective-permute-done.10.refs_0_ = bf16[4,64,256]{2,1,0:T(8,128)(2,1)S(1)} collective-permute-done((bf16[4,64,256]{2,1,0:T(8,128)(2,1)S(1)}, bf16[4,64,256]{2,1,0:T(8,128)(2,1)S(1)}, u32[]{:S(2)}, u32[]{:S(2)}) %collective-permute-start.10) | collective-permute-done | bytes 131104 | tf_op jit(solution)/shard_map/ppermute | solution.py:43
  (57 shorter events, 22.0 us)
Async XLA Ops:
  1.2 9.3 %collective-permute-start.8 = (bf16[128,512]{1,0:T(8,128)(2,1)}, bf16[128,512]{1,0:T(8,128)(2,1)S(1)}, u32[]{:S(2)}, u32[]{:S(2)}) collective-permute-start(bf16[128,512]{1,0:T(8,128)(2,1)} %refs_8_.4), channel_id=1, source_target_pairs={{0,2},{1,3},{2,0},{3,1},{4,6},{5,7},{6,4},{7,5},{8,10},{9,11},{10,... | collective-permute-start | bytes 393224 | tf_op jit(solution)/shard_map/ppermute | solution.py:43
  1.4 10.5 %collective-permute-start.7 = (bf16[128,512]{1,0:T(8,128)(2,1)}, bf16[128,512]{1,0:T(8,128)(2,1)S(1)}, u32[]{:S(2)}, u32[]{:S(2)}) collective-permute-start(bf16[128,512]{1,0:T(8,128)(2,1)} %refs_8_.4), channel_id=1, source_target_pairs={{0,1},{1,0},{2,3},{3,2},{4,5},{5,4},{6,7},{7,6},{8,9},{9,8},{10,11... | collective-permute-start | bytes 393224 | tf_op jit(solution)/shard_map/ppermute | solution.py:43
  10.6 33.2 %collective-permute-start.5 = (bf16[64,8,256]{2,1,0:T(8,128)(2,1)S(1)}, bf16[64,8,256]{2,1,0:T(8,128)(2,1)S(1)}, u32[]{:S(2)}, u32[]{:S(2)}) collective-permute-start(bf16[64,8,256]{2,1,0:T(8,128)(2,1)S(1)} %lift.1), channel_id=1, source_target_pairs={{0,24},{4,28},{8,16},{12,20},{16,8},{20,12},{24,0},{28,4},{1,25},{... | collective-permute-start | bytes 786440 | tf_op jit(solution)/shard_map/ppermute | solution.py:43
  11.9 22.4 %collective-permute-start.3 = (bf16[4,64,256]{2,1,0:T(8,128)(2,1)S(1)}, bf16[4,64,256]{2,1,0:T(8,128)(2,1)S(1)}, u32[]{:S(2)}, u32[]{:S(2)}) collective-permute-start(bf16[4,64,256]{2,1,0:T(8,128)(2,1)S(1)} %get-tuple-element.39), channel_id=1, source_target_pairs={{0,16},{4,20},{8,24},{12,28},{16,0},{20,4},{24,8},{28,12},{1,17},{... | collective-permute-start | bytes 393224 | tf_op jit(solution)/shard_map/ppermute | solution.py:43
  13.0 24.1 %collective-permute-start.4 = (bf16[4,64,256]{2,1,0:T(8,128)(2,1)S(1)}, bf16[4,64,256]{2,1,0:T(8,128)(2,1)S(1)}, u32[]{:S(2)}, u32[]{:S(2)}) collective-permute-start(bf16[4,64,256]{2,1,0:T(8,128)(2,1)S(1)} %get-tuple-element.40), channel_id=1, source_target_pairs={{0,20},{4,16},{8,28},{12,24},{16,4},{20,0},{24,12},{28,8},{1,21},{... | collective-permute-start | bytes 393224 | tf_op jit(solution)/shard_map/ppermute | solution.py:43
  14.9 26.5 %collective-permute-start.6 = (bf16[4,64,256]{2,1,0:T(8,128)(2,1)S(1)}, bf16[4,64,256]{2,1,0:T(8,128)(2,1)S(1)}, u32[]{:S(2)}, u32[]{:S(2)}) collective-permute-start(bf16[4,64,256]{2,1,0:T(8,128)(2,1)S(1)} %get-tuple-element.41), channel_id=1, source_target_pairs={{0,28},{4,24},{8,20},{12,16},{16,12},{20,8},{24,4},{28,0},{1,29},{... | collective-permute-start | bytes 393224 | tf_op jit(solution)/shard_map/ppermute | solution.py:43
  16.7 24.7 %collective-permute-start.11 = (bf16[4,64,256]{2,1,0:T(8,128)(2,1)S(1)}, bf16[4,64,256]{2,1,0:T(8,128)(2,1)S(1)}, u32[]{:S(2)}, u32[]{:S(2)}) collective-permute-start(bf16[4,64,256]{2,1,0:T(8,128)(2,1)S(1)} %get-tuple-element.44), channel_id=1, source_target_pairs={{0,4},{4,0},{8,12},{12,8},{16,20},{20,16},{24,28},{28,24},{1,5},{5... | collective-permute-start | bytes 393224 | tf_op jit(solution)/shard_map/ppermute | solution.py:43
  34.3 15.7 %collective-permute-start.12 = (bf16[4,64,256]{2,1,0:T(8,128)(2,1)S(1)}, bf16[4,64,256]{2,1,0:T(8,128)(2,1)S(1)}, u32[]{:S(2)}, u32[]{:S(2)}) collective-permute-start(bf16[4,64,256]{2,1,0:T(8,128)(2,1)S(1)} %get-tuple-element.45), channel_id=1, source_target_pairs={{0,8},{4,12},{8,0},{12,4},{16,24},{20,28},{24,16},{28,20},{1,9},{5... | collective-permute-start | bytes 393224 | tf_op jit(solution)/shard_map/ppermute | solution.py:43
  37.1 13.9 %collective-permute-start.13 = (bf16[4,64,256]{2,1,0:T(8,128)(2,1)S(1)}, bf16[4,64,256]{2,1,0:T(8,128)(2,1)S(1)}, u32[]{:S(2)}, u32[]{:S(2)}) collective-permute-start(bf16[4,64,256]{2,1,0:T(8,128)(2,1)S(1)} %get-tuple-element.46), channel_id=1, source_target_pairs={{0,12},{4,8},{8,4},{12,0},{16,28},{20,24},{24,20},{28,16},{1,13},{... | collective-permute-start | bytes 393224 | tf_op jit(solution)/shard_map/ppermute | solution.py:43
  41.4 17.4 %collective-permute-start.14 = (bf16[4,64,256]{2,1,0:T(8,128)(2,1)S(1)}, bf16[4,64,256]{2,1,0:T(8,128)(2,1)S(1)}, u32[]{:S(2)}, u32[]{:S(2)}) collective-permute-start(bf16[4,64,256]{2,1,0:T(8,128)(2,1)S(1)} %get-tuple-element.47), channel_id=1, source_target_pairs={{0,16},{4,20},{8,24},{12,28},{16,0},{20,4},{24,8},{28,12},{1,17},{... | collective-permute-start | bytes 393224 | tf_op jit(solution)/shard_map/ppermute | solution.py:43
  41.4 20.2 %collective-permute-start.15 = (bf16[4,64,256]{2,1,0:T(8,128)(2,1)S(1)}, bf16[4,64,256]{2,1,0:T(8,128)(2,1)S(1)}, u32[]{:S(2)}, u32[]{:S(2)}) collective-permute-start(bf16[4,64,256]{2,1,0:T(8,128)(2,1)S(1)} %get-tuple-element.48), channel_id=1, source_target_pairs={{0,20},{4,16},{8,28},{12,24},{16,4},{20,0},{24,12},{28,8},{1,21},{... | collective-permute-start | bytes 393224 | tf_op jit(solution)/shard_map/ppermute | solution.py:43
  43.7 22.7 %collective-permute-start.16 = (bf16[4,64,256]{2,1,0:T(8,128)(2,1)S(1)}, bf16[4,64,256]{2,1,0:T(8,128)(2,1)S(1)}, u32[]{:S(2)}, u32[]{:S(2)}) collective-permute-start(bf16[4,64,256]{2,1,0:T(8,128)(2,1)S(1)} %get-tuple-element.49), channel_id=1, source_target_pairs={{0,28},{4,24},{8,20},{12,16},{16,12},{20,8},{24,4},{28,0},{1,29},{... | collective-permute-start | bytes 393224 | tf_op jit(solution)/shard_map/ppermute | solution.py:43
  50.0 21.0 %collective-permute-start.20 = (bf16[4,64,256]{2,1,0:T(8,128)(2,1)S(1)}, bf16[4,64,256]{2,1,0:T(8,128)(2,1)S(1)}, u32[]{:S(2)}, u32[]{:S(2)}) collective-permute-start(bf16[4,64,256]{2,1,0:T(8,128)(2,1)S(1)} %get-tuple-element.53), channel_id=1, source_target_pairs={{20,0},{16,4},{28,8},{24,12},{4,16},{0,20},{12,24},{8,28},{21,1},{... | collective-permute-start | bytes 393224 | tf_op jit(solution)/shard_map/ppermute | solution.py:43
  51.0 21.8 %collective-permute-start.22 = (bf16[4,64,256]{2,1,0:T(8,128)(2,1)S(1)}, bf16[4,64,256]{2,1,0:T(8,128)(2,1)S(1)}, u32[]{:S(2)}, u32[]{:S(2)}) collective-permute-start(bf16[4,64,256]{2,1,0:T(8,128)(2,1)S(1)} %get-tuple-element.55), channel_id=1, source_target_pairs={{16,0},{20,4},{24,8},{28,12},{0,16},{4,20},{8,24},{12,28},{17,1},{... | collective-permute-start | bytes 393224 | tf_op jit(solution)/shard_map/ppermute | solution.py:43
  58.8 14.3 %collective-permute-start.24 = (bf16[4,64,256]{2,1,0:T(8,128)(2,1)S(1)}, bf16[4,64,256]{2,1,0:T(8,128)(2,1)S(1)}, u32[]{:S(2)}, u32[]{:S(2)}) collective-permute-start(bf16[4,64,256]{2,1,0:T(8,128)(2,1)S(1)} %get-tuple-element.59), channel_id=1, source_target_pairs={{4,0},{0,4},{12,8},{8,12},{20,16},{16,20},{28,24},{24,28},{5,1},{1... | collective-permute-start | bytes 393224 | tf_op jit(solution)/shard_map/ppermute | solution.py:43
  61.6 12.1 %collective-permute-start.26 = (bf16[4,64,256]{2,1,0:T(8,128)(2,1)S(1)}, bf16[4,64,256]{2,1,0:T(8,128)(2,1)S(1)}, u32[]{:S(2)}, u32[]{:S(2)}) collective-permute-start(bf16[4,64,256]{2,1,0:T(8,128)(2,1)S(1)} %get-tuple-element.61), channel_id=1, source_target_pairs={{8,0},{12,4},{0,8},{4,12},{24,16},{28,20},{16,24},{20,28},{9,1},{1... | collective-permute-start | bytes 393224 | tf_op jit(solution)/shard_map/ppermute | solution.py:43
  66.4 10.0 %collective-permute-start.28 = (bf16[4,64,256]{2,1,0:T(8,128)(2,1)S(1)}, bf16[4,64,256]{2,1,0:T(8,128)(2,1)S(1)}, u32[]{:S(2)}, u32[]{:S(2)}) collective-permute-start(bf16[4,64,256]{2,1,0:T(8,128)(2,1)S(1)} %get-tuple-element.63), channel_id=1, source_target_pairs={{12,0},{8,4},{4,8},{0,12},{28,16},{24,20},{20,24},{16,28},{13,1},{... | collective-permute-start | bytes 393224 | tf_op jit(solution)/shard_map/ppermute | solution.py:43
  73.1 10.1 %collective-permute-start.27 = (bf16[4,64,256]{2,1,0:T(8,128)(2,1)S(1)}, bf16[4,64,256]{2,1,0:T(8,128)(2,1)S(1)}, u32[]{:S(2)}, u32[]{:S(2)}) collective-permute-start(bf16[4,64,256]{2,1,0:T(8,128)(2,1)S(1)} %get-tuple-element.62), channel_id=1, source_target_pairs={{8,0},{12,4},{0,8},{4,12},{24,16},{28,20},{16,24},{20,28},{9,1},{1... | collective-permute-start | bytes 393224 | tf_op jit(solution)/shard_map/ppermute | solution.py:43
  73.7 21.4 %collective-permute-start.29 = (bf16[4,64,256]{2,1,0:T(8,128)(2,1)S(1)}, bf16[4,64,256]{2,1,0:T(8,128)(2,1)S(1)}, u32[]{:S(2)}, u32[]{:S(2)}) collective-permute-start(bf16[4,64,256]{2,1,0:T(8,128)(2,1)S(1)} %get-tuple-element.64), channel_id=1, source_target_pairs={{12,0},{8,4},{4,8},{0,12},{28,16},{24,20},{20,24},{16,28},{13,1},{... | collective-permute-start | bytes 393224 | tf_op jit(solution)/shard_map/ppermute | solution.py:43
  76.4 22.5 %collective-permute-start.21 = (bf16[4,64,256]{2,1,0:T(8,128)(2,1)S(1)}, bf16[4,64,256]{2,1,0:T(8,128)(2,1)S(1)}, u32[]{:S(2)}, u32[]{:S(2)}) collective-permute-start(bf16[4,64,256]{2,1,0:T(8,128)(2,1)S(1)} %get-tuple-element.54), channel_id=1, source_target_pairs={{20,0},{16,4},{28,8},{24,12},{4,16},{0,20},{12,24},{8,28},{21,1},{... | collective-permute-start | bytes 393224 | tf_op jit(solution)/shard_map/ppermute | solution.py:43
  78.7 21.2 %collective-permute-start.18 = (bf16[4,64,256]{2,1,0:T(8,128)(2,1)S(1)}, bf16[4,64,256]{2,1,0:T(8,128)(2,1)S(1)}, u32[]{:S(2)}, u32[]{:S(2)}) collective-permute-start(bf16[4,64,256]{2,1,0:T(8,128)(2,1)S(1)} %get-tuple-element.51), channel_id=1, source_target_pairs={{24,0},{28,4},{16,8},{20,12},{8,16},{12,20},{0,24},{4,28},{25,1},{... | collective-permute-start | bytes 393224 | tf_op jit(solution)/shard_map/ppermute | solution.py:43
  80.4 19.6 %collective-permute-start.19 = (bf16[4,64,256]{2,1,0:T(8,128)(2,1)S(1)}, bf16[4,64,256]{2,1,0:T(8,128)(2,1)S(1)}, u32[]{:S(2)}, u32[]{:S(2)}) collective-permute-start(bf16[4,64,256]{2,1,0:T(8,128)(2,1)S(1)} %get-tuple-element.52), channel_id=1, source_target_pairs={{24,0},{28,4},{16,8},{20,12},{8,16},{12,20},{0,24},{4,28},{25,1},{... | collective-permute-start | bytes 393224 | tf_op jit(solution)/shard_map/ppermute | solution.py:43
  83.2 25.1 %collective-permute-start.10 = (bf16[4,64,256]{2,1,0:T(8,128)(2,1)S(1)}, bf16[4,64,256]{2,1,0:T(8,128)(2,1)S(1)}, u32[]{:S(2)}, u32[]{:S(2)}) collective-permute-start(bf16[4,64,256]{2,1,0:T(8,128)(2,1)S(1)} %get-tuple-element.42), channel_id=1, source_target_pairs={{28,0},{24,4},{20,8},{16,12},{12,16},{8,20},{4,24},{0,28},{29,1},{... | collective-permute-start | bytes 393224 | tf_op jit(solution)/shard_map/ppermute | solution.py:43
  95.1 14.4 %collective-permute-start.17 = (bf16[4,64,256]{2,1,0:T(8,128)(2,1)S(1)}, bf16[4,64,256]{2,1,0:T(8,128)(2,1)S(1)}, u32[]{:S(2)}, u32[]{:S(2)}) collective-permute-start(bf16[4,64,256]{2,1,0:T(8,128)(2,1)S(1)} %get-tuple-element.50), channel_id=1, source_target_pairs={{28,0},{24,4},{20,8},{16,12},{12,16},{8,20},{4,24},{0,28},{29,1},{... | collective-permute-start | bytes 393224 | tf_op jit(solution)/shard_map/ppermute | solution.py:43
  (12 other events, 343.1 us)

commit v4 on v3

--- a/solution.py
+++ b/solution.py
@@ -59,7 +59,7 @@
 
 def split_kernel(messages, chunks, count, x_ref, *refs):
     outs = refs[: len(messages)]
-    landed, sems = refs[len(messages) :]
+    back_ref, landed, sems = refs[len(messages) :]
     rows, _, width = x_ref.shape
     me = lax.axis_index("emb")
     distinct = sorted({m for m, _ in messages}, key=[m for m, _ in messages].index)
@@ -73,6 +73,7 @@
     block = row_block(rows)
     part = GROUP // chunks
     pick = pick_matrix(GROUP * block, block * GROUP, block, GROUP)
+    back_ref[...] = pick_matrix(block * GROUP, GROUP * block, GROUP, block)
     for k, m in enumerate(distinct):
         fetch(k).wait()
         for q, (m2, c) in enumerate(messages):
@@ -114,9 +115,9 @@
     out = jax.ShapeDtypeStruct((part, rows, width), jnp.bfloat16)
     return pl.pallas_call(
         functools.partial(split_kernel, messages, chunks, count),
-        out_shape=[out] * len(messages),
+        out_shape=[out] * len(messages) + [jax.ShapeDtypeStruct((row_block(rows) * GROUP,) * 2, jnp.bfloat16)],
         in_specs=[pl.BlockSpec(memory_space=pltpu.HBM)],
-        out_specs=[pl.BlockSpec(memory_space=pltpu.VMEM)] * len(messages),
+        out_specs=[pl.BlockSpec(memory_space=pltpu.VMEM)] * (len(messages) + 1),
         scratch_shapes=[
             pltpu.VMEM((distinct, rows, GROUP, width), jnp.bfloat16),
             pltpu.SemaphoreType.DMA((distinct,)),
@@ -129,13 +130,13 @@
 
 def merge_kernel(messages, chunks, count, first, *refs):
     pieces = refs[: len(messages) * chunks]
-    gain_ref, bias_ref = refs[len(messages) * chunks : len(messages) * chunks + 2]
-    rest = refs[len(messages) * chunks + 2 :]
+    gain_ref, bias_ref, pick_ref = refs[len(messages) * chunks : len(messages) * chunks + 3]
+    rest = refs[len(messages) * chunks + 3 :]
     out_ref, ready, sems = rest if first else rest[1:]
     _, rows, width = pieces[0].shape
     me = lax.axis_index("emb")
     block = row_block(rows)
-    pick = pick_matrix(block * GROUP, GROUP * block, GROUP, block)
+    pick = pick_ref[...]
     blocks = rows // block
     copies = []
     for k, m in enumerate(messages):
@@ -160,16 +161,16 @@
         copy.wait()
 
 
-def merge(out, pieces, gain, bias, messages, chunks, count, samples):
+def merge(out, pieces, gain, bias, pick, messages, chunks, count, samples):
     _, rows, width = pieces[0].shape
     first = out is None
     vmem = pl.BlockSpec(memory_space=pltpu.VMEM)
     hbm = pl.BlockSpec(memory_space=pl.ANY)
-    operands = list(pieces) + [gain, bias] + ([] if first else [out])
+    operands = list(pieces) + [gain, bias, pick] + ([] if first else [out])
     return pl.pallas_call(
         functools.partial(merge_kernel, messages, chunks, count, first),
         out_shape=jax.ShapeDtypeStruct((rows, samples, width), jnp.bfloat16),
-        in_specs=[vmem] * (len(pieces) + 2) + ([] if first else [hbm]),
+        in_specs=[vmem] * (len(pieces) + 3) + ([] if first else [hbm]),
         out_specs=hbm,
         input_output_aliases={} if first else {len(operands) - 1: 0},
         scratch_shapes=[
@@ -267,7 +268,8 @@
     if fast:
 
         def cut(names):
-            sends.update(zip(names, split(embeddings, names, chunks, count)))
+            *cuts, sends["pick"] = split(embeddings, names, chunks, count)
+            sends.update(zip(names, cuts))
 
     else:
         turned = embeddings.reshape(rows, count, chunks, part, width).transpose(1, 2, 3, 0, 4)
@@ -306,7 +308,7 @@
         out = None
         for messages in [[0] + near] + [[m] for m in sorted(far)]:
             pieces = [returned[m, c] for m in messages for c in range(chunks)]
-            out = merge(out, pieces, ln_gain, ln_bias, messages, chunks, count, samples)
+            out = merge(out, pieces, ln_gain, ln_bias, sends["pick"], messages, chunks, count, samples)
         return out
     me = lax.axis_index("emb")
     stacked = jnp.stack([jnp.concatenate([returned[m, c] for c in range(chunks)]) for m in range(count)])

time: 111 us -> 111 us (level)
  the two profiles are of different devices: /device:TPU:11 before, /device:TPU:9 now
where the time goes in v4:
time: 111 us
  waiting for transfers between devices  53.1 us (48%)
  starting transfers between devices  38.3 us (35%)
  Pallas kernels  17.4 us (16%)
  local copies, waits for them, and re-layouts  1.61 us (1%)
    ppermute x30, waiting for transfers between devices, send(): return lax.ppermute(value, axis, pairs)  53.1 us
    ppermute x30, starting transfers between devices, send(): return lax.ppermute(value, axis, pairs)  38.3 us
    pallas_call x2, Pallas kernels, layer(): pl.pallas_call(functools.partial(layer_kernel, count, len(weights), raw,...  9.16 us
    pallas_call x5, Pallas kernels, merge(): pl.pallas_call(functools.partial(merge_kernel, messages, chunks, count, f...  5.2 us
  transfers between devices with their start and end apart: 30, of which 11 were waited for; matrix products, arithmetic and copies ran while one was open for 0% of the time, Pallas kernels for 15%

profile of v4, /device:TPU:9, one launch (start us, length us, event | category | flops | bytes accessed | tf_op | source)
XLA Modules:
  0.0 110.5 jit_solution(15155849038491339646)
XLA Ops:
  0.0 2.2 %collective-permute-start.9 = (bf16[128,512]{1,0:T(8,128)(2,1)}, bf16[128,512]{1,0:T(8,128)(2,1)S(1)}, u32[]{:S(2)}, u32[]{:S(2)}) collective-permute-start(bf16[128,512]{1,0:T(8,128)(2,1)} %refs_8_.4), channel_id=1, source_target_pairs={{0,3},{1,2},{2,1},{3,0},{4,7},{5,6},{6,5},{7,4},{8,11},{9,10},{10,... | collective-permute-start | bytes 393224 | tf_op jit(solution)/shard_map/ppermute | solution.py:43
  4.2 2.1 %split.1 = (bf16[4,64,256]{2,1,0:T(8,128)(2,1)S(1)}, bf16[4,64,256]{2,1,0:T(8,128)(2,1)S(1)}, bf16[4,64,256]{2,1,0:T(8,128)(2,1)S(1)}, bf16[4,64,256]{2,1,0:T(8,...) custom-call(bf16[64,64,256]{2,1,0:T(8,128)(2,1)S(1)} %copy-done), custom_call_target="tpu_custom_call" | custom-call | flops 100000000 | bytes 1000000 | tf_op jit(solution)/shard_map/split/pallas_call | solution.py:116
  7.9 1.7 %collective-permute-start.2 = (bf16[4,64,256]{2,1,0:T(8,128)(2,1)S(1)}, bf16[4,64,256]{2,1,0:T(8,128)(2,1)S(1)}, u32[]{:S(2)}, u32[]{:S(2)}) collective-permute-start(bf16[4,64,256]{2,1,0:T(8,128)(2,1)S(1)} %get-tuple-element.39), channel_id=1, source_target_pairs={{0,12},{4,8},{8,4},{12,0},{16,28},{20,24},{24,20},{28,16},{1,13},{... | collective-permute-start | bytes 393224 | tf_op jit(solution)/shard_map/ppermute | solution.py:43
  13.1 1.9 %collective-permute-start.4 = (bf16[4,64,256]{2,1,0:T(8,128)(2,1)S(1)}, bf16[4,64,256]{2,1,0:T(8,128)(2,1)S(1)}, u32[]{:S(2)}, u32[]{:S(2)}) collective-permute-start(bf16[4,64,256]{2,1,0:T(8,128)(2,1)S(1)} %get-tuple-element.41), channel_id=1, source_target_pairs={{0,20},{4,16},{8,28},{12,24},{16,4},{20,0},{24,12},{28,8},{1,21},{... | collective-permute-start | bytes 393224 | tf_op jit(solution)/shard_map/ppermute | solution.py:43
  16.8 17.6 %collective-permute-done.3.refs_4_ = bf16[4,64,256]{2,1,0:T(8,128)(2,1)S(1)} collective-permute-done((bf16[4,64,256]{2,1,0:T(8,128)(2,1)S(1)}, bf16[4,64,256]{2,1,0:T(8,128)(2,1)S(1)}, u32[]{:S(2)}, u32[]{:S(2)}) %collective-permute-start.3) | collective-permute-done | bytes 131104 | tf_op jit(solution)/shard_map/ppermute | solution.py:43
  34.3 2.1 %collective-permute-start.12 = (bf16[4,64,256]{2,1,0:T(8,128)(2,1)S(1)}, bf16[4,64,256]{2,1,0:T(8,128)(2,1)S(1)}, u32[]{:S(2)}, u32[]{:S(2)}) collective-permute-start(bf16[4,64,256]{2,1,0:T(8,128)(2,1)S(1)} %get-tuple-element.46), channel_id=1, source_target_pairs={{0,8},{4,12},{8,0},{12,4},{16,24},{20,28},{24,16},{28,20},{1,9},{5... | collective-permute-start | bytes 393224 | tf_op jit(solution)/shard_map/ppermute | solution.py:43
  37.2 2.4 %collective-permute-start.13 = (bf16[4,64,256]{2,1,0:T(8,128)(2,1)S(1)}, bf16[4,64,256]{2,1,0:T(8,128)(2,1)S(1)}, u32[]{:S(2)}, u32[]{:S(2)}) collective-permute-start(bf16[4,64,256]{2,1,0:T(8,128)(2,1)S(1)} %get-tuple-element.47), channel_id=1, source_target_pairs={{0,12},{4,8},{8,4},{12,0},{16,28},{20,24},{24,20},{28,16},{1,13},{... | collective-permute-start | bytes 393224 | tf_op jit(solution)/shard_map/ppermute | solution.py:43
  39.5 2.0 %collective-permute-done.6.refs_7_ = bf16[4,64,256]{2,1,0:T(8,128)(2,1)S(1)} collective-permute-done((bf16[4,64,256]{2,1,0:T(8,128)(2,1)S(1)}, bf16[4,64,256]{2,1,0:T(8,128)(2,1)S(1)}, u32[]{:S(2)}, u32[]{:S(2)}) %collective-permute-start.6) | collective-permute-done | bytes 131104 | tf_op jit(solution)/shard_map/ppermute | solution.py:43
  41.5 2.3 %collective-permute-start.15 = (bf16[4,64,256]{2,1,0:T(8,128)(2,1)S(1)}, bf16[4,64,256]{2,1,0:T(8,128)(2,1)S(1)}, u32[]{:S(2)}, u32[]{:S(2)}) collective-permute-start(bf16[4,64,256]{2,1,0:T(8,128)(2,1)S(1)} %get-tuple-element.49), channel_id=1, source_target_pairs={{0,20},{4,16},{8,28},{12,24},{16,4},{20,0},{24,12},{28,8},{1,21},{... | collective-permute-start | bytes 393224 | tf_op jit(solution)/shard_map/ppermute | solution.py:43
  43.8 1.6 %collective-permute-start.16 = (bf16[4,64,256]{2,1,0:T(8,128)(2,1)S(1)}, bf16[4,64,256]{2,1,0:T(8,128)(2,1)S(1)}, u32[]{:S(2)}, u32[]{:S(2)}) collective-permute-start(bf16[4,64,256]{2,1,0:T(8,128)(2,1)S(1)} %get-tuple-element.50), channel_id=1, source_target_pairs={{0,28},{4,24},{8,20},{12,16},{16,12},{20,8},{24,4},{28,0},{1,29},{... | collective-permute-start | bytes 393224 | tf_op jit(solution)/shard_map/ppermute | solution.py:43
  45.4 4.6 %layer.2 = (bf16[4,64,256]{2,1,0:T(8,128)(2,1)S(1)}, bf16[4,64,256]{2,1,0:T(8,128)(2,1)S(1)}, bf16[4,64,256]{2,1,0:T(8,128)(2,1)S(1)}, bf16[4,64,256]{2,1,0:T(8,...) custom-call(bf16[4,64,256]{2,1,0:T(8,128)(2,1)S(1)} %get-tuple-eleme, ...), custom_call_target="tpu_custom_call" | custom-call | flops 536870912 | bytes 2097152 | tf_op jit(solution)/shard_map/layer/pallas_call | solution.py:238
  52.4 6.5 %collective-permute-done.14.refs_4_ = bf16[4,64,256]{2,1,0:T(8,128)(2,1)S(1)} collective-permute-done((bf16[4,64,256]{2,1,0:T(8,128)(2,1)S(1)}, bf16[4,64,256]{2,1,0:T(8,128)(2,1)S(1)}, u32[]{:S(2)}, u32[]{:S(2)}) %collective-permute-start.14) | collective-permute-done | bytes 131104 | tf_op jit(solution)/shard_map/ppermute | solution.py:43
  59.1 2.6 %collective-permute-done.15.refs_5_ = bf16[4,64,256]{2,1,0:T(8,128)(2,1)S(1)} collective-permute-done((bf16[4,64,256]{2,1,0:T(8,128)(2,1)S(1)}, bf16[4,64,256]{2,1,0:T(8,128)(2,1)S(1)}, u32[]{:S(2)}, u32[]{:S(2)}) %collective-permute-start.15) | collective-permute-done | bytes 131104 | tf_op jit(solution)/shard_map/ppermute | solution.py:43
  61.7 3.1 %collective-permute-start.26 = (bf16[4,64,256]{2,1,0:T(8,128)(2,1)S(1)}, bf16[4,64,256]{2,1,0:T(8,128)(2,1)S(1)}, u32[]{:S(2)}, u32[]{:S(2)}) collective-permute-start(bf16[4,64,256]{2,1,0:T(8,128)(2,1)S(1)} %get-tuple-element.63), channel_id=1, source_target_pairs={{8,0},{12,4},{0,8},{4,12},{24,16},{28,20},{16,24},{20,28},{9,1},{1... | collective-permute-start | bytes 393224 | tf_op jit(solution)/shard_map/ppermute | solution.py:43
  64.8 1.6 %collective-permute-done.16.refs_7_ = bf16[4,64,256]{2,1,0:T(8,128)(2,1)S(1)} collective-permute-done((bf16[4,64,256]{2,1,0:T(8,128)(2,1)S(1)}, bf16[4,64,256]{2,1,0:T(8,128)(2,1)S(1)}, u32[]{:S(2)}, u32[]{:S(2)}) %collective-permute-start.16) | collective-permute-done | bytes 131104 | tf_op jit(solution)/shard_map/ppermute | solution.py:43
  66.5 4.6 %layer.3 = (bf16[4,64,256]{2,1,0:T(8,128)(2,1)S(1)}, bf16[4,64,256]{2,1,0:T(8,128)(2,1)S(1)}, bf16[4,64,256]{2,1,0:T(8,128)(2,1)S(1)}, bf16[4,64,256]{2,1,0:T(8,...) custom-call(bf16[4,64,256]{2,1,0:T(8,128)(2,1)S(1)} %get-tuple-eleme, ...), custom_call_target="tpu_custom_call" | custom-call | flops 536870912 | bytes 2097152 | tf_op jit(solution)/shard_map/layer/pallas_call | solution.py:238
  71.1 1.8 %collective-permute-start.23 = (bf16[4,64,256]{2,1,0:T(8,128)(2,1)S(1)}, bf16[4,64,256]{2,1,0:T(8,128)(2,1)S(1)}, u32[]{:S(2)}, u32[]{:S(2)}) collective-permute-start(bf16[4,64,256]{2,1,0:T(8,128)(2,1)S(1)} %get-tuple-element.58), channel_id=1, source_target_pairs={{16,0},{20,4},{24,8},{28,12},{0,16},{4,20},{8,24},{12,28},{17,1},{... | collective-permute-start | bytes 393224 | tf_op jit(solution)/shard_map/ppermute | solution.py:43
  73.8 2.7 %collective-permute-start.29 = (bf16[4,64,256]{2,1,0:T(8,128)(2,1)S(1)}, bf16[4,64,256]{2,1,0:T(8,128)(2,1)S(1)}, u32[]{:S(2)}, u32[]{:S(2)}) collective-permute-start(bf16[4,64,256]{2,1,0:T(8,128)(2,1)S(1)} %get-tuple-element.66), channel_id=1, source_target_pairs={{12,0},{8,4},{4,8},{0,12},{28,16},{24,20},{20,24},{16,28},{13,1},{... | collective-permute-start | bytes 393224 | tf_op jit(solution)/shard_map/ppermute | solution.py:43
  76.5 2.3 %collective-permute-start.21 = (bf16[4,64,256]{2,1,0:T(8,128)(2,1)S(1)}, bf16[4,64,256]{2,1,0:T(8,128)(2,1)S(1)}, u32[]{:S(2)}, u32[]{:S(2)}) collective-permute-start(bf16[4,64,256]{2,1,0:T(8,128)(2,1)S(1)} %get-tuple-element.56), channel_id=1, source_target_pairs={{20,0},{16,4},{28,8},{24,12},{4,16},{0,20},{12,24},{8,28},{21,1},{... | collective-permute-start | bytes 393224 | tf_op jit(solution)/shard_map/ppermute | solution.py:43
  78.8 1.7 %collective-permute-start.18 = (bf16[4,64,256]{2,1,0:T(8,128)(2,1)S(1)}, bf16[4,64,256]{2,1,0:T(8,128)(2,1)S(1)}, u32[]{:S(2)}, u32[]{:S(2)}) collective-permute-start(bf16[4,64,256]{2,1,0:T(8,128)(2,1)S(1)} %get-tuple-element.53), channel_id=1, source_target_pairs={{24,0},{28,4},{16,8},{20,12},{8,16},{12,20},{0,24},{4,28},{25,1},{... | collective-permute-start | bytes 393224 | tf_op jit(solution)/shard_map/ppermute | solution.py:43
  80.5 2.7 %collective-permute-done.27.refs_5_ = bf16[4,64,256]{2,1,0:T(8,128)(2,1)S(1)} collective-permute-done((bf16[4,64,256]{2,1,0:T(8,128)(2,1)S(1)}, bf16[4,64,256]{2,1,0:T(8,128)(2,1)S(1)}, u32[]{:S(2)}, u32[]{:S(2)}) %collective-permute-start.27) | collective-permute-done | bytes 131104 | tf_op jit(solution)/shard_map/ppermute | solution.py:43
  83.2 1.9 %collective-permute-start.10 = (bf16[4,64,256]{2,1,0:T(8,128)(2,1)S(1)}, bf16[4,64,256]{2,1,0:T(8,128)(2,1)S(1)}, u32[]{:S(2)}, u32[]{:S(2)}) collective-permute-start(bf16[4,64,256]{2,1,0:T(8,128)(2,1)S(1)} %get-tuple-element.43), channel_id=1, source_target_pairs={{28,0},{24,4},{20,8},{16,12},{12,16},{8,20},{4,24},{0,28},{29,1},{... | collective-permute-start | bytes 393224 | tf_op jit(solution)/shard_map/ppermute | solution.py:43
  85.1 10.1 %collective-permute-done.29.refs_7_ = bf16[4,64,256]{2,1,0:T(8,128)(2,1)S(1)} collective-permute-done((bf16[4,64,256]{2,1,0:T(8,128)(2,1)S(1)}, bf16[4,64,256]{2,1,0:T(8,128)(2,1)S(1)}, u32[]{:S(2)}, u32[]{:S(2)}) %collective-permute-start.29) | collective-permute-done | bytes 131104 | tf_op jit(solution)/shard_map/ppermute | solution.py:43
  101.0 7.3 %collective-permute-done.10.refs_0_ = bf16[4,64,256]{2,1,0:T(8,128)(2,1)S(1)} collective-permute-done((bf16[4,64,256]{2,1,0:T(8,128)(2,1)S(1)}, bf16[4,64,256]{2,1,0:T(8,128)(2,1)S(1)}, u32[]{:S(2)}, u32[]{:S(2)}) %collective-permute-start.10) | collective-permute-done | bytes 131104 | tf_op jit(solution)/shard_map/ppermute | solution.py:43
  (57 shorter events, 21.2 us)
Async XLA Ops:
  2.4 9.6 %collective-permute-start.7 = (bf16[128,512]{1,0:T(8,128)(2,1)}, bf16[128,512]{1,0:T(8,128)(2,1)S(1)}, u32[]{:S(2)}, u32[]{:S(2)}) collective-permute-start(bf16[128,512]{1,0:T(8,128)(2,1)} %refs_8_.4), channel_id=1, source_target_pairs={{0,1},{1,0},{2,3},{3,2},{4,5},{5,4},{6,7},{7,6},{8,9},{9,8},{10,11... | collective-permute-start | bytes 393224 | tf_op jit(solution)/shard_map/ppermute | solution.py:43
  7.9 8.9 %collective-permute-start.2 = (bf16[4,64,256]{2,1,0:T(8,128)(2,1)S(1)}, bf16[4,64,256]{2,1,0:T(8,128)(2,1)S(1)}, u32[]{:S(2)}, u32[]{:S(2)}) collective-permute-start(bf16[4,64,256]{2,1,0:T(8,128)(2,1)S(1)} %get-tuple-element.39), channel_id=1, source_target_pairs={{0,12},{4,8},{8,4},{12,0},{16,28},{20,24},{24,20},{28,16},{1,13},{... | collective-permute-start | bytes 393224 | tf_op jit(solution)/shard_map/ppermute | solution.py:43
  10.6 33.2 %collective-permute-start.5 = (bf16[64,8,256]{2,1,0:T(8,128)(2,1)S(1)}, bf16[64,8,256]{2,1,0:T(8,128)(2,1)S(1)}, u32[]{:S(2)}, u32[]{:S(2)}) collective-permute-start(bf16[64,8,256]{2,1,0:T(8,128)(2,1)S(1)} %lift.1), channel_id=1, source_target_pairs={{0,24},{4,28},{8,16},{12,20},{16,8},{20,12},{24,0},{28,4},{1,25},{... | collective-permute-start | bytes 786440 | tf_op jit(solution)/shard_map/ppermute | solution.py:43
  12.0 22.4 %collective-permute-start.3 = (bf16[4,64,256]{2,1,0:T(8,128)(2,1)S(1)}, bf16[4,64,256]{2,1,0:T(8,128)(2,1)S(1)}, u32[]{:S(2)}, u32[]{:S(2)}) collective-permute-start(bf16[4,64,256]{2,1,0:T(8,128)(2,1)S(1)} %get-tuple-element.40), channel_id=1, source_target_pairs={{0,16},{4,20},{8,24},{12,28},{16,0},{20,4},{24,8},{28,12},{1,17},{... | collective-permute-start | bytes 393224 | tf_op jit(solution)/shard_map/ppermute | solution.py:43
  13.1 24.1 %collective-permute-start.4 = (bf16[4,64,256]{2,1,0:T(8,128)(2,1)S(1)}, bf16[4,64,256]{2,1,0:T(8,128)(2,1)S(1)}, u32[]{:S(2)}, u32[]{:S(2)}) collective-permute-start(bf16[4,64,256]{2,1,0:T(8,128)(2,1)S(1)} %get-tuple-element.41), channel_id=1, source_target_pairs={{0,20},{4,16},{8,28},{12,24},{16,4},{20,0},{24,12},{28,8},{1,21},{... | collective-permute-start | bytes 393224 | tf_op jit(solution)/shard_map/ppermute | solution.py:43
  15.0 26.5 %collective-permute-start.6 = (bf16[4,64,256]{2,1,0:T(8,128)(2,1)S(1)}, bf16[4,64,256]{2,1,0:T(8,128)(2,1)S(1)}, u32[]{:S(2)}, u32[]{:S(2)}) collective-permute-start(bf16[4,64,256]{2,1,0:T(8,128)(2,1)S(1)} %get-tuple-element.42), channel_id=1, source_target_pairs={{0,28},{4,24},{8,20},{12,16},{16,12},{20,8},{24,4},{28,0},{1,29},{... | collective-permute-start | bytes 393224 | tf_op jit(solution)/shard_map/ppermute | solution.py:43
  16.8 24.7 %collective-permute-start.11 = (bf16[4,64,256]{2,1,0:T(8,128)(2,1)S(1)}, bf16[4,64,256]{2,1,0:T(8,128)(2,1)S(1)}, u32[]{:S(2)}, u32[]{:S(2)}) collective-permute-start(bf16[4,64,256]{2,1,0:T(8,128)(2,1)S(1)} %get-tuple-element.45), channel_id=1, source_target_pairs={{0,4},{4,0},{8,12},{12,8},{16,20},{20,16},{24,28},{28,24},{1,5},{5... | collective-permute-start | bytes 393224 | tf_op jit(solution)/shard_map/ppermute | solution.py:43
  34.3 15.7 %collective-permute-start.12 = (bf16[4,64,256]{2,1,0:T(8,128)(2,1)S(1)}, bf16[4,64,256]{2,1,0:T(8,128)(2,1)S(1)}, u32[]{:S(2)}, u32[]{:S(2)}) collective-permute-start(bf16[4,64,256]{2,1,0:T(8,128)(2,1)S(1)} %get-tuple-element.46), channel_id=1, source_target_pairs={{0,8},{4,12},{8,0},{12,4},{16,24},{20,28},{24,16},{28,20},{1,9},{5... | collective-permute-start | bytes 393224 | tf_op jit(solution)/shard_map/ppermute | solution.py:43
  37.2 13.9 %collective-permute-start.13 = (bf16[4,64,256]{2,1,0:T(8,128)(2,1)S(1)}, bf16[4,64,256]{2,1,0:T(8,128)(2,1)S(1)}, u32[]{:S(2)}, u32[]{:S(2)}) collective-permute-start(bf16[4,64,256]{2,1,0:T(8,128)(2,1)S(1)} %get-tuple-element.47), channel_id=1, source_target_pairs={{0,12},{4,8},{8,4},{12,0},{16,28},{20,24},{24,20},{28,16},{1,13},{... | collective-permute-start | bytes 393224 | tf_op jit(solution)/shard_map/ppermute | solution.py:43
  41.5 17.4 %collective-permute-start.14 = (bf16[4,64,256]{2,1,0:T(8,128)(2,1)S(1)}, bf16[4,64,256]{2,1,0:T(8,128)(2,1)S(1)}, u32[]{:S(2)}, u32[]{:S(2)}) collective-permute-start(bf16[4,64,256]{2,1,0:T(8,128)(2,1)S(1)} %get-tuple-element.48), channel_id=1, source_target_pairs={{0,16},{4,20},{8,24},{12,28},{16,0},{20,4},{24,8},{28,12},{1,17},{... | collective-permute-start | bytes 393224 | tf_op jit(solution)/shard_map/ppermute | solution.py:43
  41.5 20.2 %collective-permute-start.15 = (bf16[4,64,256]{2,1,0:T(8,128)(2,1)S(1)}, bf16[4,64,256]{2,1,0:T(8,128)(2,1)S(1)}, u32[]{:S(2)}, u32[]{:S(2)}) collective-permute-start(bf16[4,64,256]{2,1,0:T(8,128)(2,1)S(1)} %get-tuple-element.49), channel_id=1, source_target_pairs={{0,20},{4,16},{8,28},{12,24},{16,4},{20,0},{24,12},{28,8},{1,21},{... | collective-permute-start | bytes 393224 | tf_op jit(solution)/shard_map/ppermute | solution.py:43
  43.8 22.7 %collective-permute-start.16 = (bf16[4,64,256]{2,1,0:T(8,128)(2,1)S(1)}, bf16[4,64,256]{2,1,0:T(8,128)(2,1)S(1)}, u32[]{:S(2)}, u32[]{:S(2)}) collective-permute-start(bf16[4,64,256]{2,1,0:T(8,128)(2,1)S(1)} %get-tuple-element.50), channel_id=1, source_target_pairs={{0,28},{4,24},{8,20},{12,16},{16,12},{20,8},{24,4},{28,0},{1,29},{... | collective-permute-start | bytes 393224 | tf_op jit(solution)/shard_map/ppermute | solution.py:43
  50.0 21.0 %collective-permute-start.20 = (bf16[4,64,256]{2,1,0:T(8,128)(2,1)S(1)}, bf16[4,64,256]{2,1,0:T(8,128)(2,1)S(1)}, u32[]{:S(2)}, u32[]{:S(2)}) collective-permute-start(bf16[4,64,256]{2,1,0:T(8,128)(2,1)S(1)} %get-tuple-element.55), channel_id=1, source_target_pairs={{20,0},{16,4},{28,8},{24,12},{4,16},{0,20},{12,24},{8,28},{21,1},{... | collective-permute-start | bytes 393224 | tf_op jit(solution)/shard_map/ppermute | solution.py:43
  51.1 21.8 %collective-permute-start.22 = (bf16[4,64,256]{2,1,0:T(8,128)(2,1)S(1)}, bf16[4,64,256]{2,1,0:T(8,128)(2,1)S(1)}, u32[]{:S(2)}, u32[]{:S(2)}) collective-permute-start(bf16[4,64,256]{2,1,0:T(8,128)(2,1)S(1)} %get-tuple-element.57), channel_id=1, source_target_pairs={{16,0},{20,4},{24,8},{28,12},{0,16},{4,20},{8,24},{12,28},{17,1},{... | collective-permute-start | bytes 393224 | tf_op jit(solution)/shard_map/ppermute | solution.py:43
  58.9 14.3 %collective-permute-start.24 = (bf16[4,64,256]{2,1,0:T(8,128)(2,1)S(1)}, bf16[4,64,256]{2,1,0:T(8,128)(2,1)S(1)}, u32[]{:S(2)}, u32[]{:S(2)}) collective-permute-start(bf16[4,64,256]{2,1,0:T(8,128)(2,1)S(1)} %get-tuple-element.61), channel_id=1, source_target_pairs={{4,0},{0,4},{12,8},{8,12},{20,16},{16,20},{28,24},{24,28},{5,1},{1... | collective-permute-start | bytes 393224 | tf_op jit(solution)/shard_map/ppermute | solution.py:43
  61.7 12.1 %collective-permute-start.26 = (bf16[4,64,256]{2,1,0:T(8,128)(2,1)S(1)}, bf16[4,64,256]{2,1,0:T(8,128)(2,1)S(1)}, u32[]{:S(2)}, u32[]{:S(2)}) collective-permute-start(bf16[4,64,256]{2,1,0:T(8,128)(2,1)S(1)} %get-tuple-element.63), channel_id=1, source_target_pairs={{8,0},{12,4},{0,8},{4,12},{24,16},{28,20},{16,24},{20,28},{9,1},{1... | collective-permute-start | bytes 393224 | tf_op jit(solution)/shard_map/ppermute | solution.py:43
  66.5 10.0 %collective-permute-start.28 = (bf16[4,64,256]{2,1,0:T(8,128)(2,1)S(1)}, bf16[4,64,256]{2,1,0:T(8,128)(2,1)S(1)}, u32[]{:S(2)}, u32[]{:S(2)}) collective-permute-start(bf16[4,64,256]{2,1,0:T(8,128)(2,1)S(1)} %get-tuple-element.65), channel_id=1, source_target_pairs={{12,0},{8,4},{4,8},{0,12},{28,16},{24,20},{20,24},{16,28},{13,1},{... | collective-permute-start | bytes 393224 | tf_op jit(solution)/shard_map/ppermute | solution.py:43
  73.2 10.1 %collective-permute-start.27 = (bf16[4,64,256]{2,1,0:T(8,128)(2,1)S(1)}, bf16[4,64,256]{2,1,0:T(8,128)(2,1)S(1)}, u32[]{:S(2)}, u32[]{:S(2)}) collective-permute-start(bf16[4,64,256]{2,1,0:T(8,128)(2,1)S(1)} %get-tuple-element.64), channel_id=1, source_target_pairs={{8,0},{12,4},{0,8},{4,12},{24,16},{28,20},{16,24},{20,28},{9,1},{1... | collective-permute-start | bytes 393224 | tf_op jit(solution)/shard_map/ppermute | solution.py:43
  73.8 21.4 %collective-permute-start.29 = (bf16[4,64,256]{2,1,0:T(8,128)(2,1)S(1)}, bf16[4,64,256]{2,1,0:T(8,128)(2,1)S(1)}, u32[]{:S(2)}, u32[]{:S(2)}) collective-permute-start(bf16[4,64,256]{2,1,0:T(8,128)(2,1)S(1)} %get-tuple-element.66), channel_id=1, source_target_pairs={{12,0},{8,4},{4,8},{0,12},{28,16},{24,20},{20,24},{16,28},{13,1},{... | collective-permute-start | bytes 393224 | tf_op jit(solution)/shard_map/ppermute | solution.py:43
  76.5 22.5 %collective-permute-start.21 = (bf16[4,64,256]{2,1,0:T(8,128)(2,1)S(1)}, bf16[4,64,256]{2,1,0:T(8,128)(2,1)S(1)}, u32[]{:S(2)}, u32[]{:S(2)}) collective-permute-start(bf16[4,64,256]{2,1,0:T(8,128)(2,1)S(1)} %get-tuple-element.56), channel_id=1, source_target_pairs={{20,0},{16,4},{28,8},{24,12},{4,16},{0,20},{12,24},{8,28},{21,1},{... | collective-permute-start | bytes 393224 | tf_op jit(solution)/shard_map/ppermute | solution.py:43
  78.8 21.2 %collective-permute-start.18 = (bf16[4,64,256]{2,1,0:T(8,128)(2,1)S(1)}, bf16[4,64,256]{2,1,0:T(8,128)(2,1)S(1)}, u32[]{:S(2)}, u32[]{:S(2)}) collective-permute-start(bf16[4,64,256]{2,1,0:T(8,128)(2,1)S(1)} %get-tuple-element.53), channel_id=1, source_target_pairs={{24,0},{28,4},{16,8},{20,12},{8,16},{12,20},{0,24},{4,28},{25,1},{... | collective-permute-start | bytes 393224 | tf_op jit(solution)/shard_map/ppermute | solution.py:43
  80.5 19.5 %collective-permute-start.19 = (bf16[4,64,256]{2,1,0:T(8,128)(2,1)S(1)}, bf16[4,64,256]{2,1,0:T(8,128)(2,1)S(1)}, u32[]{:S(2)}, u32[]{:S(2)}) collective-permute-start(bf16[4,64,256]{2,1,0:T(8,128)(2,1)S(1)} %get-tuple-element.54), channel_id=1, source_target_pairs={{24,0},{28,4},{16,8},{20,12},{8,16},{12,20},{0,24},{4,28},{25,1},{... | collective-permute-start | bytes 393224 | tf_op jit(solution)/shard_map/ppermute | solution.py:43
  83.2 25.1 %collective-permute-start.10 = (bf16[4,64,256]{2,1,0:T(8,128)(2,1)S(1)}, bf16[4,64,256]{2,1,0:T(8,128)(2,1)S(1)}, u32[]{:S(2)}, u32[]{:S(2)}) collective-permute-start(bf16[4,64,256]{2,1,0:T(8,128)(2,1)S(1)} %get-tuple-element.43), channel_id=1, source_target_pairs={{28,0},{24,4},{20,8},{16,12},{12,16},{8,20},{4,24},{0,28},{29,1},{... | collective-permute-start | bytes 393224 | tf_op jit(solution)/shard_map/ppermute | solution.py:43
  95.2 14.4 %collective-permute-start.17 = (bf16[4,64,256]{2,1,0:T(8,128)(2,1)S(1)}, bf16[4,64,256]{2,1,0:T(8,128)(2,1)S(1)}, u32[]{:S(2)}, u32[]{:S(2)}) collective-permute-start(bf16[4,64,256]{2,1,0:T(8,128)(2,1)S(1)} %get-tuple-element.51), channel_id=1, source_target_pairs={{28,0},{24,4},{20,8},{16,12},{12,16},{8,20},{4,24},{0,28},{29,1},{... | collective-permute-start | bytes 393224 | tf_op jit(solution)/shard_map/ppermute | solution.py:43
  (12 other events, 342.9 us)

commit v5 on v4

--- a/solution.py
+++ b/solution.py
@@ -50,6 +50,10 @@
     return size
 
 
+def merge_block(rows):
+    return min(row_block(rows), 16)
+
+
 def pick_matrix(height, width, inner_out, inner_in):
     i = lax.broadcasted_iota(jnp.int32, (height, width), 0)
     j = lax.broadcasted_iota(jnp.int32, (height, width), 1)
@@ -73,7 +77,8 @@
     block = row_block(rows)
     part = GROUP // chunks
     pick = pick_matrix(GROUP * block, block * GROUP, block, GROUP)
-    back_ref[...] = pick_matrix(block * GROUP, GROUP * block, GROUP, block)
+    turn = merge_block(rows)
+    back_ref[...] = pick_matrix(turn * GROUP, GROUP * turn, GROUP, turn)
     for k, m in enumerate(distinct):
         fetch(k).wait()
         for q, (m2, c) in enumerate(messages):
@@ -115,7 +120,7 @@
     out = jax.ShapeDtypeStruct((part, rows, width), jnp.bfloat16)
     return pl.pallas_call(
         functools.partial(split_kernel, messages, chunks, count),
-        out_shape=[out] * len(messages) + [jax.ShapeDtypeStruct((row_block(rows) * GROUP,) * 2, jnp.bfloat16)],
+        out_shape=[out] * len(messages) + [jax.ShapeDtypeStruct((merge_block(rows) * GROUP,) * 2, jnp.bfloat16)],
         in_specs=[pl.BlockSpec(memory_space=pltpu.HBM)],
         out_specs=[pl.BlockSpec(memory_space=pltpu.VMEM)] * (len(messages) + 1),
         scratch_shapes=[
@@ -135,7 +140,7 @@
     out_ref, ready, sems = rest if first else rest[1:]
     _, rows, width = pieces[0].shape
     me = lax.axis_index("emb")
-    block = row_block(rows)
+    block = merge_block(rows)
     pick = pick_ref[...]
     blocks = rows // block
     copies = []
@@ -175,7 +180,7 @@
         input_output_aliases={} if first else {len(operands) - 1: 0},
         scratch_shapes=[
             pltpu.VMEM((len(messages), rows, GROUP, width), jnp.bfloat16),
-            pltpu.SemaphoreType.DMA((len(messages) * (rows // row_block(rows)),)),
+            pltpu.SemaphoreType.DMA((len(messages) * (rows // merge_block(rows)),)),
         ],
         compiler_params=pltpu.CompilerParams(vmem_limit_bytes=12 * 1024 * 1024),
         cost_estimate=pl.CostEstimate(flops=10**8, bytes_accessed=10**6, transcendentals=0),

time: 111 us -> 111 us (level)
  the two profiles are of different devices: /device:TPU:9 before, /device:TPU:13 now
where the time goes in v5:
time: 111 us; the launch traced here: 110 us
  waiting for transfers between devices  53.2 us (48%)
  starting transfers between devices  38.3 us (35%)
  Pallas kernels  17.1 us (15%)
  local copies, waits for them, and re-layouts  1.61 us (1%)
    ppermute x30, waiting for transfers between devices, send(): return lax.ppermute(value, axis, pairs)  53.2 us
    ppermute x30, starting transfers between devices, send(): return lax.ppermute(value, axis, pairs)  38.3 us
    pallas_call x2, Pallas kernels, layer(): pl.pallas_call(functools.partial(layer_kernel, count, len(weights), raw,...  9.16 us
    pallas_call x5, Pallas kernels, merge(): pl.pallas_call(functools.partial(merge_kernel, messages, chunks, count, f...  4.98 us
  transfers between devices with their start and end apart: 30, of which 11 were waited for; matrix products, arithmetic and copies ran while one was open for 0% of the time, Pallas kernels for 15%

profile of v5, /device:TPU:13, one launch (start us, length us, event | category | flops | bytes accessed | tf_op | source)
XLA Modules:
  0.0 110.4 jit_solution(5891549956138719511)
XLA Ops:
  2.7 1.6 %copy-done = bf16[64,64,256]{2,1,0:T(8,128)(2,1)S(1)} copy-done((bf16[64,64,256]{2,1,0:T(8,128)(2,1)S(1)}, bf16[64,64,256]{2,1,0:T(8,128)(2,1)}, u32[]{:S(2)}) %copy-start) | copy-done | bytes 2097176
  4.2 2.0 %split.1 = (bf16[4,64,256]{2,1,0:T(8,128)(2,1)S(1)}, bf16[4,64,256]{2,1,0:T(8,128)(2,1)S(1)}, bf16[4,64,256]{2,1,0:T(8,128)(2,1)S(1)}, bf16[4,64,256]{2,1,0:T(8,...) custom-call(bf16[64,64,256]{2,1,0:T(8,128)(2,1)S(1)} %copy-done), custom_call_target="tpu_custom_call" | custom-call | flops 100000000 | bytes 1000000 | tf_op jit(solution)/shard_map/split/pallas_call | solution.py:121
  6.3 1.6 %collective-permute-start = (bf16[4,64,256]{2,1,0:T(8,128)(2,1)S(1)}, bf16[4,64,256]{2,1,0:T(8,128)(2,1)S(1)}, u32[]{:S(2)}, u32[]{:S(2)}) collective-permute-start(bf16[4,64,256]{2,1,0:T(8,128)(2,1)S(1)} %get-tuple-element.37), channel_id=1, source_target_pairs={{0,4},{4,0},{8,12},{12,8},{16,20},{20,16},{24,28},{28,24},{1,5},{5... | collective-permute-start | bytes 393224 | tf_op jit(solution)/shard_map/ppermute | solution.py:43
  13.1 1.9 %collective-permute-start.4 = (bf16[4,64,256]{2,1,0:T(8,128)(2,1)S(1)}, bf16[4,64,256]{2,1,0:T(8,128)(2,1)S(1)}, u32[]{:S(2)}, u32[]{:S(2)}) collective-permute-start(bf16[4,64,256]{2,1,0:T(8,128)(2,1)S(1)} %get-tuple-element.41), channel_id=1, source_target_pairs={{0,20},{4,16},{8,28},{12,24},{16,4},{20,0},{24,12},{28,8},{1,21},{... | collective-permute-start | bytes 393224 | tf_op jit(solution)/shard_map/ppermute | solution.py:43
  16.7 17.6 %collective-permute-done.3.refs_4_ = bf16[4,64,256]{2,1,0:T(8,128)(2,1)S(1)} collective-permute-done((bf16[4,64,256]{2,1,0:T(8,128)(2,1)S(1)}, bf16[4,64,256]{2,1,0:T(8,128)(2,1)S(1)}, u32[]{:S(2)}, u32[]{:S(2)}) %collective-permute-start.3) | collective-permute-done | bytes 131104 | tf_op jit(solution)/shard_map/ppermute | solution.py:43
  34.3 2.1 %collective-permute-start.12 = (bf16[4,64,256]{2,1,0:T(8,128)(2,1)S(1)}, bf16[4,64,256]{2,1,0:T(8,128)(2,1)S(1)}, u32[]{:S(2)}, u32[]{:S(2)}) collective-permute-start(bf16[4,64,256]{2,1,0:T(8,128)(2,1)S(1)} %get-tuple-element.46), channel_id=1, source_target_pairs={{0,8},{4,12},{8,0},{12,4},{16,24},{20,28},{24,16},{28,20},{1,9},{5... | collective-permute-start | bytes 393224 | tf_op jit(solution)/shard_map/ppermute | solution.py:43
  37.1 2.4 %collective-permute-start.13 = (bf16[4,64,256]{2,1,0:T(8,128)(2,1)S(1)}, bf16[4,64,256]{2,1,0:T(8,128)(2,1)S(1)}, u32[]{:S(2)}, u32[]{:S(2)}) collective-permute-start(bf16[4,64,256]{2,1,0:T(8,128)(2,1)S(1)} %get-tuple-element.47), channel_id=1, source_target_pairs={{0,12},{4,8},{8,4},{12,0},{16,28},{20,24},{24,20},{28,16},{1,13},{... | collective-permute-start | bytes 393224 | tf_op jit(solution)/shard_map/ppermute | solution.py:43
  39.5 2.0 %collective-permute-done.6.refs_7_ = bf16[4,64,256]{2,1,0:T(8,128)(2,1)S(1)} collective-permute-done((bf16[4,64,256]{2,1,0:T(8,128)(2,1)S(1)}, bf16[4,64,256]{2,1,0:T(8,128)(2,1)S(1)}, u32[]{:S(2)}, u32[]{:S(2)}) %collective-permute-start.6) | collective-permute-done | bytes 131104 | tf_op jit(solution)/shard_map/ppermute | solution.py:43
  41.5 2.3 %collective-permute-start.15 = (bf16[4,64,256]{2,1,0:T(8,128)(2,1)S(1)}, bf16[4,64,256]{2,1,0:T(8,128)(2,1)S(1)}, u32[]{:S(2)}, u32[]{:S(2)}) collective-permute-start(bf16[4,64,256]{2,1,0:T(8,128)(2,1)S(1)} %get-tuple-element.49), channel_id=1, source_target_pairs={{0,20},{4,16},{8,28},{12,24},{16,4},{20,0},{24,12},{28,8},{1,21},{... | collective-permute-start | bytes 393224 | tf_op jit(solution)/shard_map/ppermute | solution.py:43
  43.8 1.6 %collective-permute-start.16 = (bf16[4,64,256]{2,1,0:T(8,128)(2,1)S(1)}, bf16[4,64,256]{2,1,0:T(8,128)(2,1)S(1)}, u32[]{:S(2)}, u32[]{:S(2)}) collective-permute-start(bf16[4,64,256]{2,1,0:T(8,128)(2,1)S(1)} %get-tuple-element.50), channel_id=1, source_target_pairs={{0,28},{4,24},{8,20},{12,16},{16,12},{20,8},{24,4},{28,0},{1,29},{... | collective-permute-start | bytes 393224 | tf_op jit(solution)/shard_map/ppermute | solution.py:43
  45.4 4.6 %layer.2 = (bf16[4,64,256]{2,1,0:T(8,128)(2,1)S(1)}, bf16[4,64,256]{2,1,0:T(8,128)(2,1)S(1)}, bf16[4,64,256]{2,1,0:T(8,128)(2,1)S(1)}, bf16[4,64,256]{2,1,0:T(8,...) custom-call(bf16[4,64,256]{2,1,0:T(8,128)(2,1)S(1)} %get-tuple-eleme, ...), custom_call_target="tpu_custom_call" | custom-call | flops 536870912 | bytes 2097152 | tf_op jit(solution)/shard_map/layer/pallas_call | solution.py:243
  52.4 6.5 %collective-permute-done.14.refs_4_ = bf16[4,64,256]{2,1,0:T(8,128)(2,1)S(1)} collective-permute-done((bf16[4,64,256]{2,1,0:T(8,128)(2,1)S(1)}, bf16[4,64,256]{2,1,0:T(8,128)(2,1)S(1)}, u32[]{:S(2)}, u32[]{:S(2)}) %collective-permute-start.14) | collective-permute-done | bytes 131104 | tf_op jit(solution)/shard_map/ppermute | solution.py:43
  59.0 2.6 %collective-permute-done.15.refs_5_ = bf16[4,64,256]{2,1,0:T(8,128)(2,1)S(1)} collective-permute-done((bf16[4,64,256]{2,1,0:T(8,128)(2,1)S(1)}, bf16[4,64,256]{2,1,0:T(8,128)(2,1)S(1)}, u32[]{:S(2)}, u32[]{:S(2)}) %collective-permute-start.15) | collective-permute-done | bytes 131104 | tf_op jit(solution)/shard_map/ppermute | solution.py:43
  61.7 3.1 %collective-permute-start.26 = (bf16[4,64,256]{2,1,0:T(8,128)(2,1)S(1)}, bf16[4,64,256]{2,1,0:T(8,128)(2,1)S(1)}, u32[]{:S(2)}, u32[]{:S(2)}) collective-permute-start(bf16[4,64,256]{2,1,0:T(8,128)(2,1)S(1)} %get-tuple-element.63), channel_id=1, source_target_pairs={{8,0},{12,4},{0,8},{4,12},{24,16},{28,20},{16,24},{20,28},{9,1},{1... | collective-permute-start | bytes 393224 | tf_op jit(solution)/shard_map/ppermute | solution.py:43
  64.8 1.6 %collective-permute-done.16.refs_7_ = bf16[4,64,256]{2,1,0:T(8,128)(2,1)S(1)} collective-permute-done((bf16[4,64,256]{2,1,0:T(8,128)(2,1)S(1)}, bf16[4,64,256]{2,1,0:T(8,128)(2,1)S(1)}, u32[]{:S(2)}, u32[]{:S(2)}) %collective-permute-start.16) | collective-permute-done | bytes 131104 | tf_op jit(solution)/shard_map/ppermute | solution.py:43
  66.4 4.6 %layer.3 = (bf16[4,64,256]{2,1,0:T(8,128)(2,1)S(1)}, bf16[4,64,256]{2,1,0:T(8,128)(2,1)S(1)}, bf16[4,64,256]{2,1,0:T(8,128)(2,1)S(1)}, bf16[4,64,256]{2,1,0:T(8,...) custom-call(bf16[4,64,256]{2,1,0:T(8,128)(2,1)S(1)} %get-tuple-eleme, ...), custom_call_target="tpu_custom_call" | custom-call | flops 536870912 | bytes 2097152 | tf_op jit(solution)/shard_map/layer/pallas_call | solution.py:243
  71.0 1.8 %collective-permute-start.23 = (bf16[4,64,256]{2,1,0:T(8,128)(2,1)S(1)}, bf16[4,64,256]{2,1,0:T(8,128)(2,1)S(1)}, u32[]{:S(2)}, u32[]{:S(2)}) collective-permute-start(bf16[4,64,256]{2,1,0:T(8,128)(2,1)S(1)} %get-tuple-element.58), channel_id=1, source_target_pairs={{16,0},{20,4},{24,8},{28,12},{0,16},{4,20},{8,24},{12,28},{17,1},{... | collective-permute-start | bytes 393224 | tf_op jit(solution)/shard_map/ppermute | solution.py:43
  73.7 2.7 %collective-permute-start.29 = (bf16[4,64,256]{2,1,0:T(8,128)(2,1)S(1)}, bf16[4,64,256]{2,1,0:T(8,128)(2,1)S(1)}, u32[]{:S(2)}, u32[]{:S(2)}) collective-permute-start(bf16[4,64,256]{2,1,0:T(8,128)(2,1)S(1)} %get-tuple-element.66), channel_id=1, source_target_pairs={{12,0},{8,4},{4,8},{0,12},{28,16},{24,20},{20,24},{16,28},{13,1},{... | collective-permute-start | bytes 393224 | tf_op jit(solution)/shard_map/ppermute | solution.py:43
  76.5 2.3 %collective-permute-start.21 = (bf16[4,64,256]{2,1,0:T(8,128)(2,1)S(1)}, bf16[4,64,256]{2,1,0:T(8,128)(2,1)S(1)}, u32[]{:S(2)}, u32[]{:S(2)}) collective-permute-start(bf16[4,64,256]{2,1,0:T(8,128)(2,1)S(1)} %get-tuple-element.56), channel_id=1, source_target_pairs={{20,0},{16,4},{28,8},{24,12},{4,16},{0,20},{12,24},{8,28},{21,1},{... | collective-permute-start | bytes 393224 | tf_op jit(solution)/shard_map/ppermute | solution.py:43
  78.8 1.7 %collective-permute-start.18 = (bf16[4,64,256]{2,1,0:T(8,128)(2,1)S(1)}, bf16[4,64,256]{2,1,0:T(8,128)(2,1)S(1)}, u32[]{:S(2)}, u32[]{:S(2)}) collective-permute-start(bf16[4,64,256]{2,1,0:T(8,128)(2,1)S(1)} %get-tuple-element.53), channel_id=1, source_target_pairs={{24,0},{28,4},{16,8},{20,12},{8,16},{12,20},{0,24},{4,28},{25,1},{... | collective-permute-start | bytes 393224 | tf_op jit(solution)/shard_map/ppermute | solution.py:43
  80.5 2.7 %collective-permute-done.27.refs_5_ = bf16[4,64,256]{2,1,0:T(8,128)(2,1)S(1)} collective-permute-done((bf16[4,64,256]{2,1,0:T(8,128)(2,1)S(1)}, bf16[4,64,256]{2,1,0:T(8,128)(2,1)S(1)}, u32[]{:S(2)}, u32[]{:S(2)}) %collective-permute-start.27) | collective-permute-done | bytes 131104 | tf_op jit(solution)/shard_map/ppermute | solution.py:43
  83.2 1.9 %collective-permute-start.10 = (bf16[4,64,256]{2,1,0:T(8,128)(2,1)S(1)}, bf16[4,64,256]{2,1,0:T(8,128)(2,1)S(1)}, u32[]{:S(2)}, u32[]{:S(2)}) collective-permute-start(bf16[4,64,256]{2,1,0:T(8,128)(2,1)S(1)} %get-tuple-element.43), channel_id=1, source_target_pairs={{28,0},{24,4},{20,8},{16,12},{12,16},{8,20},{4,24},{0,28},{29,1},{... | collective-permute-start | bytes 393224 | tf_op jit(solution)/shard_map/ppermute | solution.py:43
  85.1 10.1 %collective-permute-done.29.refs_7_ = bf16[4,64,256]{2,1,0:T(8,128)(2,1)S(1)} collective-permute-done((bf16[4,64,256]{2,1,0:T(8,128)(2,1)S(1)}, bf16[4,64,256]{2,1,0:T(8,128)(2,1)S(1)}, u32[]{:S(2)}, u32[]{:S(2)}) %collective-permute-start.29) | collective-permute-done | bytes 131104 | tf_op jit(solution)/shard_map/ppermute | solution.py:43
  100.8 7.5 %collective-permute-done.10.refs_0_ = bf16[4,64,256]{2,1,0:T(8,128)(2,1)S(1)} collective-permute-done((bf16[4,64,256]{2,1,0:T(8,128)(2,1)S(1)}, bf16[4,64,256]{2,1,0:T(8,128)(2,1)S(1)}, u32[]{:S(2)}, u32[]{:S(2)}) %collective-permute-start.10) | collective-permute-done | bytes 131104 | tf_op jit(solution)/shard_map/ppermute | solution.py:43
  (57 shorter events, 21.7 us)
Async XLA Ops:
  1.2 9.4 %collective-permute-start.8 = (bf16[128,512]{1,0:T(8,128)(2,1)}, bf16[128,512]{1,0:T(8,128)(2,1)S(1)}, u32[]{:S(2)}, u32[]{:S(2)}) collective-permute-start(bf16[128,512]{1,0:T(8,128)(2,1)} %refs_8_.4), channel_id=1, source_target_pairs={{0,2},{1,3},{2,0},{3,1},{4,6},{5,7},{6,4},{7,5},{8,10},{9,11},{10,... | collective-permute-start | bytes 393224 | tf_op jit(solution)/shard_map/ppermute | solution.py:43
  2.4 9.6 %collective-permute-start.7 = (bf16[128,512]{1,0:T(8,128)(2,1)}, bf16[128,512]{1,0:T(8,128)(2,1)S(1)}, u32[]{:S(2)}, u32[]{:S(2)}) collective-permute-start(bf16[128,512]{1,0:T(8,128)(2,1)} %refs_8_.4), channel_id=1, source_target_pairs={{0,1},{1,0},{2,3},{3,2},{4,5},{5,4},{6,7},{7,6},{8,9},{9,8},{10,11... | collective-permute-start | bytes 393224 | tf_op jit(solution)/shard_map/ppermute | solution.py:43
  10.6 33.2 %collective-permute-start.5 = (bf16[64,8,256]{2,1,0:T(8,128)(2,1)S(1)}, bf16[64,8,256]{2,1,0:T(8,128)(2,1)S(1)}, u32[]{:S(2)}, u32[]{:S(2)}) collective-permute-start(bf16[64,8,256]{2,1,0:T(8,128)(2,1)S(1)} %lift.1), channel_id=1, source_target_pairs={{0,24},{4,28},{8,16},{12,20},{16,8},{20,12},{24,0},{28,4},{1,25},{... | collective-permute-start | bytes 786440 | tf_op jit(solution)/shard_map/ppermute | solution.py:43
  11.9 22.4 %collective-permute-start.3 = (bf16[4,64,256]{2,1,0:T(8,128)(2,1)S(1)}, bf16[4,64,256]{2,1,0:T(8,128)(2,1)S(1)}, u32[]{:S(2)}, u32[]{:S(2)}) collective-permute-start(bf16[4,64,256]{2,1,0:T(8,128)(2,1)S(1)} %get-tuple-element.40), channel_id=1, source_target_pairs={{0,16},{4,20},{8,24},{12,28},{16,0},{20,4},{24,8},{28,12},{1,17},{... | collective-permute-start | bytes 393224 | tf_op jit(solution)/shard_map/ppermute | solution.py:43
  13.1 24.1 %collective-permute-start.4 = (bf16[4,64,256]{2,1,0:T(8,128)(2,1)S(1)}, bf16[4,64,256]{2,1,0:T(8,128)(2,1)S(1)}, u32[]{:S(2)}, u32[]{:S(2)}) collective-permute-start(bf16[4,64,256]{2,1,0:T(8,128)(2,1)S(1)} %get-tuple-element.41), channel_id=1, source_target_pairs={{0,20},{4,16},{8,28},{12,24},{16,4},{20,0},{24,12},{28,8},{1,21},{... | collective-permute-start | bytes 393224 | tf_op jit(solution)/shard_map/ppermute | solution.py:43
  14.9 26.5 %collective-permute-start.6 = (bf16[4,64,256]{2,1,0:T(8,128)(2,1)S(1)}, bf16[4,64,256]{2,1,0:T(8,128)(2,1)S(1)}, u32[]{:S(2)}, u32[]{:S(2)}) collective-permute-start(bf16[4,64,256]{2,1,0:T(8,128)(2,1)S(1)} %get-tuple-element.42), channel_id=1, source_target_pairs={{0,28},{4,24},{8,20},{12,16},{16,12},{20,8},{24,4},{28,0},{1,29},{... | collective-permute-start | bytes 393224 | tf_op jit(solution)/shard_map/ppermute | solution.py:43
  16.7 24.7 %collective-permute-start.11 = (bf16[4,64,256]{2,1,0:T(8,128)(2,1)S(1)}, bf16[4,64,256]{2,1,0:T(8,128)(2,1)S(1)}, u32[]{:S(2)}, u32[]{:S(2)}) collective-permute-start(bf16[4,64,256]{2,1,0:T(8,128)(2,1)S(1)} %get-tuple-element.45), channel_id=1, source_target_pairs={{0,4},{4,0},{8,12},{12,8},{16,20},{20,16},{24,28},{28,24},{1,5},{5... | collective-permute-start | bytes 393224 | tf_op jit(solution)/shard_map/ppermute | solution.py:43
  34.3 15.7 %collective-permute-start.12 = (bf16[4,64,256]{2,1,0:T(8,128)(2,1)S(1)}, bf16[4,64,256]{2,1,0:T(8,128)(2,1)S(1)}, u32[]{:S(2)}, u32[]{:S(2)}) collective-permute-start(bf16[4,64,256]{2,1,0:T(8,128)(2,1)S(1)} %get-tuple-element.46), channel_id=1, source_target_pairs={{0,8},{4,12},{8,0},{12,4},{16,24},{20,28},{24,16},{28,20},{1,9},{5... | collective-permute-start | bytes 393224 | tf_op jit(solution)/shard_map/ppermute | solution.py:43
  37.1 13.9 %collective-permute-start.13 = (bf16[4,64,256]{2,1,0:T(8,128)(2,1)S(1)}, bf16[4,64,256]{2,1,0:T(8,128)(2,1)S(1)}, u32[]{:S(2)}, u32[]{:S(2)}) collective-permute-start(bf16[4,64,256]{2,1,0:T(8,128)(2,1)S(1)} %get-tuple-element.47), channel_id=1, source_target_pairs={{0,12},{4,8},{8,4},{12,0},{16,28},{20,24},{24,20},{28,16},{1,13},{... | collective-permute-start | bytes 393224 | tf_op jit(solution)/shard_map/ppermute | solution.py:43
  41.4 17.4 %collective-permute-start.14 = (bf16[4,64,256]{2,1,0:T(8,128)(2,1)S(1)}, bf16[4,64,256]{2,1,0:T(8,128)(2,1)S(1)}, u32[]{:S(2)}, u32[]{:S(2)}) collective-permute-start(bf16[4,64,256]{2,1,0:T(8,128)(2,1)S(1)} %get-tuple-element.48), channel_id=1, source_target_pairs={{0,16},{4,20},{8,24},{12,28},{16,0},{20,4},{24,8},{28,12},{1,17},{... | collective-permute-start | bytes 393224 | tf_op jit(solution)/shard_map/ppermute | solution.py:43
  41.5 20.2 %collective-permute-start.15 = (bf16[4,64,256]{2,1,0:T(8,128)(2,1)S(1)}, bf16[4,64,256]{2,1,0:T(8,128)(2,1)S(1)}, u32[]{:S(2)}, u32[]{:S(2)}) collective-permute-start(bf16[4,64,256]{2,1,0:T(8,128)(2,1)S(1)} %get-tuple-element.49), channel_id=1, source_target_pairs={{0,20},{4,16},{8,28},{12,24},{16,4},{20,0},{24,12},{28,8},{1,21},{... | collective-permute-start | bytes 393224 | tf_op jit(solution)/shard_map/ppermute | solution.py:43
  43.8 22.7 %collective-permute-start.16 = (bf16[4,64,256]{2,1,0:T(8,128)(2,1)S(1)}, bf16[4,64,256]{2,1,0:T(8,128)(2,1)S(1)}, u32[]{:S(2)}, u32[]{:S(2)}) collective-permute-start(bf16[4,64,256]{2,1,0:T(8,128)(2,1)S(1)} %get-tuple-element.50), channel_id=1, source_target_pairs={{0,28},{4,24},{8,20},{12,16},{16,12},{20,8},{24,4},{28,0},{1,29},{... | collective-permute-start | bytes 393224 | tf_op jit(solution)/shard_map/ppermute | solution.py:43
  50.0 21.0 %collective-permute-start.20 = (bf16[4,64,256]{2,1,0:T(8,128)(2,1)S(1)}, bf16[4,64,256]{2,1,0:T(8,128)(2,1)S(1)}, u32[]{:S(2)}, u32[]{:S(2)}) collective-permute-start(bf16[4,64,256]{2,1,0:T(8,128)(2,1)S(1)} %get-tuple-element.55), channel_id=1, source_target_pairs={{20,0},{16,4},{28,8},{24,12},{4,16},{0,20},{12,24},{8,28},{21,1},{... | collective-permute-start | bytes 393224 | tf_op jit(solution)/shard_map/ppermute | solution.py:43
  51.0 21.8 %collective-permute-start.22 = (bf16[4,64,256]{2,1,0:T(8,128)(2,1)S(1)}, bf16[4,64,256]{2,1,0:T(8,128)(2,1)S(1)}, u32[]{:S(2)}, u32[]{:S(2)}) collective-permute-start(bf16[4,64,256]{2,1,0:T(8,128)(2,1)S(1)} %get-tuple-element.57), channel_id=1, source_target_pairs={{16,0},{20,4},{24,8},{28,12},{0,16},{4,20},{8,24},{12,28},{17,1},{... | collective-permute-start | bytes 393224 | tf_op jit(solution)/shard_map/ppermute | solution.py:43
  58.8 14.3 %collective-permute-start.24 = (bf16[4,64,256]{2,1,0:T(8,128)(2,1)S(1)}, bf16[4,64,256]{2,1,0:T(8,128)(2,1)S(1)}, u32[]{:S(2)}, u32[]{:S(2)}) collective-permute-start(bf16[4,64,256]{2,1,0:T(8,128)(2,1)S(1)} %get-tuple-element.61), channel_id=1, source_target_pairs={{4,0},{0,4},{12,8},{8,12},{20,16},{16,20},{28,24},{24,28},{5,1},{1... | collective-permute-start | bytes 393224 | tf_op jit(solution)/shard_map/ppermute | solution.py:43
  61.7 12.1 %collective-permute-start.26 = (bf16[4,64,256]{2,1,0:T(8,128)(2,1)S(1)}, bf16[4,64,256]{2,1,0:T(8,128)(2,1)S(1)}, u32[]{:S(2)}, u32[]{:S(2)}) collective-permute-start(bf16[4,64,256]{2,1,0:T(8,128)(2,1)S(1)} %get-tuple-element.63), channel_id=1, source_target_pairs={{8,0},{12,4},{0,8},{4,12},{24,16},{28,20},{16,24},{20,28},{9,1},{1... | collective-permute-start | bytes 393224 | tf_op jit(solution)/shard_map/ppermute | solution.py:43
  66.4 10.0 %collective-permute-start.28 = (bf16[4,64,256]{2,1,0:T(8,128)(2,1)S(1)}, bf16[4,64,256]{2,1,0:T(8,128)(2,1)S(1)}, u32[]{:S(2)}, u32[]{:S(2)}) collective-permute-start(bf16[4,64,256]{2,1,0:T(8,128)(2,1)S(1)} %get-tuple-element.65), channel_id=1, source_target_pairs={{12,0},{8,4},{4,8},{0,12},{28,16},{24,20},{20,24},{16,28},{13,1},{... | collective-permute-start | bytes 393224 | tf_op jit(solution)/shard_map/ppermute | solution.py:43
  73.1 10.1 %collective-permute-start.27 = (bf16[4,64,256]{2,1,0:T(8,128)(2,1)S(1)}, bf16[4,64,256]{2,1,0:T(8,128)(2,1)S(1)}, u32[]{:S(2)}, u32[]{:S(2)}) collective-permute-start(bf16[4,64,256]{2,1,0:T(8,128)(2,1)S(1)} %get-tuple-element.64), channel_id=1, source_target_pairs={{8,0},{12,4},{0,8},{4,12},{24,16},{28,20},{16,24},{20,28},{9,1},{1... | collective-permute-start | bytes 393224 | tf_op jit(solution)/shard_map/ppermute | solution.py:43
  73.7 21.4 %collective-permute-start.29 = (bf16[4,64,256]{2,1,0:T(8,128)(2,1)S(1)}, bf16[4,64,256]{2,1,0:T(8,128)(2,1)S(1)}, u32[]{:S(2)}, u32[]{:S(2)}) collective-permute-start(bf16[4,64,256]{2,1,0:T(8,128)(2,1)S(1)} %get-tuple-element.66), channel_id=1, source_target_pairs={{12,0},{8,4},{4,8},{0,12},{28,16},{24,20},{20,24},{16,28},{13,1},{... | collective-permute-start | bytes 393224 | tf_op jit(solution)/shard_map/ppermute | solution.py:43
  76.5 22.4 %collective-permute-start.21 = (bf16[4,64,256]{2,1,0:T(8,128)(2,1)S(1)}, bf16[4,64,256]{2,1,0:T(8,128)(2,1)S(1)}, u32[]{:S(2)}, u32[]{:S(2)}) collective-permute-start(bf16[4,64,256]{2,1,0:T(8,128)(2,1)S(1)} %get-tuple-element.56), channel_id=1, source_target_pairs={{20,0},{16,4},{28,8},{24,12},{4,16},{0,20},{12,24},{8,28},{21,1},{... | collective-permute-start | bytes 393224 | tf_op jit(solution)/shard_map/ppermute | solution.py:43
  78.8 21.1 %collective-permute-start.18 = (bf16[4,64,256]{2,1,0:T(8,128)(2,1)S(1)}, bf16[4,64,256]{2,1,0:T(8,128)(2,1)S(1)}, u32[]{:S(2)}, u32[]{:S(2)}) collective-permute-start(bf16[4,64,256]{2,1,0:T(8,128)(2,1)S(1)} %get-tuple-element.53), channel_id=1, source_target_pairs={{24,0},{28,4},{16,8},{20,12},{8,16},{12,20},{0,24},{4,28},{25,1},{... | collective-permute-start | bytes 393224 | tf_op jit(solution)/shard_map/ppermute | solution.py:43
  80.4 19.4 %collective-permute-start.19 = (bf16[4,64,256]{2,1,0:T(8,128)(2,1)S(1)}, bf16[4,64,256]{2,1,0:T(8,128)(2,1)S(1)}, u32[]{:S(2)}, u32[]{:S(2)}) collective-permute-start(bf16[4,64,256]{2,1,0:T(8,128)(2,1)S(1)} %get-tuple-element.54), channel_id=1, source_target_pairs={{24,0},{28,4},{16,8},{20,12},{8,16},{12,20},{0,24},{4,28},{25,1},{... | collective-permute-start | bytes 393224 | tf_op jit(solution)/shard_map/ppermute | solution.py:43
  83.2 25.1 %collective-permute-start.10 = (bf16[4,64,256]{2,1,0:T(8,128)(2,1)S(1)}, bf16[4,64,256]{2,1,0:T(8,128)(2,1)S(1)}, u32[]{:S(2)}, u32[]{:S(2)}) collective-permute-start(bf16[4,64,256]{2,1,0:T(8,128)(2,1)S(1)} %get-tuple-element.43), channel_id=1, source_target_pairs={{28,0},{24,4},{20,8},{16,12},{12,16},{8,20},{4,24},{0,28},{29,1},{... | collective-permute-start | bytes 393224 | tf_op jit(solution)/shard_map/ppermute | solution.py:43
  95.1 14.4 %collective-permute-start.17 = (bf16[4,64,256]{2,1,0:T(8,128)(2,1)S(1)}, bf16[4,64,256]{2,1,0:T(8,128)(2,1)S(1)}, u32[]{:S(2)}, u32[]{:S(2)}) collective-permute-start(bf16[4,64,256]{2,1,0:T(8,128)(2,1)S(1)} %get-tuple-element.51), channel_id=1, source_target_pairs={{28,0},{24,4},{20,8},{16,12},{12,16},{8,20},{4,24},{0,28},{29,1},{... | collective-permute-start | bytes 393224 | tf_op jit(solution)/shard_map/ppermute | solution.py:43
  (12 other events, 343.2 us)
